TPU v7x, 8 devices: a whole 2x2x1 slice. The times are simulated.
8 devices in a mesh: dp: 1 (over z), tp: 8 (over y, x, core).
Axes of the slice: x: 2, y: 2, z: 1, core: 2. Of those that a mesh axis runs over, the one named last changes fastest.
Arguments:
- x_in: bfloat16 [512, 7168], P('dp')
- pos_ids: int32 [512], P('dp')
- ckv_cache: bfloat16 [2, 512, 256, 512], P(None, 'dp')
- kpe_cache: bfloat16 [2, 512, 256, 64], P(None, 'dp')
- attn_gain: bfloat16 [2, 7168], replicated
- w_dq: bfloat16 [2, 7168, 1536], replicated
- q_gain: bfloat16 [2, 1536], replicated
- w_dkv: bfloat16 [2, 7168, 576], replicated
- kv_gain: bfloat16 [2, 512], replicated
- w_uq: bfloat16 [2, 1536, 64, 192], P(None, None, 'tp')
- w_uk: bfloat16 [2, 512, 64, 128], P(None, None, 'tp')
- w_uv: bfloat16 [2, 512, 64, 128], P(None, None, 'tp')
- w_o: bfloat16 [2, 64, 128, 7168], P(None, 'tp')
- mlp_gain: bfloat16 [2, 7168], replicated
- w_gate: bfloat16 [2, 7168, 9216], P(None, None, 'tp')
- w_up: bfloat16 [2, 7168, 9216], P(None, None, 'tp')
- w_down: bfloat16 [2, 9216, 7168], P(None, 'tp')
Outputs:
- output 1: bfloat16 [512, 7168], P('dp')
- output 2: bfloat16 [2, 512, 512], P(None, 'dp')
- output 3: bfloat16 [2, 512, 64], P(None, 'dp')
All inputs are finite; a program needn't handle non-finite values.
Results may differ from a plain program's by a relative error of at most 0.02.
Values are sent between devices in bfloat16 or wider.
A program may use at most 2 GiB of HBM per device.

v0:
```python
import math
import jax
import jax.numpy as jnp
from jax import lax
from jax.sharding import PartitionSpec as P

NORM_EPS = 1e-6
ROPE_BASE = 10000.0


def rms_norm(values, norm_gain):
    values = values.astype(jnp.float32)
    inv_rms = lax.rsqrt(jnp.mean(values * values, axis=-1, keepdims=True) + NORM_EPS)
    return (values * inv_rms * norm_gain.astype(jnp.float32)).astype(jnp.bfloat16)


def rotary(values, positions):
    half_dim = values.shape[-1] // 2
    inv_freq = jnp.exp(jnp.arange(half_dim, dtype=jnp.float32) * (-2.0 * math.log(ROPE_BASE) / values.shape[-1]))
    angles = positions.astype(jnp.float32)[..., None] * inv_freq
    cos_part = jnp.cos(angles)
    sin_part = jnp.sin(angles)
    lo_half = values[..., :half_dim]
    hi_half = values[..., half_dim:]
    return jnp.concatenate([lo_half * cos_part - hi_half * sin_part, hi_half * cos_part + lo_half * sin_part], axis=-1)


def latent_attention(q_lat, q_rope, ckv_old, kpe_old, ckv_new, kpe_new, positions, score_scale):
    scores = jnp.einsum('bhc,btc->bht', q_lat, ckv_old, preferred_element_type=jnp.float32)
    scores = scores + jnp.einsum('bhr,btr->bht', q_rope, kpe_old, preferred_element_type=jnp.float32)
    fresh_score = jnp.einsum('bhc,bc->bh', q_lat, ckv_new, preferred_element_type=jnp.float32)
    fresh_score = fresh_score + jnp.einsum('bhr,br->bh', q_rope, kpe_new, preferred_element_type=jnp.float32)
    key_steps = jnp.arange(ckv_old.shape[1])[None, None, :]
    pos_limit = positions[:, None, None]
    at_pos = key_steps == pos_limit
    scores = jnp.where(at_pos, fresh_score[:, :, None], scores) * score_scale
    scores = jnp.where(key_steps <= pos_limit, scores, -jnp.inf)
    attn_prob = jax.nn.softmax(scores, axis=-1).astype(jnp.bfloat16)
    bf_zero = jnp.zeros((), jnp.bfloat16)
    new_prob = jnp.sum(jnp.where(at_pos, attn_prob, bf_zero), axis=-1).astype(jnp.float32)
    context = jnp.einsum('bht,btc->bhc', jnp.where(at_pos, bf_zero, attn_prob), ckv_old, preferred_element_type=jnp.float32)
    context = context + new_prob[:, :, None] * ckv_new.astype(jnp.float32)[:, None, :]
    return context.astype(jnp.bfloat16)


def attention_heads(normed, positions, ckv_old, kpe_old, w_dq, q_gain, w_dkv, kv_gain, w_uq, w_uk, w_uv):
    value_a8 = ckv_old.shape[-1]
    nope_dim = w_uk.shape[-1]
    c_q = rms_norm(jnp.dot(normed, w_dq, preferred_element_type=jnp.float32), q_gain)
    q_full = jnp.einsum('bc,chd->bhd', c_q, w_uq, preferred_element_type=jnp.float32)
    q_nope = q_full[..., :nope_dim].astype(jnp.bfloat16)
    q_rope = rotary(q_full[..., nope_dim:], positions[:, None]).astype(jnp.bfloat16)
    q_lat = jnp.einsum('bhn,chn->bhc', q_nope, w_uk, preferred_element_type=jnp.float32).astype(jnp.bfloat16)
    kv_lat = jnp.dot(normed, w_dkv, preferred_element_type=jnp.float32)
    ckv_new = rms_norm(kv_lat[:, :value_a8], kv_gain)
    kpe_new = rotary(kv_lat[:, value_a8:], positions).astype(jnp.bfloat16)
    context = latent_attention(q_lat, q_rope, ckv_old, kpe_old, ckv_new, kpe_new, positions, w_uq.shape[-1] ** -0.5)
    head_out = jnp.einsum('bhc,chv->bhv', context, w_uv, preferred_element_type=jnp.float32).astype(jnp.bfloat16)
    return head_out, ckv_new, kpe_new


def gated_mlp(mlp_in, w_gate, w_up, w_down):
    gate_pre = jnp.dot(mlp_in, w_gate, preferred_element_type=jnp.float32)
    up_pre = jnp.dot(mlp_in, w_up, preferred_element_type=jnp.float32)
    act_out = (jax.nn.silu(gate_pre) * up_pre).astype(jnp.bfloat16)
    return jnp.dot(act_out, w_down, preferred_element_type=jnp.float32)


def local_layer(hidden, positions, ckv_old, kpe_old, weights):
    (attn_gain, w_dq, q_gain, w_dkv, kv_gain, w_uq, w_uk, w_uv, w_o, mlp_gain, w_gate, w_up, w_down) = weights
    normed = rms_norm(hidden, attn_gain)
    head_out, ckv_new, kpe_new = attention_heads(normed, positions, ckv_old, kpe_old, w_dq, q_gain, w_dkv, kv_gain, w_uq, w_uk, w_uv)
    attn_part = jnp.einsum('bhv,hvd->bd', head_out, w_o, preferred_element_type=jnp.float32).astype(jnp.bfloat16)
    attn_sum = lax.psum(attn_part, 'tp')
    mid_state = (hidden.astype(jnp.float32) + attn_sum.astype(jnp.float32)).astype(jnp.bfloat16)
    mlp_part = gated_mlp(rms_norm(mid_state, mlp_gain), w_gate, w_up, w_down).astype(jnp.bfloat16)
    mlp_sum = lax.psum(mlp_part, 'tp')
    layer_out = (mid_state.astype(jnp.float32) + mlp_sum.astype(jnp.float32)).astype(jnp.bfloat16)
    return layer_out, ckv_new, kpe_new


def solution(mesh):
    cache_spec = P(None, 'dp', None, None)
    head_spec = P(None, None, 'tp', None)
    weight_specs = (P(), P(), P(), P(), P(), head_spec, head_spec, head_spec, P(None, 'tp', None, None), P(), P(None, None, 'tp'), P(None, None, 'tp'), P(None, 'tp', None))
    in_specs = (P('dp', None), P('dp'), cache_spec, cache_spec) + weight_specs
    out_specs = (P('dp', None), P(None, 'dp', None), P(None, 'dp', None))

    def device_body(x_in, pos_ids, ckv_cache, kpe_cache, *params):
        hidden = x_in
        c_rows = []
        k_rows = []
        for layer_idx in range(ckv_cache.shape[0]):
            weights = [weight[layer_idx] for weight in params]
            hidden, c_row, k_row = local_layer(hidden, pos_ids, ckv_cache[layer_idx], kpe_cache[layer_idx], weights)
            c_rows.append(c_row)
            k_rows.append(k_row)
        return hidden, jnp.stack(c_rows), jnp.stack(k_rows)

    return jax.shard_map(device_body, mesh=mesh, in_specs=in_specs, out_specs=out_specs, check_vma=False)
```

profile of v0, /device:TPU:1, one launch (start us, length us, event | category | flops | bytes accessed | tf_op | source)
XLA Modules:
  0.0 950.1 jit_solution(17378462137864241905)
XLA Ops:
  7.3 0.8 convert_element_type.191
  8.1 1.0 iota_compare_fusion
  9.2 4.9 fusion.44
  14.1 0.6 slice_convert_fusion.8
  14.7 0.6 slice_convert_fusion.5
  15.3 7.1 fusion.78
  22.9 0.4 copy-done.34
  23.4 0.6 convert_reduce_fusion
  24.0 0.3 fusion.159
  24.5 2.0 copy.32
  26.8 2.6 fusion.172
  29.4 3.0 slice_bitcast_fusion
  32.5 19.7 %multiply_reduce_fusion.1 = (f32[512]{0:T(512)S(1)}, f32[512,1536]{1,0:T(8,128)}) fusion(bf16[2,7168,1536]{2,1,0:T(8,128)(2,1)} %param.22, bf16[512,7168]{1,0:T(8,128)(2,1)} %param.17, f32[7168]{0:T(1024)S(1)} %bitcast.183, f32[512]{0:T(512)S(1)} %add_rsqrt_fusion.7), kind=kOutput, calls=%fused_computation.113 | convolution fusion | flops 11290542080 | bytes 32538624 | tf_op jit(solution)/shard_map/dot_general | solution.py:49
  52.2 6.5 fusion.171
  58.8 4.7 fusion.128
  63.4 3.3 convert_bitcast_fusion.1
  66.9 0.8 copy.23
  67.7 0.7 fusion.175
  68.4 10.2 %fusion.22 = f32[512,8,256]{2,1,0:T(8,128)} fusion(bf16[512,8,64]{2,1,0:T(8,128)(2,1)S(1)} %copy.23, bf16[2,512,256,64]{2,3,1,0:T(8,128)(2,1)} %param.20), kind=kOutput, calls=%fused_computation.34 | convolution fusion | flops 134217728 | bytes 21495808 | tf_op jit(solution)/shard_map/bhr,btr->bht/dot_general | solution.py:30
  78.6 3.5 fusion.89
  82.2 53.0 %multiply_select_fusion.1 = f32[512,8,256]{2,1,0:T(8,128)} fusion(f32[512,8,256]{2,1,0:T(8,128)} %fusion.22, bf16[2,512,256,512]{3,2,1,0:T(8,128)(2,1)} %param.19, bf16[512,8,512]{2,0,1:T(8,128)(2,1)} %convert_bitcast_fusion.1, f32[512,8]{1,0:T(8,128)S(1)} %add.126, pred[512,256]{1,0:T(8,128)(4,1)S(1)} %get-tuple-element.40, ...), kind=kOutput, calls=%fused_computation.100 | convolution fusion | flops 1077936128 | bytes 147079168 | tf_op jit(solution)/shard_map/bhc,btc->bht/dot_general | solution.py:29
  135.2 4.6 fusion.173
  139.8 1.7 select_reduce_fusion.1
  141.6 44.1 %add_convert_fusion.1 = bf16[512,8,512]{2,1,0:T(8,128)(2,1)} fusion(f32[512,512]{1,0:T(8,128)S(1)} %copy.24, f32[512,8]{1,0:T(8,128)S(1)} %convert_element_type.193, bf16[2,512,256,512]{3,2,1,0:T(8,128)(2,1)} %param.19, bf16[512,8,256]{2,1,0:T(8,128)(2,1)S(1)} %get-tuple-element.17, pred[512,256]{1,0:T(8,128)(4,1)S(1)} %get-tuple-element.41), kind=kOutput, calls=%fused_computation.83 | convolution fusion | flops 1081081856 | bytes 141705216 | tf_op jit(solution)/shard_map/bht,btc->bhc/dot_general | solution.py:41
  185.7 3.9 fusion.143
  189.6 12.9 %bitcast_convert_fusion.1 = bf16[512,7168]{1,0:T(8,128)(2,1)} fusion(bf16[512,8,128]{2,0,1:T(8,128)(2,1)S(1)} %fusion.143, bf16[2,8,128,7168]{3,2,1,0:T(8,128)(2,1)} %param.29), kind=kOutput, calls=%fused_computation.75 | convolution fusion | flops 7519862784 | bytes 23068672 | tf_op jit(solution)/shard_map/bhv,hvd->bd/dot_general | solution.py:73
  202.6 0.3 all-reduce.7.cloned.1.call-start
  202.8 0.5 copy-done.29
  203.3 0.7 slice_convert_fusion.4
  203.9 104.1 %all-reduce.5.cloned.1.call-done = bf16[512,7168]{1,0:T(8,128)(2,1)} async-done(((bf16[512,7168]{1,0:T(8,128)(2,1)}), bf16[512,7168]{1,0:T(8,128)(2,1)}) %all-reduce.5.cloned.1.call-update) | async-done | bytes 7340048 | tf_op jit(solution)/shard_map/psum | solution.py:74
  308.1 11.7 %fusion.48 = (f32[512]{0:T(512)S(1)}, bf16[512,7168]{1,0:T(8,128)(2,1)}) fusion(bf16[512,7168]{1,0:T(8,128)(2,1)} %all-reduce.5.cloned.1.call-done, bf16[512,7168]{1,0:T(8,128)(2,1)} %param.17), kind=kLoop, calls=%fused_computation.60 | loop fusion | flops 25689600 | bytes 22022144 | tf_op jit(solution)/shard_map/reduce_sum | solution.py:13
  319.7 17.9 %fusion.36 = f32[512,1152]{1,0:T(8,128)} fusion(bf16[2,7168,1152]{2,1,0:T(8,128)(2,1)} %param.31, bf16[512,7168]{1,0:T(8,128)(2,1)} %get-tuple-element.15, f32[7168]{0:T(1024)S(1)} %bitcast.184, f32[512]{0:T(512)S(1)} %add_rsqrt_fusion.4), kind=kOutput, calls=%fused_computation.48 | convolution fusion | flops 8470396928 | bytes 26245120 | tf_op jit(solution)/shard_map/dot_general | solution.py:63
  337.7 15.8 %fusion.105 = bf16[512,1152]{1,0:T(8,128)(2,1)} fusion(bf16[2,7168,1152]{2,1,0:T(8,128)(2,1)} %param.32, f32[512,1152]{1,0:T(8,128)} %fusion.36, bf16[512,7168]{1,0:T(8,128)(2,1)S(1)} %copy-done.1, f32[7168]{0:T(1024)S(1)} %bitcast.185, f32[512]{0:T(512)S(1)} %add_rsqrt_fusion.4), kind=kOutput, calls=%fused_computation.115 | convolution fusion | flops 8473935872 | bytes 27424768 | tf_op jit(solution)/shard_map/dot_general | solution.py:64
  353.5 15.3 %fusion.70 = bf16[512,7168]{1,0:T(8,128)(2,1)} fusion(bf16[512,1152]{1,0:T(8,128)(2,1)} %fusion.105, bf16[2,1152,7168]{2,1,0:T(8,128)(2,1)} %param.33), kind=kOutput, calls=%fused_computation.80 | convolution fusion | flops 8459386880 | bytes 25034752 | tf_op jit(solution)/shard_map/dot_general | solution.py:66
  368.8 0.4 all-reduce.9.cloned.1.call-start
  369.3 103.7 %all-reduce.7.cloned.1.call-done = bf16[512,7168]{1,0:T(8,128)(2,1)} async-done(((bf16[512,7168]{1,0:T(8,128)(2,1)}), bf16[512,7168]{1,0:T(8,128)(2,1)}) %all-reduce.7.cloned.1.call-update) | async-done | bytes 7340048 | tf_op jit(solution)/shard_map/psum | solution.py:77
  473.0 11.7 %fusion.52 = (f32[512]{0:T(512)S(1)}, bf16[512,7168]{1,0:T(8,128)(2,1)}) fusion(bf16[512,7168]{1,0:T(8,128)(2,1)} %all-reduce.7.cloned.1.call-done, bf16[512,7168]{1,0:T(8,128)(2,1)} %get-tuple-element.15), kind=kLoop, calls=%fused_computation.64 | loop fusion | flops 25689600 | bytes 22022144 | tf_op jit(solution)/shard_map/reduce_sum | solution.py:13
  484.7 9.5 fusion.76
  494.4 0.3 fusion.163
  494.9 0.3 copy-done.7
  495.4 19.4 %multiply_reduce_fusion = (f32[512]{0:T(512)S(1)}, f32[512,1536]{1,0:T(8,128)}) fusion(bf16[2,7168,1536]{2,1,0:T(8,128)(2,1)} %param.22, bf16[512,7168]{1,0:T(8,128)(2,1)} %get-tuple-element.13, f32[7168]{0:T(1024)S(1)} %bitcast.179, f32[512]{0:T(512)S(1)} %add_rsqrt_fusion.3), kind=kOutput, calls=%fused_computation.111 | convolution fusion | flops 11290542080 | bytes 32538624 | tf_op jit(solution)/shard_map/dot_general | solution.py:49
  515.0 2.0 copy.39
  517.3 5.9 fusion.129
  523.5 3.3 convert_bitcast_fusion
  526.8 0.8 copy.28
  527.6 10.2 %fusion.20 = f32[512,8,256]{2,1,0:T(8,128)} fusion(bf16[512,8,64]{2,1,0:T(8,128)(2,1)S(1)} %copy.28, bf16[2,512,256,64]{2,3,1,0:T(8,128)(2,1)} %param.20), kind=kOutput, calls=%fused_computation.32 | convolution fusion | flops 134217728 | bytes 21495808 | tf_op jit(solution)/shard_map/bhr,btr->bht/dot_general | solution.py:30
  537.7 0.7 fusion.176
  538.5 3.5 fusion.86
  542.0 53.1 %multiply_select_fusion = f32[512,8,256]{2,1,0:T(8,128)} fusion(f32[512,8,256]{2,1,0:T(8,128)} %fusion.20, bf16[2,512,256,512]{3,2,1,0:T(8,128)(2,1)} %param.19, bf16[512,8,512]{2,0,1:T(8,128)(2,1)} %convert_bitcast_fusion, f32[512,8]{1,0:T(8,128)S(1)} %add.138, pred[512,256]{1,0:T(8,128)(4,1)S(1)} %copy-done.13, pred[512,256]{1,0:T(8,128)(4,1)S(1)} %copy-done.10), kind=kOutput, calls=%fused_computation.96 | convolution fusion | flops 1077936128 | bytes 147079168 | tf_op jit(solution)/shard_map/bhc,btc->bht/dot_general | solution.py:29
  595.1 4.6 fusion.174
  599.8 1.7 select_reduce_fusion
  601.5 44.1 %add_convert_fusion = bf16[512,8,512]{2,1,0:T(8,128)(2,1)} fusion(f32[512,512]{1,0:T(8,128)S(1)} %copy.29, f32[512,8]{1,0:T(8,128)S(1)} %convert_element_type.214, bf16[2,512,256,512]{3,2,1,0:T(8,128)(2,1)} %param.19, bf16[512,8,256]{2,1,0:T(8,128)(2,1)S(1)} %get-tuple-element.11, pred[512,256]{1,0:T(8,128)(4,1)S(1)} %copy-done.10), kind=kOutput, calls=%fused_computation.82 | convolution fusion | flops 1081081856 | bytes 141705216 | tf_op jit(solution)/shard_map/bht,btc->bhc/dot_general | solution.py:41
  645.7 3.9 fusion.140
  649.6 13.0 %bitcast_convert_fusion = bf16[512,7168]{1,0:T(8,128)(2,1)} fusion(bf16[512,8,128]{2,0,1:T(8,128)(2,1)S(1)} %fusion.140, bf16[2,8,128,7168]{3,2,1,0:T(8,128)(2,1)} %param.29), kind=kOutput, calls=%fused_computation.72 | convolution fusion | flops 7519862784 | bytes 23068672 | tf_op jit(solution)/shard_map/bhv,hvd->bd/dot_general | solution.py:73
  662.7 104.2 %all-reduce.9.cloned.1.call-done = bf16[512,7168]{1,0:T(8,128)(2,1)} async-done(((bf16[512,7168]{1,0:T(8,128)(2,1)}), bf16[512,7168]{1,0:T(8,128)(2,1)}) %all-reduce.9.cloned.1.call-update) | async-done | bytes 7340048 | tf_op jit(solution)/shard_map/psum | solution.py:74
  766.8 11.7 %fusion.56 = (f32[512]{0:T(512)S(1)}, bf16[512,7168]{1,0:T(8,128)(2,1)}) fusion(bf16[512,7168]{1,0:T(8,128)(2,1)} %all-reduce.9.cloned.1.call-done, bf16[512,7168]{1,0:T(8,128)(2,1)} %get-tuple-element.13), kind=kLoop, calls=%fused_computation.68 | loop fusion | flops 25689600 | bytes 22022144 | tf_op jit(solution)/shard_map/reduce_sum | solution.py:13
  778.5 18.2 %fusion.30 = f32[512,1152]{1,0:T(8,128)} fusion(bf16[2,7168,1152]{2,1,0:T(8,128)(2,1)} %param.31, bf16[512,7168]{1,0:T(8,128)(2,1)} %get-tuple-element.9, f32[7168]{0:T(1024)S(1)} %bitcast.180, f32[512]{0:T(512)S(1)} %add_rsqrt_fusion), kind=kOutput, calls=%fused_computation.42 | convolution fusion | flops 8470396928 | bytes 26245120 | tf_op jit(solution)/shard_map/dot_general | solution.py:63
  796.7 15.8 %fusion.102 = bf16[512,1152]{1,0:T(8,128)(2,1)} fusion(bf16[2,7168,1152]{2,1,0:T(8,128)(2,1)} %param.32, f32[512,1152]{1,0:T(8,128)} %fusion.30, bf16[512,7168]{1,0:T(8,128)(2,1)S(1)} %copy-done.2, f32[7168]{0:T(1024)S(1)} %bitcast.181, f32[512]{0:T(512)S(1)} %add_rsqrt_fusion), kind=kOutput, calls=%fused_computation.114 | convolution fusion | flops 8473935872 | bytes 27424768 | tf_op jit(solution)/shard_map/dot_general | solution.py:64
  812.5 15.4 %fusion.73 = bf16[512,7168]{1,0:T(8,128)(2,1)} fusion(bf16[512,1152]{1,0:T(8,128)(2,1)} %fusion.102, bf16[2,1152,7168]{2,1,0:T(8,128)(2,1)} %param.33), kind=kOutput, calls=%fused_computation.81 | convolution fusion | flops 8459386880 | bytes 25034752 | tf_op jit(solution)/shard_map/dot_general | solution.py:66
  828.0 1.2 copy-done.6
  829.8 1.6 copy.30
  831.5 0.7 maximum_maximum_fusion
  832.1 100.1 %all-reduce.11.cloned.1.call-done = bf16[512,7168]{1,0:T(8,128)(2,1)} async-done(((bf16[512,7168]{1,0:T(8,128)(2,1)}), bf16[512,7168]{1,0:T(8,128)(2,1)}) %all-reduce.11.cloned.1.call-update) | async-done | bytes 7340048 | tf_op jit(solution)/shard_map/psum | solution.py:77
  932.3 10.8 %fusion.59 = bf16[512,7168]{1,0:T(8,128)(2,1)} fusion(bf16[512,7168]{1,0:T(8,128)(2,1)} %get-tuple-element.9, bf16[512,7168]{1,0:T(8,128)(2,1)} %all-reduce.11.cloned.1.call-done), kind=kLoop, calls=%fused_computation.71 | loop fusion | flops 14680064 | bytes 22020096 | tf_op jit(solution)/shard_map/convert_element_type | solution.py:78
  (128 shorter events, 3.1 us)
Async XLA Ops:
  7.2 6.9 copy-start.44
  7.2 7.5 copy-start.28
  7.2 300.9 %all-reduce.5.cloned.1.call-start = ((), (), s32[]{:S(2)}) async-start(), calls=%async_computation | async-start | bytes 14680064 | tf_op jit(solution)/shard_map/psum | solution.py:74
  7.2 8.1 copy-start
  7.3 16.7 %copy-start.45 = (f32[32]{0:T(128)}, f32[32]{0:T(128)S(1)}, u32[]{:S(2)}) copy-start(f32[32]{0:T(128)S(1)} %multiply_exponential_fusion) | copy-start | bytes 388
  8.1 15.9 %copy-start.41 = (f32[512]{0:T(512)}, f32[512]{0:T(512)S(1)}, u32[]{:S(2)}) copy-start(f32[512]{0:T(512)S(1)} %convert_element_type.191) | copy-start | bytes 6148
  9.2 73.0 %copy-start.12 = (pred[512,256]{1,0:T(8,128)(4,1)}, pred[512,256]{1,0:T(8,128)(4,1)S(1)}, u32[]{:S(2)}) copy-start(pred[512,256]{1,0:T(8,128)(4,1)S(1)} %get-tuple-element.40) | copy-start | bytes 393220
  9.2 132.4 %copy-start.9 = (pred[512,256]{1,0:T(8,128)(4,1)}, pred[512,256]{1,0:T(8,128)(4,1)S(1)}, u32[]{:S(2)}) copy-start(pred[512,256]{1,0:T(8,128)(4,1)S(1)} %get-tuple-element.41) | copy-start | bytes 393220
  14.7 8.1 copy-start.32
  15.3 8.0 copy-start.40
  22.5 1.5 copy-start.5
  22.6 0.8 copy-start.34
  24.3 27.9 %copy-start.20 = (bf16[512,32]{0,1:T(8,128)(2,1)}, bf16[512,32]{0,1:T(8,128)(2,1)S(1)}, u32[]{:S(2)}) copy-start(bf16[512,32]{0,1:T(8,128)(2,1)S(1)} %get-tuple-element.30) | copy-start | bytes 98308
  24.3 27.9 %copy-start.22 = (bf16[512,32]{0,1:T(8,128)(2,1)}, bf16[512,32]{0,1:T(8,128)(2,1)S(1)}, u32[]{:S(2)}) copy-start(bf16[512,32]{0,1:T(8,128)(2,1)S(1)} %get-tuple-element.31) | copy-start | bytes 98308
  24.3 42.3 %copy-start.16 = (f32[512,32]{0,1:T(8,128)}, f32[512,32]{0,1:T(8,128)S(1)}, u32[]{:S(2)}) copy-start(f32[512,32]{0,1:T(8,128)S(1)} %get-tuple-element.36) | copy-start | bytes 196612
  24.3 42.3 %copy-start.18 = (f32[512,32]{0,1:T(8,128)}, f32[512,32]{0,1:T(8,128)S(1)}, u32[]{:S(2)}) copy-start(f32[512,32]{0,1:T(8,128)S(1)} %get-tuple-element.37) | copy-start | bytes 196612
  68.4 10.2 %copy-start.3 = (bf16[512,8,512]{2,0,1:T(8,128)(2,1)S(1)}, bf16[512,8,512]{2,0,1:T(8,128)(2,1)}, u32[]{:S(2)}) copy-start(bf16[512,8,512]{2,0,1:T(8,128)(2,1)} %convert_bitcast_fusion.1) | copy-start | bytes 12582916
  68.4 10.2 %copy-start.14 = (bf16[512,512,1]{1,2,0:T(2,128)(2,1)S(1)}, bf16[512,512,1]{1,2,0:T(2,128)(2,1)}, u32[]{:S(2)}) copy-start(bf16[512,512,1]{1,2,0:T(2,128)(2,1)} %copy.32) | copy-start | bytes 1572868
  202.5 0.7 copy-start.29
  202.6 270.5 %all-reduce.7.cloned.1.call-start = ((), (), s32[]{:S(2)}) async-start(), calls=%async_computation.1 | async-start | bytes 14680064 | tf_op jit(solution)/shard_map/psum | solution.py:77
  319.7 18.0 %copy-start.1 = (bf16[512,7168]{1,0:T(8,128)(2,1)S(1)}, bf16[512,7168]{1,0:T(8,128)(2,1)}, u32[]{:S(2)}) copy-start(bf16[512,7168]{1,0:T(8,128)(2,1)} %get-tuple-element.15) | copy-start | bytes 22020100
  368.8 115.9 %copy-start.38 = (f32[1,7168]{1,0:T(1,128)S(1)}, f32[1,7168]{1,0:T(1,128)}, u32[]{:S(2)}) copy-start(f32[1,7168]{1,0:T(1,128)} %get-tuple-element.34) | copy-start | bytes 86020
  368.8 398.0 %all-reduce.9.cloned.1.call-start = ((), (), s32[]{:S(2)}) async-start(), calls=%async_computation.2 | async-start | bytes 14680064 | tf_op jit(solution)/shard_map/psum | solution.py:74
  484.7 9.7 %copy-start.42 = (f32[512]{0:T(512)S(1)}, f32[512]{0:T(512)}, u32[]{:S(2)}) copy-start(f32[512]{0:T(512)} %copy-done.41) | copy-start | bytes 6148
  484.7 9.7 %copy-start.46 = (f32[32]{0:T(128)S(1)}, f32[32]{0:T(128)}, u32[]{:S(2)}) copy-start(f32[32]{0:T(128)} %copy-done.45) | copy-start | bytes 388
  484.7 10.0 %copy-start.30 = (f32[1,512]{1,0:T(1,128)S(1)}, f32[1,512]{1,0:T(1,128)}, u32[]{:S(2)}) copy-start(f32[1,512]{1,0:T(1,128)} %get-tuple-element.38) | copy-start | bytes 6148
  494.2 1.0 copy-start.7
  494.7 20.1 %copy-start.24 = (bf16[512,32]{0,1:T(8,128)(2,1)}, bf16[512,32]{0,1:T(8,128)(2,1)S(1)}, u32[]{:S(2)}) copy-start(bf16[512,32]{0,1:T(8,128)(2,1)S(1)} %get-tuple-element.28) | copy-start | bytes 98308
  494.7 20.1 %copy-start.26 = (bf16[512,32]{0,1:T(8,128)(2,1)}, bf16[512,32]{0,1:T(8,128)(2,1)S(1)}, u32[]{:S(2)}) copy-start(bf16[512,32]{0,1:T(8,128)(2,1)S(1)} %get-tuple-element.29) | copy-start | bytes 98308
  494.7 20.1 %copy-start.36 = (f32[512]{0:T(512)}, f32[512]{0:T(512)S(1)}, u32[]{:S(2)}) copy-start(f32[512]{0:T(512)S(1)} %add_rsqrt_fusion.1) | copy-start | bytes 6148
  495.4 21.9 %copy-start.43 = (f32[1536]{0:T(1024)S(1)}, f32[1536]{0:T(1024)}, u32[]{:S(2)}) copy-start(f32[1536]{0:T(1024)} %get-tuple-element.6) | copy-start | bytes 18436
  517.3 5.9 copy-start.17
  517.3 5.9 copy-start.19
  517.3 6.1 copy-start.11
  527.5 10.9 %copy-start.4 = (bf16[512,8,512]{2,0,1:T(8,128)(2,1)S(1)}, bf16[512,8,512]{2,0,1:T(8,128)(2,1)}, u32[]{:S(2)}) copy-start(bf16[512,8,512]{2,0,1:T(8,128)(2,1)} %convert_bitcast_fusion) | copy-start | bytes 12582916
  527.5 10.9 %copy-start.15 = (bf16[512,512,1]{1,2,0:T(2,128)(2,1)S(1)}, bf16[512,512,1]{1,2,0:T(2,128)(2,1)}, u32[]{:S(2)}) copy-start(bf16[512,512,1]{1,2,0:T(2,128)(2,1)} %copy.39) | copy-start | bytes 1572868
  537.7 4.3 copy-start.10
  537.7 4.3 copy-start.13
  662.6 115.9 %copy-start.39 = (f32[1,7168]{1,0:T(1,128)S(1)}, f32[1,7168]{1,0:T(1,128)}, u32[]{:S(2)}) copy-start(f32[1,7168]{1,0:T(1,128)} %get-tuple-element.32) | copy-start | bytes 86020
  662.6 269.6 %all-reduce.11.cloned.1.call-start = ((), (), s32[]{:S(2)}) async-start(), calls=%async_computation.3 | async-start | bytes 14680064 | tf_op jit(solution)/shard_map/psum | solution.py:77
  778.5 18.2 %copy-start.2 = (bf16[512,7168]{1,0:T(8,128)(2,1)S(1)}, bf16[512,7168]{1,0:T(8,128)(2,1)}, u32[]{:S(2)}) copy-start(bf16[512,7168]{1,0:T(8,128)(2,1)} %get-tuple-element.9) | copy-start | bytes 22020100
  827.9 1.3 copy-start.6
  827.9 1.3 copy-start.33
  827.9 1.3 copy-start.35
  827.9 1.6 copy-start.8
  828.0 1.6 copy-start.31
  828.0 1.6 copy-start.37
  828.0 3.5 copy-start.21
  828.0 3.5 copy-start.23
  828.0 3.5 copy-start.25
  828.0 3.5 copy-start.27
Sparse Core Ops, SparseCore 0:
  202.7 105.3 all-reduce.4
  368.9 104.0 all-reduce.6
  662.7 104.0 all-reduce.8
  828.2 104.0 all-reduce.10
where the time goes:
time: 959 us; the launch traced here: 950 us
  matrix products  428 us (45%)
  waiting for transfers between devices  412 us (43%)
  other arithmetic  70.9 us (7%)
  local copies, waits for them, and re-layouts  22.9 us (2%)
  between operations  15.1 us (2%)
    psum x2, waiting for transfers between devices, local_layer(): attn_sum = lax.psum(attn_part, 'tp')  208 us
    psum x2, waiting for transfers between devices, local_layer(): mlp_sum = lax.psum(mlp_part, 'tp')  204 us
    dot_general x2, matrix products, latent_attention(): jnp.einsum('bhc,btc->bht', q_lat, ckv_old, preferred_element_type=jnp.flo...  106 us
    dot_general x2, matrix products, latent_attention(): jnp.einsum('bht,btc->bhc', jnp.where(at_pos, bf_zero, attn_prob), ckv_old...  88.3 us
    reduce_sum x6, other arithmetic, rms_norm(): jnp.mean(values * values, axis=-1, keepdims=True) + NORM_EPS  40.1 us
    dot_general x2, matrix products, attention_heads(): jnp.dot(normed, w_dq, preferred_element_type=jnp.float32)  39.1 us
    dot_general x2, matrix products, gated_mlp(): gate_pre = jnp.dot(mlp_in, w_gate, preferred_element_type=jnp.float32)  36.1 us
    dot_general x2, matrix products, gated_mlp(): up_pre = jnp.dot(mlp_in, w_up, preferred_element_type=jnp.float32)  31.6 us
  transfers between devices with their start and end apart: 4, of which 4 were waited for; matrix products, arithmetic and copies ran while one was open for 0% of the time, Pallas kernels for 0%

commit v1 on v0

v1 whole, which is shorter than its diff:
```python
import functools
import math
import jax
import jax.numpy as jnp
from jax import lax
from jax.experimental import pallas as pl
from jax.experimental.pallas import tpu as pltpu
from jax.sharding import PartitionSpec as P

NORM_EPS = 1e-6
ROPE_BASE = 10000.0
BF = jnp.bfloat16
F32 = jnp.float32
NT = (((1,), (1,)), ((), ()))
MESH = pl.DeviceIdType.MESH

SUB = 8
CHUNKS = 4
WIDE = 1024

ORDER_LAST = (
    'O00', 'O01', 'O02', 'A000', 'O03', 'A001', 'A002', 'A003', 'A100', 'A200', 'A101', 'B000', 'A102', 'A201',
    'A103', 'A202', 'B001', 'B100', 'B200', 'M10', 'B101', 'B002', 'A203', 'A010', 'B201', 'M11', 'B102', 'B003',
    'A011', 'A110', 'B202', 'M12', 'B103', 'A210', 'A012', 'B203', 'M13', 'B010', 'A111', 'A112', 'A013', 'A211',
    'B110', 'A212', 'B210', 'A113', 'B011', 'B012', 'B111', 'A213', 'B211', 'B112', 'B013', 'B212', 'B113', 'B213',
)
ORDER_MID = (
    'O00', 'O01', 'O02', 'A000', 'O03', 'A001', 'A002', 'A003', 'A100', 'A200', 'A101', 'B000', 'A102', 'A201',
    'A103', 'A202', 'B001', 'B100', 'B200', 'M10', 'B101', 'B002', 'A203', 'A010', 'B201', 'M11', 'B102', 'B003',
    'A011', 'A110', 'B202', 'M12', 'B103', 'A210', 'A012', 'B203', 'M13', 'A111', 'A112', 'A013', 'A211', 'A212',
    'A113', 'A213',
)


def rms_norm(values, norm_gain):
    values = values.astype(F32)
    inv_rms = lax.rsqrt(jnp.mean(values * values, axis=-1, keepdims=True) + NORM_EPS)
    return (values * inv_rms * norm_gain.astype(F32)).astype(BF)


def rotate(values, cos_part, sin_part):
    half_dim = values.shape[-1] // 2
    lo_half = values[..., :half_dim]
    hi_half = values[..., half_dim:]
    return jnp.concatenate([lo_half * cos_part - hi_half * sin_part, hi_half * cos_part + lo_half * sin_part], axis=-1)


def attn_body(sb, nslot, steps, layer, scale, pos_ref, q_ref, r_ref, c_hbm, k_hbm, cn_ref, kn_ref, o_ref, cbuf, kbuf, s_ref, f_ref, csem, ksem):
    heads = q_ref.shape[1]
    step = pl.program_id(0)
    base = step * sb
    nsub = sb // SUB
    total = steps * nsub

    def copies(t, slot):
        return (pltpu.make_async_copy(c_hbm.at[layer, pl.ds(t * SUB, SUB)], cbuf.at[slot], csem.at[slot]),
                pltpu.make_async_copy(k_hbm.at[layer, pl.ds(t * SUB, SUB)], kbuf.at[slot], ksem.at[slot]))

    @pl.when(step == 0)
    def _():
        for t in range(nslot):
            for c in copies(t, t):
                c.start()

    par = lax.rem(step, nslot // nsub) * nsub
    for i in range(sb):
        f_ref[i * heads:(i + 1) * heads, :] = jnp.full((heads, 128), pos_ref[base + i], jnp.int32)
    for j in range(nsub):
        slot = par + j
        for c in copies(step * nsub + j, slot):
            c.wait()
        for i in range(j * SUB, (j + 1) * SUB):
            s = lax.dot_general(q_ref[i], cbuf[slot, i - j * SUB], NT, preferred_element_type=F32)
            s_ref[i * heads:(i + 1) * heads, :] = s + jnp.dot(r_ref[i], kbuf[slot, i - j * SUB], preferred_element_type=F32)
    n = sb * heads
    col = lax.broadcasted_iota(jnp.int32, (n, s_ref.shape[1]), 1)
    pv = f_ref[:, 0:1]
    cn = cn_ref[...].astype(F32)[:, None, :]
    fresh = jnp.sum(q_ref[...].astype(F32) * cn, axis=-1, keepdims=True)
    fresh = fresh + jnp.sum(r_ref[...].astype(F32) * kn_ref[...].astype(F32)[:, None, :], axis=-1, keepdims=True)
    hit = col == pv
    s = jnp.where(hit, fresh.reshape(n, 1), s_ref[...]) * scale
    s = jnp.where(col <= pv, s, -jnp.inf)
    e = jnp.exp(s - jnp.max(s, axis=-1, keepdims=True))
    w = (e / jnp.sum(e, axis=-1, keepdims=True)).astype(BF).astype(F32)
    new_prob = jnp.sum(jnp.where(hit, w, 0.0), axis=-1, keepdims=True)
    new_part = new_prob.reshape(sb, heads, 1) * cn
    s_ref[...] = jnp.where(hit, 0.0, w)
    for j in range(nsub):
        slot = par + j
        for i in range(j * SUB, (j + 1) * SUB):
            ctx = jnp.dot(s_ref[i * heads:(i + 1) * heads, :].astype(BF), cbuf[slot, i - j * SUB], preferred_element_type=F32)
            o_ref[i] = (ctx + new_part[i]).astype(BF)
        nxt = step * nsub + j + nslot

        @pl.when(nxt < total)
        def _():
            for c in copies(nxt, slot):
                c.start()


def latent_attention(q_lat, q_rope, ckv, kpe_t, c_new, k_new, pos, layer, scale, sb=32, nslot=8):
    n, heads, lat = q_lat.shape
    rope = q_rope.shape[-1]
    keys = ckv.shape[2]

    def im3(b, p):
        return (b, 0, 0)

    spec = pltpu.PrefetchScalarGridSpec(
        num_scalar_prefetch=1, grid=(n // sb,),
        in_specs=[pl.BlockSpec((sb, heads, lat), im3), pl.BlockSpec((sb, heads, rope), im3),
                  pl.BlockSpec(memory_space=pl.ANY), pl.BlockSpec(memory_space=pl.ANY),
                  pl.BlockSpec((sb, lat), lambda b, p: (b, 0)), pl.BlockSpec((sb, rope), lambda b, p: (b, 0))],
        out_specs=pl.BlockSpec((sb, heads, lat), im3),
        scratch_shapes=[pltpu.VMEM((nslot, SUB, keys, lat), BF), pltpu.VMEM((nslot, SUB, rope, keys), BF),
                        pltpu.VMEM((sb * heads, keys), F32), pltpu.VMEM((sb * heads, 128), jnp.int32),
                        pltpu.SemaphoreType.DMA((nslot,)), pltpu.SemaphoreType.DMA((nslot,))])
    return pl.pallas_call(
        functools.partial(attn_body, sb, nslot, n // sb, layer, scale), grid_spec=spec, name='mla_attn',
        out_shape=jax.ShapeDtypeStruct((n, heads, lat), BF),
        compiler_params=pltpu.CompilerParams(dimension_semantics=('arbitrary',)),
        cost_estimate=pl.CostEstimate(flops=2 * n * heads * keys * (2 * lat + rope), bytes_accessed=n * keys * (lat + rope) * 2, transcendentals=n * heads * keys),
    )(pos, q_lat, q_rope, ckv, kpe_t, c_new, k_new)


def post_body(layer, last, *refs):
    if last:
        (ho_ref, x_hbm, gain_ref, wo_hbm, wg_hbm, wu_hbm, wd_hbm,
         out_hbm, wgu, wod, buf, r0, r1, r2, own, act, wsem, gsem, xsem, osem, ss, rs, ack) = refs
    else:
        (ho_ref, x_hbm, gain_ref, wo_hbm, wg_hbm, wu_hbm, wd_hbm,
         next_gain_ref, q_gain_ref, kv_gain_ref, cos_hbm, sin_hbm, wdq_hbm, wdkv_hbm,
         own_out, cq_out, ckv_out, kpe_out,
         wgu, wod, buf, r0, r1, r2, own, act, cos_v, sin_v, wsem, gsem, xsem, osem, ss, rs, ack) = refs
    depth = wo_hbm.shape[1]
    cols = wd_hbm.shape[1]
    width = wd_hbm.shape[2]
    rows = buf.shape[1]
    half, quart, eighth = rows // 2, rows // 4, rows // 8
    tiles = width // WIDE

    me = lax.axis_index('tp')
    c = lax.rem(me, 2)
    x = lax.rem(me // 2, 2)
    y = me // 4
    f = x * (1 - c) + y * c
    s = y * (1 - c) + x * c
    pair = y * 4 + x * 2 + (1 - c)
    n1 = (y * (1 - c) + (1 - y) * c) * 4 + ((1 - x) * (1 - c) + x * c) * 2 + c
    n2 = ((1 - y) * (1 - c) + y * c) * 4 + (x * (1 - c) + (1 - x) * c) * 2 + c
    half_own, half_oth = c * half, (1 - c) * half
    quart_own, quart_oth = half_own + f * quart, half_own + (1 - f) * quart
    eig_own, eig_oth = quart_own + s * eighth, quart_own + (1 - s) * eighth
    al = lambda v: pl.multiple_of(v, 16)

    barrier = pltpu.get_barrier_semaphore()
    for dev in (pair, n1, n2):
        pl.semaphore_signal(barrier, inc=1, device_id={'tp': dev}, device_id_type=MESH)

    wo_cp = [pltpu.make_async_copy(wo_hbm.at[layer, :, pl.ds(j * WIDE, WIDE)], wod.at[pl.ds(0, depth), pl.ds(j * WIDE, WIDE)], wsem.at[j]) for j in range(tiles)]
    for cp in wo_cp:
        cp.start()
    if last:
        x_cp = [pltpu.make_async_copy(x_hbm, own, xsem.at[0])]
    else:
        x_cp = [pltpu.make_async_copy(x_hbm.at[:, pl.ds(al(eig_own), eighth)], own, xsem.at[0]),
                pltpu.make_async_copy(cos_hbm.at[:, pl.ds(al(eig_own), eighth)], cos_v, xsem.at[1]),
                pltpu.make_async_copy(sin_hbm.at[:, pl.ds(al(eig_own), eighth)], sin_v, xsem.at[2])]
    for cp in x_cp:
        cp.start()
    gu_cp = []
    for j in range(cols // 128):
        gu_cp.append(pltpu.make_async_copy(wg_hbm.at[layer, :, pl.ds(j * 128, 128)], wgu.at[:, pl.ds(2 * j * 128, 128)], gsem.at[2 * j]))
        gu_cp.append(pltpu.make_async_copy(wu_hbm.at[layer, :, pl.ds(j * 128, 128)], wgu.at[:, pl.ds((2 * j + 1) * 128, 128)], gsem.at[2 * j + 1]))
    wd_cp = [pltpu.make_async_copy(wd_hbm.at[layer, :, pl.ds(j * WIDE, WIDE)], wod.at[:, pl.ds(j * WIDE, WIDE)], wsem.at[j]) for j in range(tiles)]
    if not last:
        dq = wdq_hbm.shape[2]
        dkv = wdkv_hbm.shape[1]
        lat = kv_gain_ref.shape[1]
        dq_cp = [pltpu.make_async_copy(wdq_hbm.at[layer + 1, :, pl.ds(j * 256, 256)], wgu.at[:, pl.ds(j * 256, 256)], gsem.at[j]) for j in range(dq // 256)]
        dkv_cp = [pltpu.make_async_copy(wdkv_hbm.at[layer + 1], wod.at[pl.ds(0, dkv)], wsem.at[0])]
    pl.semaphore_wait(barrier, 3)

    sent = {}

    def send(kind, ph, r, dev):
        k = 6 * ph + ('S0', 'S1', 'S2', 'G0', 'G1', 'G2').index(kind)
        if kind == 'S0':
            src, dst = buf.at[r, pl.ds(al(half_oth), half)], r0.at[r]
        elif kind == 'S1':
            src, dst = buf.at[r, pl.ds(al(quart_oth), quart)], r1.at[r]
        elif kind == 'S2':
            src, dst = buf.at[r, pl.ds(al(eig_oth), eighth)], r2.at[r]
        else:
            off, n = {'G0': (eig_own, eighth), 'G1': (quart_own, quart), 'G2': (half_own, half)}[kind]
            src = buf.at[r, pl.ds(al(off), n)]
            dst = src
        cp = pltpu.make_async_remote_copy(src_ref=src, dst_ref=dst, send_sem=ss.at[k, r], recv_sem=rs.at[k, r],
                                          device_id={'tp': dev}, device_id_type=MESH)
        cp.start()
        sent[kind, ph, r] = cp

    def landed(kind, ph, r, dev):
        sent[kind, ph, r].wait_recv()
        sent[kind, ph, r].wait_send()
        pl.semaphore_signal(ack.at[3 * ph + int(kind[1]), r], inc=1, device_id={'tp': dev}, device_id_type=MESH)

    def granted(kind, ph, r):
        pl.semaphore_wait(ack.at[3 * ph + int(kind[1]), r], 1)

    def add_rows(r, off, src, src_off, n):
        def tile(t, _):
            cs = pl.ds(pl.multiple_of(t * WIDE, WIDE), WIDE)
            rw = pl.ds(al(off), n)
            buf[r, rw, cs] = (buf[r, rw, cs].astype(F32) + src[r, pl.ds(al(src_off), n), cs].astype(F32)).astype(BF)
            return 0
        lax.fori_loop(0, tiles, tile, 0)

    def step_o(r):
        if r == 0:
            for cp in x_cp:
                cp.wait()

        def tile(t, _):
            if r == 0:
                pltpu.make_async_copy(wo_hbm.at[layer, :, pl.ds(0, WIDE)], wod.at[pl.ds(0, depth), pl.ds(0, WIDE)], wsem.at[t]).wait()
            cs = pl.ds(pl.multiple_of(t * WIDE, WIDE), WIDE)
            buf[r, :, cs] = jnp.dot(ho_ref[r], wod[0:depth, cs], preferred_element_type=F32).astype(BF)
            return 0
        lax.fori_loop(0, tiles, tile, 0)
        send('S0', 0, r, pair)
        if r == 0:
            for cp in gu_cp:
                cp.start()
        if r == CHUNKS - 1:
            for cp in wd_cp:
                cp.start()

    def step_m(r):
        if r == 0:
            for cp in gu_cp:
                cp.wait()

        def gate(j, _):
            cs = pl.ds(pl.multiple_of(j * 256, 256), 256)
            pre = jnp.dot(buf[r], wgu[:, cs], preferred_element_type=F32)
            act[:, pl.ds(pl.multiple_of(j * 128, 128), 128)] = (jax.nn.silu(pre[:, :128]) * pre[:, 128:]).astype(BF)
            return 0
        lax.fori_loop(0, cols // 128, gate, 0)
        if r == CHUNKS - 1 and not last:
            for cp in dq_cp:
                cp.start()
        if r == 0:
            for cp in wd_cp:
                cp.wait()
        for kind in ('G0', 'G1', 'G2'):
            sent[kind, 0, r].wait_send()

        def tile(t, _):
            cs = pl.ds(pl.multiple_of(t * WIDE, WIDE), WIDE)
            buf[r, :, cs] = jnp.dot(act[...], wod[:, cs], preferred_element_type=F32).astype(BF)
            return 0
        lax.fori_loop(0, tiles, tile, 0)
        send('S0', 1, r, pair)
        if r == CHUNKS - 1 and not last:
            for cp in dkv_cp:
                cp.start()

    def reduce_own(ph, r):
        def tile(t, acc):
            cs = pl.ds(pl.multiple_of(t * WIDE, WIDE), WIDE)
            v = own[r, :, cs].astype(F32) + (buf[r, pl.ds(al(eig_own), eighth), cs].astype(F32) + r2[r, :, cs].astype(F32))
            v = v.astype(BF)
            own[r, :, cs] = v
            if ph == 1 and last:
                buf[r, pl.ds(al(eig_own), eighth), cs] = v
            v = v.astype(F32)
            return acc + v * v
        acc = lax.fori_loop(0, tiles, tile, jnp.zeros((eighth, WIDE), F32))
        return lax.rsqrt(jnp.sum(acc, axis=-1, keepdims=True) * (1.0 / width) + NORM_EPS)

    def norm_own(r, inv, gain, put):
        def tile(t, _):
            cs = pl.ds(pl.multiple_of(t * WIDE, WIDE), WIDE)
            put(r, cs, (own[r, :, cs].astype(F32) * inv * gain[:, cs].astype(F32)).astype(BF))
            return 0
        lax.fori_loop(0, tiles, tile, 0)

    def put_buf(r, cs, v):
        buf[r, pl.ds(al(eig_own), eighth), cs] = v

    def put_r2(r, cs, v):
        r2[r, :, cs] = v

    for token in (ORDER_LAST if last else ORDER_MID):
        op, ph, r = token[:-2], int(token[-2]), int(token[-1])
        if op == 'O':
            step_o(r)
        elif op == 'M':
            step_m(r)
        elif op == 'A0':
            landed('S0', ph, r, pair)
            add_rows(r, quart_oth, r0, (1 - f) * quart, quart)
            add_rows(r, quart_own, r0, f * quart, quart)
            send('S1', ph, r, n1)
        elif op == 'A1':
            landed('S1', ph, r, n1)
            add_rows(r, eig_oth, r1, (1 - s) * eighth, eighth)
            add_rows(r, eig_own, r1, s * eighth, eighth)
            send('S2', ph, r, n2)
        elif op == 'A2':
            landed('S2', ph, r, n2)
            inv = reduce_own(ph, r)
            if ph == 0:
                norm_own(r, inv, gain_ref, put_buf)
            elif not last:
                norm_own(r, inv, next_gain_ref, put_r2)
            if ph == 0 or last:
                granted('S2', ph, r)
                send('G0', ph, r, n2)
        elif op == 'B0':
            sent['G0', ph, r].wait_recv()
            granted('S1', ph, r)
            send('G1', ph, r, n1)
        elif op == 'B1':
            sent['G1', ph, r].wait_recv()
            granted('S0', ph, r)
            send('G2', ph, r, pair)
        elif op == 'B2':
            sent['G2', ph, r].wait_recv()
            if ph == 1:
                cp = pltpu.make_async_copy(buf.at[r], out_hbm.at[r], osem.at[r])
                cp.start()
                sent['out', 1, r] = cp

    if last:
        for r in range(CHUNKS):
            for kind in ('G0', 'G1', 'G2'):
                sent[kind, 1, r].wait_send()
            sent['out', 1, r].wait()
        return

    own_cp = pltpu.make_async_copy(own, own_out, osem.at[0])
    own_cp.start()
    n = CHUNKS * eighth
    mine = pl.ds(al(eig_own), eighth)
    a = r2[...].reshape(n, width)
    for cp in dkv_cp:
        cp.wait()
    kv = lax.dot_general(a, wod[0:lat, :], NT, preferred_element_type=F32)
    inv = lax.rsqrt(jnp.mean(kv * kv, axis=-1, keepdims=True) + NORM_EPS)
    buf[:, mine, dq:dq + lat] = (kv * inv * kv_gain_ref[...].astype(F32)).astype(BF).reshape(CHUNKS, eighth, lat)
    kp = lax.dot_general(a, wod[lat:lat + 128, :], NT, preferred_element_type=F32)
    rope = dkv - lat
    lane = lax.broadcasted_iota(jnp.int32, (n, 128), 1)
    swap = jnp.where(lane < rope // 2, pltpu.roll(kp, 128 - rope // 2, 1), pltpu.roll(kp, rope // 2, 1))
    kp = jnp.where(lane < rope, kp * cos_v[...].reshape(n, 128) + swap * sin_v[...].reshape(n, 128), 0.0)
    buf[:, mine, dq + lat:dq + lat + 128] = kp.astype(BF).reshape(CHUNKS, eighth, 128)
    for cp in dq_cp:
        cp.wait()
    cq = [jnp.dot(a, wgu[:, j * 512:(j + 1) * 512], preferred_element_type=F32) for j in range(dq // 512)]
    inv = lax.rsqrt(sum(jnp.sum(v * v, axis=-1, keepdims=True) for v in cq) * (1.0 / dq) + NORM_EPS)
    for j, v in enumerate(cq):
        buf[:, mine, j * 512:(j + 1) * 512] = (v * inv * q_gain_ref[:, j * 512:(j + 1) * 512].astype(F32)).astype(BF).reshape(CHUNKS, eighth, 512)

    used = dq + lat + 128

    def gather(k, off, rows_n, dev):
        part = buf.at[:, pl.ds(al(off), rows_n), pl.ds(0, used)]
        cp = pltpu.make_async_remote_copy(src_ref=part, dst_ref=part, send_sem=ss.at[k, 0], recv_sem=rs.at[k, 0],
                                          device_id={'tp': dev}, device_id_type=MESH)
        cp.start()
        return cp

    for r in range(CHUNKS):
        granted('S2', 1, r)
    g0 = gather(9, eig_own, eighth, n2)
    g0.wait_recv()
    for r in range(CHUNKS):
        granted('S1', 1, r)
    g1 = gather(10, quart_own, quart, n1)
    g1.wait_recv()
    for r in range(CHUNKS):
        granted('S0', 1, r)
    g2 = gather(11, half_own, half, pair)
    g2.wait_recv()
    outs = [pltpu.make_async_copy(buf.at[:, :, pl.ds(0, dq)], cq_out, osem.at[1]),
            pltpu.make_async_copy(buf.at[:, :, pl.ds(dq, lat)], ckv_out, osem.at[2]),
            pltpu.make_async_copy(buf.at[:, :, pl.ds(dq + lat, 128)], kpe_out, osem.at[3])]
    for cp in outs:
        cp.start()
    for cp in (g0, g1, g2):
        cp.wait_send()
    own_cp.wait()
    for cp in outs:
        cp.wait()


def post_layer(layer, last, head_out, resid, mlp_gain, w_o, w_gate, w_up, w_down, more):
    n, width = head_out.shape[0], w_down.shape[2]
    rows = n // CHUNKS
    depth, cols = w_o.shape[1], w_down.shape[1]
    vm = pl.BlockSpec(memory_space=pltpu.VMEM)
    hb = pl.BlockSpec(memory_space=pl.ANY)
    args = [head_out.reshape(CHUNKS, rows, depth), resid, mlp_gain, w_o, w_gate, w_up, w_down]
    specs = [vm, hb, vm, hb, hb, hb, hb]
    scratch = [pltpu.VMEM((width, 2 * cols), BF), pltpu.VMEM((cols, width), BF), pltpu.VMEM((CHUNKS, rows, width), BF),
               pltpu.VMEM((CHUNKS, rows // 2, width), BF), pltpu.VMEM((CHUNKS, rows // 4, width), BF),
               pltpu.VMEM((CHUNKS, rows // 8, width), BF), pltpu.VMEM((CHUNKS, rows // 8, width), BF),
               pltpu.VMEM((rows, cols), BF)]
    if last:
        outs = jax.ShapeDtypeStruct((CHUNKS, rows, width), BF)
        out_specs = hb
    else:
        next_gain, q_gain, kv_gain, cos_t, sin_t, w_dq, w_dkv_t = more
        args += [next_gain, q_gain, kv_gain, cos_t, sin_t, w_dq, w_dkv_t]
        specs += [vm, vm, vm, hb, hb, hb, hb]
        scratch += [pltpu.VMEM((CHUNKS, rows // 8, 128), F32)] * 2
        outs = (jax.ShapeDtypeStruct((CHUNKS, rows // 8, width), BF), jax.ShapeDtypeStruct((CHUNKS, rows, w_dq.shape[2]), BF),
                jax.ShapeDtypeStruct((CHUNKS, rows, kv_gain.shape[1]), BF), jax.ShapeDtypeStruct((CHUNKS, rows, 128), BF))
        out_specs = (hb,) * 4
    scratch += [pltpu.SemaphoreType.DMA((width // WIDE,)), pltpu.SemaphoreType.DMA((2 * cols // 128,)),
                pltpu.SemaphoreType.DMA((3,)), pltpu.SemaphoreType.DMA((4,)),
                pltpu.SemaphoreType.DMA((12, CHUNKS)), pltpu.SemaphoreType.DMA((12, CHUNKS)),
                pltpu.SemaphoreType.REGULAR((6, CHUNKS))]
    return pl.pallas_call(
        functools.partial(post_body, layer, last), in_specs=specs, out_specs=out_specs, out_shape=outs, scratch_shapes=scratch,
        name='post_last' if last else 'post_mid',
        compiler_params=pltpu.CompilerParams(collective_id=1 if last else 0, has_side_effects=True, vmem_limit_bytes=67043328),
        cost_estimate=pl.CostEstimate(flops=2 * n * width * (depth + 3 * cols), bytes_accessed=2 * width * (depth + 3 * cols), transcendentals=n * cols),
    )(*args)


def solution(mesh):
    cache_spec = P(None, 'dp', None, None)
    head_spec = P(None, None, 'tp', None)
    weight_specs = (P(), P(), P(), P(), P(), head_spec, head_spec, head_spec, P(None, 'tp', None, None), P(), P(None, None, 'tp'), P(None, None, 'tp'), P(None, 'tp', None))
    in_specs = (P('dp', None), P('dp'), cache_spec, cache_spec) + weight_specs
    out_specs = (P('dp', None), P(None, 'dp', None), P(None, 'dp', None))

    def device_body(x_in, pos_ids, ckv_cache, kpe_cache, attn_gain, w_dq, q_gain, w_dkv, kv_gain, w_uq, w_uk, w_uv, w_o, mlp_gain, w_gate, w_up, w_down):
        n, width = x_in.shape
        rows = n // CHUNKS
        lat = w_uk.shape[1]
        nope = w_uk.shape[3]
        rope = kpe_cache.shape[3]
        half = rope // 2
        inv_freq = jnp.exp(jnp.arange(half, dtype=F32) * (-2.0 * math.log(ROPE_BASE) / rope))
        angles = pos_ids.astype(F32)[:, None] * inv_freq
        cos_p, sin_p = jnp.cos(angles), jnp.sin(angles)
        pad = jnp.zeros((n, 128 - rope), F32)
        cos_t = jnp.concatenate([cos_p, cos_p, pad], axis=1).reshape(CHUNKS, rows, 128)
        sin_t = jnp.concatenate([-sin_p, sin_p, pad], axis=1).reshape(CHUNKS, rows, 128)
        kpe_t = jnp.swapaxes(kpe_cache, 2, 3)
        w_dkv_t = jnp.swapaxes(w_dkv, 1, 2)
        w_o2 = w_o.reshape(w_o.shape[0], -1, width)
        scale = w_uq.shape[-1] ** -0.5

        def heads_of(layer, c_q, c_new, k_new):
            q_full = jnp.einsum('bc,chd->bhd', c_q, w_uq[layer], preferred_element_type=F32)
            q_nope = q_full[..., :nope].astype(BF)
            q_rope = rotate(q_full[..., nope:], cos_p[:, None], sin_p[:, None]).astype(BF)
            q_lat = jnp.einsum('bhn,chn->bhc', q_nope, w_uk[layer], preferred_element_type=F32).astype(BF)
            ctx = latent_attention(q_lat, q_rope, ckv_cache, kpe_t, c_new, k_new, pos_ids, layer, scale)
            return jnp.einsum('bhc,chv->bhv', ctx, w_uv[layer], preferred_element_type=F32).astype(BF).reshape(n, -1)

        normed = rms_norm(x_in, attn_gain[0])
        c_q = rms_norm(jnp.dot(normed, w_dq[0], preferred_element_type=F32), q_gain[0])
        kv = jnp.dot(normed, w_dkv[0], preferred_element_type=F32)
        c_new0 = rms_norm(kv[:, :lat], kv_gain[0])
        k_new0 = rotate(kv[:, lat:], cos_p, sin_p).astype(BF)
        head_out = heads_of(0, c_q, c_new0, k_new0)
        x_own, c_q, c_new1, k_new1 = post_layer(
            0, False, head_out, x_in.reshape(CHUNKS, rows, width), mlp_gain[0:1], w_o2, w_gate, w_up, w_down,
            (attn_gain[1:2], q_gain[1:2], kv_gain[1:2], cos_t, sin_t, w_dq, w_dkv_t))
        c_new1 = c_new1.reshape(n, lat)
        k_new1 = k_new1.reshape(n, 128)[:, :rope]
        head_out = heads_of(1, c_q.reshape(n, -1), c_new1, k_new1)
        x_out = post_layer(1, True, head_out, x_own, mlp_gain[1:2], w_o2, w_gate, w_up, w_down, None)
        return x_out.reshape(n, width), jnp.stack([c_new0, c_new1]), jnp.stack([k_new0, k_new1])

    return jax.shard_map(device_body, mesh=mesh, in_specs=in_specs, out_specs=out_specs, check_vma=False)
```

time: 959 us -> 576 us (0.60)
  Pallas kernels: 0 us -> 456 us
  waiting for transfers between devices: 412 us -> 0 us
  matrix products: 428 us -> 44 us
  other arithmetic: 70.9 us -> 22.9 us
  local copies, waits for them, and re-layouts: 22.9 us -> 41.9 us
  between operations: 15.1 us -> 1.48 us
    pallas_call x0 -> x4, Pallas kernels: none -> 456 us  [the longest x2 317 us: post_layer(): pl.pallas_call(functools.partial(post_body, layer, last), in_specs=specs,...]
    psum x4 -> x0, waiting for transfers between devices: 412 us -> none  [the longest x2 208 us: local_layer(): attn_sum = lax.psum(attn_part, 'tp')]
    dot_general x26 -> x6, matrix products: 418 us -> 36 us  [the longest x1 17.5 us: device_body(): jnp.dot(normed, w_dq[0], preferred_element_type=F32)]
    reduce_sum x6 -> x2, other arithmetic: 40.1 us -> 4.74 us  [rms_norm(): jnp.mean(values * values, axis=-1, keepdims=True) + NORM_EPS]
    unnamed x95 -> x52, local copies, waits for them, and re-layouts: 4.36 us -> 17.9 us
    convert_element_type x8 -> x1, other arithmetic: 12.3 us -> 0.93 us  [rms_norm(): return (values * inv_rms * norm_gain.astype(F32)).astype(BF)]
  transfers between devices with their start and end apart: 4 -> 0, of which waited for: 4 -> 0; matrix products, arithmetic and copies ran while one was open for 0% -> 0% of each run, Pallas kernels for 0% -> 0%
where the time goes in v1:
time: 576 us; the launch traced here: 566 us
  Pallas kernels  456 us (79%)
  matrix products  44 us (8%)
  local copies, waits for them, and re-layouts  41.9 us (7%)
  other arithmetic  22.9 us (4%)
    pallas_call x2, Pallas kernels, post_layer(): pl.pallas_call(functools.partial(post_body, layer, last), in_specs=specs,...  317 us
    pallas_call x2, Pallas kernels, latent_attention(): pl.pallas_call(functools.partial(attn_body, sb, nslot, n // sb, layer, sc...  139 us
    unnamed x52, local copies, waits for them, and re-layouts  17.9 us
    dot_general x1, matrix products, device_body(): jnp.dot(normed, w_dq[0], preferred_element_type=F32)  17.5 us

profile of v1, /device:TPU:1, one launch (start us, length us, event | category | flops | bytes accessed | tf_op | source)
XLA Modules:
  0.0 566.3 jit_solution(3853344745092160433)
XLA Ops:
  0.6 1.5 fusion.41
  2.2 4.6 fusion.3
  6.8 17.5 %multiply_reduce_fusion = (f32[512]{0:T(512)S(1)}, f32[512,1536]{1,0:T(8,128)S(1)}) fusion(bf16[2,7168,1536]{2,1,0:T(8,128)(2,1)} %refs_12_.1, bf16[512,7168]{1,0:T(8,128)(2,1)} %param.17, f32[7168]{0:T(1024)S(1)} %bitcast.78, f32[512]{0:T(512)S(1)} %add_rsqrt_fusion.2), kind=kOutput, calls=%fused_computation.20 | convolution fusion | flops 11290542080 | bytes 32538624 | tf_op jit(solution)/shard_map/dot_general | solution.py:469
  24.3 0.0 copy-start.18
  24.3 6.6 %fusion.37 = (bf16[1,1536,8,192]{1,3,2,0:T(8,128)(2,1)}, bf16[1,1536,8,192]{1,3,2,0:T(8,128)(2,1)S(1)}) fusion(bf16[2,1536,8,192]{1,3,2,0:T(8,128)(2,1)} %param.26), kind=kLoop, calls=%fused_computation.67 | loop fusion | bytes 18874368 | tf_op jit(solution)/shard_map/slice | solution.py:461
  30.9 2.7 fusion.17
  33.7 0.1 fusion.39
  33.8 1.5 copy-done.4
  35.3 0.8 copy.39
  36.1 2.0 copy.40
  38.1 10.9 %fusion.6 = f32[512,576]{1,0:T(8,128)S(1)} fusion(bf16[2,7168,576]{1,2,0:T(8,128)(2,1)} %param.24, bf16[512,7168]{1,0:T(8,128)(2,1)} %param.17, f32[7168]{0:T(1024)S(1)} %bitcast.79, f32[512]{0:T(512)S(1)} %add_rsqrt_fusion.2), kind=kOutput, calls=%fused_computation.10 | convolution fusion | flops 4242538496 | bytes 16807936 | tf_op jit(solution)/shard_map/dot_general | solution.py:470
  49.0 1.7 subtract_convert_fusion.2
  50.7 0.0 copy-start.8
  50.7 0.0 copy-start.10
  50.7 0.0 copy-start.14
  50.7 0.0 copy-start.15
  50.7 0.0 copy-done.1
  50.8 0.0 copy-start.22
  50.8 0.6 subtract_convert_fusion.1
  51.4 0.0 copy-start.12
  51.4 1.6 pad_maximum_fusion.r_ref
  53.0 0.0 copy-done.14
  53.0 0.8 pad_maximum_fusion.4.kn_ref
  53.7 0.1 multiply_reduce_fusion.1
  53.9 0.6 fusion.43
  54.5 0.0 copy-done
  54.5 0.9 multiply_convert_fusion.2.cn_ref
  55.4 1.1 slice_bitcast_fusion
  56.5 1.3 fusion.32
  57.8 0.0 copy-done.19
  57.9 0.0 copy-done.20
  57.9 4.4 copy.71
  62.3 69.3 %mla_attn.2 = bf16[512,8,512]{2,1,0:T(8,128)(2,1)} custom-call(s32[512]{0:T(512)} %pos_ref.3, bf16[512,8,512]{2,1,0:T(8,128)(2,1)} %bitcast.65, bf16[512,8,64]{2,1,0:T(8,128)(2,1)} %pad_maximum_fusion.r_ref, bf16[2,512,256,512]{3,2,1,0:T(8,128)(2,1)} %c_hbm.3, bf16[2,512,64,256]{3,2,1,0:T(8,128)(2,1)} %bitcast.58, ...), custom_call_target="tpu_custom_call" | custom-call | flops 2281701376 | bytes 150994944 | tf_op jit(solution)/shard_map/mla_attn/pallas_call | solution.py:119
  131.6 1.1 fusion.40
  132.8 1.4 copy-done.2
  134.2 1.4 fusion.29
  135.6 0.7 copy.27
  136.3 1.3 reshape_reshape.6.refs_0_
  137.6 1.0 fusion.36
  138.6 0.1 pad.12.clone
  138.7 1.0 maximum_maximum_fusion.1
  139.7 0.6 slice.105.refs_8_
  140.3 157.1 %post_mid.1 = (bf16[4,16,7168]{2,1,0:T(8,128)(2,1)}, bf16[4,128,1536]{2,1,0:T(8,128)(2,1)}, bf16[4,128,512]{2,1,0:T(8,128)(2,1)}, bf16[4,128,128]{2,1,0:T(8,128)(2,1)}) custom-call(bf16[4,128,1024]{2,1,0:T(8,128)(2,1)} %reshape_reshape.6.refs_0_, bf16[4,128,7168]{2,1,0:T(8,128)(2,1)} %bitcast.63, bf16[1,7168]{1,0:T(2,128)(2,1)} %get-tuple-element.33.refs_2_, ...), custom_call_target="tpu_custom_call" | custom-call | flops 32883343360 | bytes 64225280 | tf_op jit(solution)/shard_map/post_mid/pallas_call | solution.py:427
  297.4 5.2 fusion.44
  302.6 0.0 copy-start.6
  302.7 0.9 fusion.38
  303.5 0.9 copy-done.6
  304.5 1.8 copy.42
  306.3 2.0 copy.43
  308.3 2.3 subtract_convert_fusion
  310.6 1.6 pad_maximum_fusion.1.r_ref
  312.1 1.3 fusion.33
  313.5 4.4 copy.72
  317.9 0.7 slice_bitcast_fusion.2
  318.6 69.3 %mla_attn.3 = bf16[512,8,512]{2,1,0:T(8,128)(2,1)} custom-call(s32[512]{0:T(512)} %pos_ref.3, bf16[512,8,512]{2,1,0:T(8,128)(2,1)} %bitcast.64, bf16[512,8,64]{2,1,0:T(8,128)(2,1)} %pad_maximum_fusion.1.r_ref, bf16[2,512,256,512]{3,2,1,0:T(8,128)(2,1)} %c_hbm.3, bf16[2,512,64,256]{3,2,1,0:T(8,128)(2,1)} %bitcast.59, bf16[512,512]{1,0:T(8,128)(2,1)} %bitcast.73, ...), custom_call_target="tpu_custom_call" | custom-call | flops 2281701376 | bytes 150994944 | tf_op jit(solution)/shard_map/mla_attn/pallas_call | solution.py:119
  387.9 3.6 fusion.26
  391.6 0.7 copy.32
  392.3 1.3 reshape_reshape.7.refs_0_
  393.5 160.3 %post_last.1 = bf16[4,128,7168]{2,1,0:T(8,128)(2,1)} custom-call(bf16[4,128,1024]{2,1,0:T(8,128)(2,1)} %reshape_reshape.7.refs_0_, bf16[4,16,7168]{2,1,0:T(8,128)(2,1)} %get-tuple-element.10.refs_1_, bf16[1,7168]{1,0:T(2,128)(2,1)} %get-tuple-element.32.refs_2_, bf16[2,1024,7168]{2,1,0:T(8,128)(2,1)} %bitcast.61, bf16[2,7168,1152]{2,1,0:T(8,128)(2,1)} %refs_4_.3, ...), custom_call_target="tpu_custom_call" | custom-call | flops 32883343360 | bytes 64225280 | tf_op jit(solution)/shard_map/post_last/pallas_call | solution.py:427
  553.8 1.1 pad_maximum_fusion.3
  555.0 0.8 copy.33
  555.8 1.4 fusion.48
  557.1 2.1 pad_maximum_fusion.2
  559.3 6.6 %copy.74 = bf16[512,7168]{1,0:T(8,128)(2,1)} copy(bf16[512,7168]{1,0:T(8,128)(2,1)} %bitcast.62) | data formatting | bytes 14680064
  (37 shorter events, 0.1 us)
Async XLA Ops:
  24.3 6.6 %copy-start.18 = (bf16[2,1536]{1,0:T(2,128)(2,1)S(1)}, bf16[2,1536]{1,0:T(2,128)(2,1)}, u32[]{:S(2)}) copy-start(bf16[2,1536]{1,0:T(2,128)(2,1)} %param.23) | copy-start | bytes 18436
  33.7 1.6 copy-start.4
  38.1 10.9 %copy-start.21 = (s32[512]{0:T(512)S(1)}, s32[512]{0:T(512)}, u32[]{:S(2)}) copy-start(s32[512]{0:T(512)} %pos_ref.3) | copy-start | bytes 6148
  38.1 12.7 %copy-start.1 = (f32[512,8,32]{2,1,0:T(8,128)S(1)}, f32[512,8,32]{2,1,0:T(8,128)}, u32[]{:S(2)}) copy-start(f32[512,8,32]{2,1,0:T(8,128)} %copy.40) | copy-start | bytes 1572868
  49.0 5.5 copy-start
  50.7 2.3 copy-start.8
  50.7 2.2 copy-start.10
  50.7 2.2 copy-start.14
  50.7 2.2 copy-start.15
  50.8 3.2 copy-start.22
  51.4 4.0 copy-start.12
  53.0 3.6 copy-start.5
  53.9 3.9 copy-start.19
  54.5 3.4 copy-start.20
  62.3 69.3 %copy-start.13 = (bf16[2,512,8,128]{3,2,1,0:T(8,128)(2,1)S(1)}, bf16[2,512,8,128]{3,2,1,0:T(8,128)(2,1)}, u32[]{:S(2)}) copy-start(bf16[2,512,8,128]{3,2,1,0:T(8,128)(2,1)} %param.28) | copy-start | bytes 6291460
  131.6 2.6 copy-start.2
  302.6 1.8 copy-start.6
  302.7 5.6 copy-start.9
  302.7 5.6 copy-start.11
  308.3 3.9 copy-start.3
  308.3 3.9 copy-start.7
  313.5 4.4 copy-start.17
  318.6 69.3 %copy-start.16 = (bf16[1,512,8,128]{3,2,1,0:T(8,128)(2,1)S(1)}, bf16[1,512,8,128]{3,2,1,0:T(8,128)(2,1)}, u32[]{:S(2)}) copy-start(bf16[1,512,8,128]{3,2,1,0:T(8,128)(2,1)} %get-tuple-element.24) | copy-start | bytes 3145732

commit v2 on v1

v2 whole, which is shorter than its diff:
```python
import functools
import math
import jax
import jax.numpy as jnp
from jax import lax
from jax.experimental import pallas as pl
from jax.experimental.pallas import tpu as pltpu
from jax.sharding import PartitionSpec as P

NORM_EPS = 1e-6
ROPE_BASE = 10000.0
BF = jnp.bfloat16
F32 = jnp.float32
NT = (((1,), (1,)), ((), ()))
MESH = pl.DeviceIdType.MESH

SUB = 8
STEP = 32
SUBS = 5
SLOTS = 12
CHUNKS = 4
WIDE = 1024

ORDER_LAST = (
    'T', 'T', 'T', 'T', 'O00', 'T', 'A000', 'T', 'T', 'A100', 'T', 'O01', 'A200', 'T',
    'A001', 'T', 'B000', 'T', 'A101', 'T', 'O02', 'B100', 'A201', 'T', 'B200', 'A002', 'T', 'B001',
    'T', 'A102', 'T', 'O03', 'B101', 'A202', 'M', 'M', 'B201', 'A003', 'M', 'B002', 'M', 'M',
    'M', 'A103', 'M', 'A010', 'M', 'M', 'B102', 'A203', 'M', 'B202', 'M', 'A110', 'A011', 'B003',
    'M', 'M', 'M', 'A210', 'M', 'A111', 'A012', 'B010', 'B103', 'A211', 'B203', 'M', 'M', 'A112',
    'M', 'B011', 'M', 'M', 'B110', 'A212', 'A013', 'B111', 'B210', 'B012', 'B211', 'A113', 'B112', 'A213',
    'B212', 'B013', 'B113', 'B213',
)
ORDER_MID = (
    'T', 'T', 'T', 'T', 'O00', 'T', 'A000', 'T', 'T', 'A100', 'T', 'O01', 'A200', 'T',
    'A001', 'T', 'B000', 'T', 'A101', 'T', 'O02', 'B100', 'A201', 'T', 'B200', 'A002', 'T', 'B001',
    'T', 'A102', 'T', 'O03', 'B101', 'A202', 'M', 'M', 'B201', 'A003', 'M', 'B002', 'M', 'M',
    'M', 'A103', 'M', 'A010', 'M', 'M', 'B102', 'A203', 'M', 'B202', 'M', 'A110', 'A011', 'B003',
    'M', 'M', 'M', 'A210', 'M', 'A111', 'A012', 'B103', 'A211', 'B203', 'M', 'M', 'A112', 'M',
    'M', 'M', 'A212', 'A013', 'A113', 'A213',
)


def rms_norm(values, norm_gain):
    values = values.astype(F32)
    inv_rms = lax.rsqrt(jnp.mean(values * values, axis=-1, keepdims=True) + NORM_EPS)
    return (values * inv_rms * norm_gain.astype(F32)).astype(BF)


def rotate(values, cos_part, sin_part):
    half_dim = values.shape[-1] // 2
    lo_half = values[..., :half_dim]
    hi_half = values[..., half_dim:]
    return jnp.concatenate([lo_half * cos_part - hi_half * sin_part, hi_half * cos_part + lo_half * sin_part], axis=-1)


def layer_body(layer, last, scale, *refs):
    (pos_ref, cn_ref, kn_ref, uv_ref, q_hbm, qr_hbm, ckv_hbm, kpe_hbm, x_hbm, gain_ref, wo_hbm, wg_hbm, wu_hbm, wd_hbm), refs = refs[:14], refs[14:]
    if last:
        out_hbm, refs = refs[0], refs[1:]
    else:
        (next_gain_ref, q_gain_ref, kv_gain_ref, cos_hbm, sin_hbm, wdq_hbm, wdkv_hbm, own_out, cq_out, ckv_out, kpe_out), refs = refs[:11], refs[11:]
    (wgu, wod, buf, r0, r1, r2, own, act, sc, ctx, posv, wsem, gsem, xsem, osem, ss, rs, ack, credit, csem, ksem, qsem, rsem), refs = refs[:23], refs[23:]
    if not last:
        cos_v, sin_v = refs
    heads = 8
    keys = sc.shape[1]
    n_lat = q_hbm.shape[1]
    n_rope = kpe_hbm.shape[1] // (ckv_hbm.shape[1] // keys)
    steps = q_hbm.shape[0] // (STEP * heads)
    total = steps * (STEP // SUB)
    q_base = 3 * SUB * keys
    k_col = 4 * n_lat
    depth = wo_hbm.shape[1]
    cols = wd_hbm.shape[1]
    width = wd_hbm.shape[2]
    rows = buf.shape[1]
    half, quart, eighth = rows // 2, rows // 4, rows // 8
    tiles = width // WIDE

    me = lax.axis_index('tp')
    c = lax.rem(me, 2)
    x = lax.rem(me // 2, 2)
    y = me // 4
    f = x * (1 - c) + y * c
    s = y * (1 - c) + x * c
    pair = y * 4 + x * 2 + (1 - c)
    n1 = (y * (1 - c) + (1 - y) * c) * 4 + ((1 - x) * (1 - c) + x * c) * 2 + c
    n2 = ((1 - y) * (1 - c) + y * c) * 4 + (x * (1 - c) + (1 - x) * c) * 2 + c
    half_own, half_oth = c * half, (1 - c) * half
    quart_own, quart_oth = half_own + f * quart, half_own + (1 - f) * quart
    eig_own, eig_oth = quart_own + s * eighth, quart_own + (1 - s) * eighth
    al = lambda v: pl.multiple_of(v, 16)

    barrier = pltpu.get_barrier_semaphore()
    for dev in (pair, n1, n2):
        pl.semaphore_signal(barrier, inc=1, device_id={'tp': dev}, device_id_type=MESH)

    def slot_at(slot):
        return pl.multiple_of(lax.rem(slot, 3) * (SUB * keys), SUB * keys), pl.multiple_of(slot // 3 * n_lat, n_lat)

    def cache_copies(t):
        slot = lax.rem(t, SLOTS)
        row, col = slot_at(slot)
        return (pltpu.make_async_copy(ckv_hbm.at[layer, pl.ds(pl.multiple_of(t * (SUB * keys), SUB * keys), SUB * keys)],
                                      wgu.at[pl.ds(row, SUB * keys), pl.ds(col, n_lat)], csem.at[slot]),
                pltpu.make_async_copy(kpe_hbm.at[layer, pl.ds(pl.multiple_of(t * (SUB * n_rope), SUB * n_rope), SUB * n_rope)],
                                      wgu.at[pl.ds(pl.multiple_of(slot * (SUB * n_rope), SUB * n_rope), SUB * n_rope), pl.ds(k_col, keys)], ksem.at[slot]))

    def q_at(k):
        return pl.multiple_of(q_base + lax.rem(k, 4) * (STEP * heads), STEP * heads), pl.multiple_of(k // 4 * n_lat, n_lat)

    def q_copies(k):
        row, col = q_at(k)
        n = STEP * heads
        out = [pltpu.make_async_copy(q_hbm.at[pl.ds(pl.multiple_of(k * n, n), n)], wgu.at[pl.ds(row, n), pl.ds(col, n_lat)], qsem.at[k])]
        for i in range(2):
            out.append(pltpu.make_async_copy(qr_hbm.at[pl.ds(pl.multiple_of(k * n + i * 128, 128), 128)],
                                             wod.at[pl.ds(depth, 128), pl.ds(pl.multiple_of((2 * k + i) * 128, 128), 128)], rsem.at[2 * k + i]))
        return out

    def start_all(cps):
        for cp in cps:
            cp.start()

    def wait_all(cps):
        for cp in cps:
            cp.wait()

    start_all(q_copies(0))
    for t in range(STEP // SUB):
        start_all(cache_copies(t))
    for k in range(1, steps):
        start_all(q_copies(k))
    for t in range(STEP // SUB, SLOTS):
        start_all(cache_copies(t))

    wo_cp = [pltpu.make_async_copy(wo_hbm.at[layer, :, pl.ds(j * WIDE, WIDE)], wod.at[pl.ds(0, depth), pl.ds(j * WIDE, WIDE)], wsem.at[j]) for j in range(tiles)]
    for cp in wo_cp:
        cp.start()
    if last:
        x_cp = [pltpu.make_async_copy(x_hbm, own, xsem.at[0])]
    else:
        x_cp = [pltpu.make_async_copy(x_hbm.at[:, pl.ds(al(eig_own), eighth)], own, xsem.at[0]),
                pltpu.make_async_copy(cos_hbm.at[:, pl.ds(al(eig_own), eighth)], cos_v, xsem.at[1]),
                pltpu.make_async_copy(sin_hbm.at[:, pl.ds(al(eig_own), eighth)], sin_v, xsem.at[2])]
    for cp in x_cp:
        cp.start()
    gu_cp = []
    for j in range(cols // 128):
        gu_cp.append(pltpu.make_async_copy(wg_hbm.at[layer, :, pl.ds(j * 128, 128)], wgu.at[:, pl.ds(2 * j * 128, 128)], gsem.at[2 * j]))
        gu_cp.append(pltpu.make_async_copy(wu_hbm.at[layer, :, pl.ds(j * 128, 128)], wgu.at[:, pl.ds((2 * j + 1) * 128, 128)], gsem.at[2 * j + 1]))
    wd_cp = [pltpu.make_async_copy(wd_hbm.at[layer, :, pl.ds(j * WIDE, WIDE)], wod.at[:, pl.ds(j * WIDE, WIDE)], wsem.at[j]) for j in range(tiles)]
    if not last:
        dq = wdq_hbm.shape[2]
        dkv = wdkv_hbm.shape[1]
        lat = kv_gain_ref.shape[1]
        dq_cp = [pltpu.make_async_copy(wdq_hbm.at[layer + 1, :, pl.ds(j * 256, 256)], wgu.at[:, pl.ds(j * 256, 256)], gsem.at[j]) for j in range(dq // 256)]
        dkv_cp = [pltpu.make_async_copy(wdkv_hbm.at[layer + 1], wod.at[pl.ds(0, dkv)], wsem.at[0])]
    pl.semaphore_wait(barrier, 3)

    def remote(kind, ph, r):
        dev = {'0': pair, '1': n1, '2': n2}[kind[1]] if kind[0] == 'S' else {'0': n2, '1': n1, '2': pair}[kind[1]]
        k = 6 * ph + ('S0', 'S1', 'S2', 'G0', 'G1', 'G2').index(kind)
        if kind == 'S0':
            src, dst = buf.at[r, pl.ds(al(half_oth), half)], r0.at[r % 2]
        elif kind == 'S1':
            src, dst = buf.at[r, pl.ds(al(quart_oth), quart)], r1.at[r]
        elif kind == 'S2':
            src, dst = buf.at[r, pl.ds(al(eig_oth), eighth)], r2.at[r]
        else:
            off, n = {'G0': (eig_own, eighth), 'G1': (quart_own, quart), 'G2': (half_own, half)}[kind]
            src = buf.at[r, pl.ds(al(off), n)]
            dst = src
        return pltpu.make_async_remote_copy(src_ref=src, dst_ref=dst, send_sem=ss.at[k, r], recv_sem=rs.at[k, r],
                                            device_id={'tp': dev}, device_id_type=MESH)

    def send(kind, ph, r):
        if kind == 'S0' and (ph, r) not in ((0, 0), (0, 1)):
            pl.semaphore_wait(credit, 1)
        remote(kind, ph, r).start()

    def landed(kind, ph, r, dev):
        remote(kind, ph, r).wait_recv()
        remote(kind, ph, r).wait_send()
        pl.semaphore_signal(ack.at[3 * ph + int(kind[1]), r], inc=1, device_id={'tp': dev}, device_id_type=MESH)

    def granted(kind, ph, r):
        pl.semaphore_wait(ack.at[3 * ph + int(kind[1]), r], 1)

    def add_rows(r, off, src, src_off, n, slot):
        def tile(t, _):
            cs = pl.ds(pl.multiple_of(t * WIDE, WIDE), WIDE)
            rw = pl.ds(al(off), n)
            buf[r, rw, cs] = (buf[r, rw, cs].astype(F32) + src[slot, pl.ds(al(src_off), n), cs].astype(F32)).astype(BF)
            return 0
        lax.fori_loop(0, tiles, tile, 0)

    def out_copy(r):
        return pltpu.make_async_copy(buf.at[r], out_hbm.at[r], osem.at[r])

    def step_o(r):
        if r == 0:
            for cp in x_cp:
                cp.wait()

        def tile(t, _):
            if r == 0:
                pltpu.make_async_copy(wo_hbm.at[layer, :, pl.ds(0, WIDE)], wod.at[pl.ds(0, depth), pl.ds(0, WIDE)], wsem.at[t]).wait()
            cs = pl.ds(pl.multiple_of(t * WIDE, WIDE), WIDE)
            buf[r, :, cs] = jnp.dot(act[:, 0:depth], wod[0:depth, cs], preferred_element_type=F32).astype(BF)
            return 0
        lax.fori_loop(0, tiles, tile, 0)
        send('S0', 0, r)

    def step_m(m):
        r = m // SUBS
        part = lax.rem(m, SUBS)
        n_gate = cols // 128 // 3

        def gate(j, _):
            @pl.when(r == 0)
            def _():
                for i in range(2):
                    pltpu.make_async_copy(wg_hbm.at[layer, :, pl.ds(0, 128)], wgu.at[:, pl.ds(0, 128)], gsem.at[2 * j + i]).wait()
            cs = pl.ds(pl.multiple_of(j * 256, 256), 256)
            pre = jnp.dot(buf[r], wgu[:, cs], preferred_element_type=F32)
            act[:, pl.ds(pl.multiple_of(j * 128, 128), 128)] = (jax.nn.silu(pre[:, :128]) * pre[:, 128:]).astype(BF)
            return 0

        def tile(t, _):
            cs = pl.ds(pl.multiple_of(t * WIDE, WIDE), WIDE)
            buf[r, :, cs] = jnp.dot(act[...], wod[:, cs], preferred_element_type=F32).astype(BF)
            return 0

        @pl.when(part < 3)
        def _():
            lax.fori_loop(part * n_gate, (part + 1) * n_gate, gate, 0)

        @pl.when(m == 3)
        def _():
            wait_all(wd_cp)

        @pl.when(part == 3)
        def _():
            for kind in ('G0', 'G1', 'G2'):
                remote(kind, 0, r).wait_send()

        @pl.when(part >= 3)
        def _():
            cut = (tiles + 1) // 2
            lax.fori_loop((part - 3) * cut, cut + (part - 3) * (tiles - cut), tile, 0)

    def reduce_own(ph, r):
        def tile(t, acc):
            cs = pl.ds(pl.multiple_of(t * WIDE, WIDE), WIDE)
            v = own[r, :, cs].astype(F32) + (buf[r, pl.ds(al(eig_own), eighth), cs].astype(F32) + r2[r, :, cs].astype(F32))
            v = v.astype(BF)
            own[r, :, cs] = v
            if ph == 1 and last:
                buf[r, pl.ds(al(eig_own), eighth), cs] = v
            v = v.astype(F32)
            return acc + v * v
        acc = lax.fori_loop(0, tiles, tile, jnp.zeros((eighth, WIDE), F32))
        return lax.rsqrt(jnp.sum(acc, axis=-1, keepdims=True) * (1.0 / width) + NORM_EPS)

    def norm_own(r, inv, gain, put):
        def tile(t, _):
            cs = pl.ds(pl.multiple_of(t * WIDE, WIDE), WIDE)
            put(r, cs, (own[r, :, cs].astype(F32) * inv * gain[:, cs].astype(F32)).astype(BF))
            return 0
        lax.fori_loop(0, tiles, tile, 0)

    def put_buf(r, cs, v):
        buf[r, pl.ds(al(eig_own), eighth), cs] = v

    def put_r2(r, cs, v):
        r2[r, :, cs] = v

    def step_t(k):
        rows_n = STEP * heads
        nsub = STEP // SUB
        wait_all(q_copies(k))
        q_row, q_col = q_at(k)
        qr_cols = [pl.ds(pl.multiple_of((2 * k + i) * 128, 128), 128) for i in range(2)]
        for i in range(STEP):
            posv[i * heads:(i + 1) * heads, :] = jnp.full((heads, 128), pos_ref[k * STEP + i], jnp.int32)
        slots = []
        for j in range(nsub):
            t = k * nsub + j
            wait_all(cache_copies(t))
            slot = lax.rem(t, SLOTS)
            row, col = slot_at(slot)
            slots.append((row, col))
            k_row = pl.multiple_of(slot * (SUB * n_rope), SUB * n_rope)
            for e in range(SUB):
                i = j * SUB + e
                lo = i // 2 * 16
                up = i % 2 * heads
                keys_i = wgu[pl.ds(row + e * keys, keys), pl.ds(col, n_lat)]
                s_i = lax.dot_general(wgu[pl.ds(q_row + lo, 16), pl.ds(q_col, n_lat)], keys_i, NT, preferred_element_type=F32)
                s_i = s_i + jnp.dot(wod[depth + lo % 128:depth + lo % 128 + 16, qr_cols[lo // 128]][:, :n_rope], wgu[pl.ds(k_row + e * n_rope, n_rope), pl.ds(k_col, keys)], preferred_element_type=F32)
                sc[i * heads:(i + 1) * heads, :] = s_i[up:up + heads]
        seqs = pl.ds(pl.multiple_of(k * STEP, STEP), STEP)
        col_id = lax.broadcasted_iota(jnp.int32, (rows_n, keys), 1)
        pv = posv[:, 0:1]
        cn = cn_ref[seqs, :].astype(F32)
        kn = kn_ref[seqs, :].astype(F32)
        fresh = jnp.sum(wgu[pl.ds(q_row, rows_n), pl.ds(q_col, n_lat)].astype(F32) * jnp.broadcast_to(cn[:, None, :], (STEP, heads, n_lat)).reshape(rows_n, n_lat), axis=-1, keepdims=True)
        kn8 = jnp.broadcast_to(kn[:, None, :], (STEP, heads, 128)).reshape(rows_n, 128)
        fresh = fresh + jnp.sum(jnp.concatenate([wod[depth:depth + 128, cs].astype(F32) for cs in qr_cols], axis=0) * kn8, axis=-1, keepdims=True)
        hit = col_id == pv
        sco = jnp.where(hit, fresh, sc[...]) * scale
        sco = jnp.where(col_id <= pv, sco, -jnp.inf)
        e_x = jnp.exp(sco - jnp.max(sco, axis=-1, keepdims=True))
        w = (e_x / jnp.sum(e_x, axis=-1, keepdims=True)).astype(BF).astype(F32)
        new_prob = jnp.sum(jnp.where(hit, w, 0.0), axis=-1, keepdims=True)
        new_part = (new_prob.reshape(STEP, heads, 1) * cn[:, None, :]).reshape(rows_n, n_lat)
        for b in range(n_lat // 128):
            ctx[b] = new_part[:, b * 128:(b + 1) * 128]
        sc[...] = jnp.where(hit, 0.0, w)
        for j in range(nsub):
            row, col = slots[j]
            for e in range(SUB):
                rw = slice((j * SUB + e) * heads, (j * SUB + e + 1) * heads)
                val = jnp.dot(sc[rw, :].astype(BF), wgu[pl.ds(row + e * keys, keys), pl.ds(col, n_lat)], preferred_element_type=F32)
                for b in range(n_lat // 128):
                    ctx[b, rw, :] = (ctx[b, rw, :] + val[:, b * 128:(b + 1) * 128]).astype(BF).astype(F32)
            nxt = k * nsub + j + SLOTS

            @pl.when(nxt < total)
            def _():
                start_all(cache_copies(nxt))
        out_rows = pl.ds(pl.multiple_of(lax.rem(k, steps // CHUNKS) * STEP, STEP), STEP)
        for h in range(heads):
            ctx_h = jnp.concatenate([ctx[b, pl.ds(h, STEP, stride=heads), :] for b in range(n_lat // 128)], axis=1).astype(BF)
            act[out_rows, h * 128:(h + 1) * 128] = jnp.dot(ctx_h, uv_ref[:, h * 128:(h + 1) * 128], preferred_element_type=F32).astype(BF)

    def event(op, ph, r):
        if op == 'O':
            step_o(r)
        elif op == 'A0':
            landed('S0', ph, r, pair)
            add_rows(r, quart_oth, r0, (1 - f) * quart, quart, r % 2)
            add_rows(r, quart_own, r0, f * quart, quart, r % 2)
            if (ph, r) not in ((1, 2), (1, 3)):
                pl.semaphore_signal(credit, inc=1, device_id={'tp': pair}, device_id_type=MESH)
            send('S1', ph, r)
        elif op == 'A1':
            landed('S1', ph, r, n1)
            add_rows(r, eig_oth, r1, (1 - s) * eighth, eighth, r)
            add_rows(r, eig_own, r1, s * eighth, eighth, r)
            send('S2', ph, r)
        elif op == 'A2':
            landed('S2', ph, r, n2)
            inv = reduce_own(ph, r)
            if ph == 0:
                norm_own(r, inv, gain_ref, put_buf)
            elif not last:
                norm_own(r, inv, next_gain_ref, put_r2)
            if ph == 0 or last:
                granted('S2', ph, r)
                send('G0', ph, r)
        elif op == 'B0':
            remote('G0', ph, r).wait_recv()
            granted('S1', ph, r)
            send('G1', ph, r)
        elif op == 'B1':
            remote('G1', ph, r).wait_recv()
            granted('S0', ph, r)
            send('G2', ph, r)
        elif op == 'B2':
            remote('G2', ph, r).wait_recv()
            if ph == 1:
                out_copy(r).start()


    hooks = {'T': [[]], 'M': [[]]}
    now = 'T'
    for token in (ORDER_LAST if last else ORDER_MID):
        if token in hooks:
            now = token
            hooks[now].append([])
        else:
            hooks[now][-1].append((token[:-2], int(token[-2]), int(token[-1])))

    def run(name, step, k):
        step(k)
        for at, evs in enumerate(hooks[name][1:]):
            if evs or name == 'M':
                @pl.when(k == at)
                def _(at=at, evs=evs):
                    if name == 'M' and at % SUBS == SUBS - 1:
                        send('S0', 1, at // SUBS)
                        if at == SUBS * CHUNKS - 1 and not last:
                            start_all(dkv_cp)
                    if name == 'M' and at == SUBS * CHUNKS - 3 and not last:
                        start_all(dq_cp)
                    for ev in evs:
                        if ev[0] == 'O' and ev[2] == CHUNKS - 1:
                            start_all(gu_cp)
                        event(*ev)
                        if ev[0] == 'O' and ev[2] == CHUNKS - 1:
                            start_all(wd_cp)
        return 0
    lax.fori_loop(0, steps, lambda k, _: run('T', step_t, k), 0)
    lax.fori_loop(0, SUBS * CHUNKS, lambda k, _: run('M', step_m, k), 0)

    if last:
        for r in range(CHUNKS):
            for kind in ('G0', 'G1', 'G2'):
                remote(kind, 1, r).wait_send()
            out_copy(r).wait()
        return

    own_cp = pltpu.make_async_copy(own, own_out, osem.at[0])
    own_cp.start()
    n = CHUNKS * eighth
    mine = pl.ds(al(eig_own), eighth)
    def a():
        return r2[...].reshape(n, width)

    for cp in dkv_cp:
        cp.wait()
    kv = lax.dot_general(a(), wod[0:lat, :], NT, preferred_element_type=F32)
    inv = lax.rsqrt(jnp.mean(kv * kv, axis=-1, keepdims=True) + NORM_EPS)
    buf[:, mine, dq:dq + lat] = (kv * inv * kv_gain_ref[...].astype(F32)).astype(BF).reshape(CHUNKS, eighth, lat)
    kp = lax.dot_general(a(), wod[lat:lat + 128, :], NT, preferred_element_type=F32)
    rope = dkv - lat
    lane = lax.broadcasted_iota(jnp.int32, (n, 128), 1)
    swap = jnp.where(lane < rope // 2, pltpu.roll(kp, 128 - rope // 2, 1), pltpu.roll(kp, rope // 2, 1))
    kp = jnp.where(lane < rope, kp * cos_v[...].reshape(n, 128) + swap * sin_v[...].reshape(n, 128), 0.0)
    buf[:, mine, dq + lat:dq + lat + 128] = kp.astype(BF).reshape(CHUNKS, eighth, 128)
    for cp in dq_cp:
        cp.wait()
    total_sq = jnp.zeros((n, 1), F32)
    for j in range(dq // 512):
        v = jnp.dot(a(), wgu[:, j * 512:(j + 1) * 512], preferred_element_type=F32)
        total_sq = total_sq + jnp.sum(v * v, axis=-1, keepdims=True)
        for b in range(4):
            ctx[b, j * n:(j + 1) * n, :] = v[:, b * 128:(b + 1) * 128]
    inv = lax.rsqrt(total_sq * (1.0 / dq) + NORM_EPS)
    for j in range(dq // 128):
        cs = slice(j * 128, (j + 1) * 128)
        v = ctx[j % 4, j // 4 * n:(j // 4 + 1) * n, :]
        buf[:, mine, cs] = (v * inv * q_gain_ref[:, cs].astype(F32)).astype(BF).reshape(CHUNKS, eighth, 128)

    used = dq + lat + 128

    def gather(k, off, rows_n, dev):
        part = buf.at[:, pl.ds(al(off), rows_n), pl.ds(0, used)]
        cp = pltpu.make_async_remote_copy(src_ref=part, dst_ref=part, send_sem=ss.at[k, 0], recv_sem=rs.at[k, 0],
                                          device_id={'tp': dev}, device_id_type=MESH)
        cp.start()
        return cp

    for r in range(CHUNKS):
        granted('S2', 1, r)
    g0 = gather(9, eig_own, eighth, n2)
    g0.wait_recv()
    for r in range(CHUNKS):
        granted('S1', 1, r)
    g1 = gather(10, quart_own, quart, n1)
    g1.wait_recv()
    for r in range(CHUNKS):
        granted('S0', 1, r)
    g2 = gather(11, half_own, half, pair)
    g2.wait_recv()
    outs = [pltpu.make_async_copy(buf.at[:, :, pl.ds(0, dq)], cq_out, osem.at[1]),
            pltpu.make_async_copy(buf.at[:, :, pl.ds(dq, lat)], ckv_out, osem.at[2]),
            pltpu.make_async_copy(buf.at[:, :, pl.ds(dq + lat, 128)], kpe_out, osem.at[3])]
    for cp in outs:
        cp.start()
    for cp in (g0, g1, g2):
        cp.wait_send()
    own_cp.wait()
    for cp in outs:
        cp.wait()


def fused_layer(layer, last, scale, pos, c_new, k_new, w_uv, q_lat, q_rope, ckv, kpe_t, resid, mlp_gain, w_o, w_gate, w_up, w_down, more):
    n, width = c_new.shape[0], w_down.shape[2]
    lat = c_new.shape[1]
    keys = kpe_t.shape[2]
    rows = n // CHUNKS
    depth, cols = w_o.shape[1], w_down.shape[1]
    vm = pl.BlockSpec(memory_space=pltpu.VMEM)
    hb = pl.BlockSpec(memory_space=pl.ANY)
    args = [pos, c_new, k_new, w_uv, q_lat, q_rope, ckv, kpe_t, resid, mlp_gain, w_o, w_gate, w_up, w_down]
    specs = [pl.BlockSpec(memory_space=pltpu.SMEM), vm, vm, vm, hb, hb, hb, hb, hb, vm, hb, hb, hb, hb]
    scratch = [pltpu.VMEM((width, 2 * cols), BF), pltpu.VMEM((cols, width), BF), pltpu.VMEM((CHUNKS, rows, width), BF),
               pltpu.VMEM((2, rows // 2, width), BF), pltpu.VMEM((CHUNKS, rows // 4, width), BF),
               pltpu.VMEM((CHUNKS, rows // 8, width), BF), pltpu.VMEM((CHUNKS, rows // 8, width), BF),
               pltpu.VMEM((rows, cols), BF), pltpu.VMEM((STEP * 8, keys), F32), pltpu.VMEM((lat // 128, STEP * 8, 128), F32), pltpu.VMEM((STEP * 8, 128), jnp.int32)]
    if last:
        outs = jax.ShapeDtypeStruct((CHUNKS, rows, width), BF)
        out_specs = hb
    else:
        next_gain, q_gain, kv_gain, cos_t, sin_t, w_dq, w_dkv_t = more
        args += [next_gain, q_gain, kv_gain, cos_t, sin_t, w_dq, w_dkv_t]
        specs += [vm, vm, vm, hb, hb, hb, hb]
        outs = (jax.ShapeDtypeStruct((CHUNKS, rows // 8, width), BF), jax.ShapeDtypeStruct((CHUNKS, rows, w_dq.shape[2]), BF),
                jax.ShapeDtypeStruct((CHUNKS, rows, kv_gain.shape[1]), BF), jax.ShapeDtypeStruct((CHUNKS, rows, 128), BF))
        out_specs = (hb,) * 4
    scratch += [pltpu.SemaphoreType.DMA((width // WIDE,)), pltpu.SemaphoreType.DMA((2 * cols // 128,)),
                pltpu.SemaphoreType.DMA((3,)), pltpu.SemaphoreType.DMA((4,)),
                pltpu.SemaphoreType.DMA((12, CHUNKS)), pltpu.SemaphoreType.DMA((12, CHUNKS)),
                pltpu.SemaphoreType.REGULAR((6, CHUNKS)), pltpu.SemaphoreType.REGULAR, pltpu.SemaphoreType.DMA((SLOTS,)), pltpu.SemaphoreType.DMA((SLOTS,)),
                pltpu.SemaphoreType.DMA((n // STEP,)), pltpu.SemaphoreType.DMA((2 * n // STEP,))]
    if not last:
        scratch += [pltpu.VMEM((CHUNKS, rows // 8, 128), F32)] * 2
    return pl.pallas_call(
        functools.partial(layer_body, layer, last, scale), in_specs=specs, out_specs=out_specs, out_shape=outs, scratch_shapes=scratch,
        name='layer_last' if last else 'layer_mid',
        compiler_params=pltpu.CompilerParams(collective_id=1 if last else 0, has_side_effects=True, vmem_limit_bytes=67043328),
        cost_estimate=pl.CostEstimate(flops=2 * n * (width * (depth + 3 * cols) + 8 * keys * 2 * lat), bytes_accessed=2 * width * (depth + 3 * cols) + 2 * n * keys * lat, transcendentals=n * cols),
    )(*args)


def solution(mesh):
    cache_spec = P(None, 'dp', None, None)
    head_spec = P(None, None, 'tp', None)
    weight_specs = (P(), P(), P(), P(), P(), head_spec, head_spec, head_spec, P(None, 'tp', None, None), P(), P(None, None, 'tp'), P(None, None, 'tp'), P(None, 'tp', None))
    in_specs = (P('dp', None), P('dp'), cache_spec, cache_spec) + weight_specs
    out_specs = (P('dp', None), P(None, 'dp', None), P(None, 'dp', None))

    def device_body(x_in, pos_ids, ckv_cache, kpe_cache, attn_gain, w_dq, q_gain, w_dkv, kv_gain, w_uq, w_uk, w_uv, w_o, mlp_gain, w_gate, w_up, w_down):
        n, width = x_in.shape
        rows = n // CHUNKS
        lat = w_uk.shape[1]
        nope = w_uk.shape[3]
        rope = kpe_cache.shape[3]
        half = rope // 2
        inv_freq = jnp.exp(jnp.arange(half, dtype=F32) * (-2.0 * math.log(ROPE_BASE) / rope))
        angles = pos_ids.astype(F32)[:, None] * inv_freq
        cos_p, sin_p = jnp.cos(angles), jnp.sin(angles)
        pad = jnp.zeros((n, 128 - rope), F32)
        cos_t = jnp.concatenate([cos_p, cos_p, pad], axis=1).reshape(CHUNKS, rows, 128)
        sin_t = jnp.concatenate([-sin_p, sin_p, pad], axis=1).reshape(CHUNKS, rows, 128)
        kpe_t = jnp.swapaxes(kpe_cache, 2, 3)
        w_dkv_t = jnp.swapaxes(w_dkv, 1, 2)
        w_o2 = w_o.reshape(w_o.shape[0], -1, width)
        scale = w_uq.shape[-1] ** -0.5

        ckv_2d = ckv_cache.reshape(ckv_cache.shape[0], -1, lat)
        kpe_2d = kpe_t.reshape(kpe_t.shape[0], -1, kpe_t.shape[3])

        def heads_of(layer, c_q):
            q_full = jnp.einsum('bc,chd->bhd', c_q, w_uq[layer], preferred_element_type=F32)
            q_nope = q_full[..., :nope].astype(BF)
            q_rope = rotate(q_full[..., nope:], cos_p[:, None], sin_p[:, None]).astype(BF)
            q_lat = jnp.einsum('bhn,chn->bhc', q_nope, w_uk[layer], preferred_element_type=F32).astype(BF)
            q_rope = jnp.pad(q_rope, ((0, 0), (0, 0), (0, 128 - rope)))
            return w_uv[layer].reshape(lat, -1), q_lat.reshape(-1, lat), q_rope.reshape(-1, 128), ckv_2d, kpe_2d

        normed = rms_norm(x_in, attn_gain[0])
        c_q = rms_norm(jnp.dot(normed, w_dq[0], preferred_element_type=F32), q_gain[0])
        kv = jnp.dot(normed, w_dkv[0], preferred_element_type=F32)
        c_new0 = rms_norm(kv[:, :lat], kv_gain[0])
        k_new0 = rotate(kv[:, lat:], cos_p, sin_p).astype(BF)
        k_pad0 = jnp.pad(k_new0, ((0, 0), (0, 128 - rope)))
        x_own, c_q, c_new1, k_pad1 = fused_layer(
            0, False, scale, pos_ids, c_new0, k_pad0, *heads_of(0, c_q), x_in.reshape(CHUNKS, rows, width), mlp_gain[0:1], w_o2, w_gate, w_up, w_down,
            (attn_gain[1:2], q_gain[1:2], kv_gain[1:2], cos_t, sin_t, w_dq, w_dkv_t))
        c_new1 = c_new1.reshape(n, lat)
        k_pad1 = k_pad1.reshape(n, 128)
        k_new1 = k_pad1[:, :rope]
        x_out = fused_layer(1, True, scale, pos_ids, c_new1, k_pad1, *heads_of(1, c_q.reshape(n, -1)), x_own, mlp_gain[1:2], w_o2, w_gate, w_up, w_down, None)
        return x_out.reshape(n, width), jnp.stack([c_new0, c_new1]), jnp.stack([k_new0, k_new1])

    return jax.shard_map(device_body, mesh=mesh, in_specs=in_specs, out_specs=out_specs, check_vma=False)
```

time: 576 us -> 507 us (0.88)
  Pallas kernels: 456 us -> 396 us
    pallas_call x4 -> x2, Pallas kernels: 456 us -> 396 us  [fused_layer(): pl.pallas_call(functools.partial(layer_body, layer, last, scale), in_spec...]
    dot_general x2 -> x0, local copies, waits for them, and re-layouts: 8.82 us -> none  [heads_of(): jnp.einsum('bhn,chn->bhc', q_nope, w_uk[layer], preferred_element_type=F32)]
    convert_element_type x2, local copies, waits for them, and re-layouts: 1.37 us -> 8.74 us  [heads_of(): jnp.einsum('bhn,chn->bhc', q_nope, w_uk[layer], preferred_element_type=F32)]
    unnamed x52 -> x44, local copies, waits for them, and re-layouts: 17.9 us -> 13 us
where the time goes in v2:
time: 507 us; the launch traced here: 497 us
  Pallas kernels  396 us (78%)
  matrix products  44.8 us (9%)
  local copies, waits for them, and re-layouts  36.5 us (7%)
  other arithmetic  18.3 us (4%)
    pallas_call x2, Pallas kernels, fused_layer(): pl.pallas_call(functools.partial(layer_body, layer, last, scale), in_spec...  396 us
    dot_general x1, matrix products, device_body(): jnp.dot(normed, w_dq[0], preferred_element_type=F32)  19.4 us
    unnamed x44, local copies, waits for them, and re-layouts  13 us
    unnamed x2, matrix products  11.8 us

profile of v2, /device:TPU:1, one launch (start us, length us, event | category | flops | bytes accessed | tf_op | source)
XLA Modules:
  0.0 497.4 jit_solution(17957952852799148388)
XLA Ops:
  0.6 1.6 fusion.21
  2.2 4.6 fusion.3
  6.8 19.4 %multiply_reduce_fusion = (f32[512]{0:T(512)S(1)}, f32[512,1536]{1,0:T(8,128)}) fusion(bf16[2,7168,1536]{2,1,0:T(8,128)(2,1)} %refs_19_.1, bf16[512,7168]{1,0:T(8,128)(2,1)} %param.17, f32[7168]{0:T(1024)S(1)} %bitcast.98, f32[512]{0:T(512)S(1)} %add_rsqrt_fusion.2), kind=kOutput, calls=%fused_computation.16 | convolution fusion | flops 11290542080 | bytes 32538624 | tf_op jit(solution)/shard_map/dot_general | solution.py:556
  26.2 0.0 slice-start
  26.2 6.7 %fusion.18 = (bf16[1,1536,8,192]{1,3,2,0:T(8,128)(2,1)}, bf16[1,1536,8,192]{1,3,2,0:T(8,128)(2,1)S(1)}) fusion(bf16[2,1536,8,192]{1,3,2,0:T(8,128)(2,1)} %param.26), kind=kLoop, calls=%fused_computation.60 | loop fusion | bytes 18874368 | tf_op jit(solution)/shard_map/slice | solution.py:548
  32.9 0.0 copy-done.12
  32.9 0.0 slice-start.1
  32.9 6.5 %fusion.11 = f32[512,1536]{0,1} fusion(bf16[1536,1536]{0,1:T(8,128)(2,1)S(1)} %bitcast.83, f32[512,1536]{1,0:T(8,128)} %get-tuple-element.45, f32[1536]{0:T(1024)S(1)} %convert_reduce_fusion, f32[512]{0:T(512)S(1)} %add_rsqrt_fusion), kind=kOutput, calls=%fused_computation.19 | convolution fusion | flops 2418278400 | bytes 11018240
  39.5 0.0 slice-done
  39.5 0.0 slice-done.1
  39.5 9.4 %fusion.6 = f32[512,576]{1,0:T(8,128)S(1)} fusion(bf16[2,7168,576]{1,2,0:T(8,128)(2,1)} %param.24, bf16[512,7168]{1,0:T(8,128)(2,1)S(1)} %bitcast.77, f32[7168]{0:T(1024)S(1)} %bitcast.99, f32[512]{0:T(512)S(1)} %add_rsqrt_fusion.2), kind=kOutput, calls=%fused_computation.8 | convolution fusion | flops 4242538496 | bytes 16807936 | tf_op jit(solution)/shard_map/dot_general | solution.py:557
  48.9 0.0 copy-done.13
  48.9 0.0 copy-start
  49.0 0.0 copy-start.16
  49.0 1.4 subtract_convert_fusion.2
  50.4 0.0 copy-start.6
  50.4 0.0 copy-start.7
  50.4 0.1 copy.41
  50.5 0.1 copy.42
  50.6 1.4 subtract_convert_fusion.1
  52.0 0.0 copy-done.8
  52.0 0.0 copy-done.10
  52.1 0.8 copy.55
  52.9 0.0 copy-start.3
  52.9 1.2 pad_bitcast_fusion.1.refs_5_
  54.1 0.8 fusion.16.refs_2_
  54.9 0.1 multiply_reduce_fusion.1
  55.0 0.0 copy-done.16
  55.1 0.0 copy-start.14
  55.1 0.5 fusion.23
  55.6 0.0 copy-done
  55.6 1.0 multiply_convert_fusion.2.refs_1_
  56.6 0.0 copy-done.6
  56.6 0.0 copy-done.7
  56.6 2.7 fusion.19
  59.2 0.0 copy-done.3
  59.3 1.3 convert_bitcast_fusion.1
  60.6 0.0 copy-start.5
  60.6 4.3 copy.68
  64.9 1.0 fusion.17
  65.9 0.1 pad.26.clone
  66.0 1.0 maximum_maximum_fusion.1
  67.1 1.1 fusion.20
  68.2 1.3 copy.70
  69.4 0.6 slice.105.refs_15_
  70.0 198.3 %layer_mid.1 = (bf16[4,16,7168]{2,1,0:T(8,128)(2,1)}, bf16[4,128,1536]{2,1,0:T(8,128)(2,1)}, bf16[4,128,512]{2,1,0:T(8,128)(2,1)}, bf16[4,128,128]{2,1,0:T(8,128)(2,1)}) custom-call(s32[512]{0:T(512)} %refs_0_.3, bf16[512,512]{1,0:T(8,128)(2,1)} %multiply_convert_fusion.2.refs_1_, bf16[512,128]{1,0:T(8,128)(2,1)} %fusion.16.refs_2_, ...), custom_call_target="tpu_custom_call" | custom-call | flops 35030827008 | bytes 198443008 | tf_op jit(solution)/shard_map/layer_mid/pallas_call | solution.py:511
  268.4 5.3 %fusion.24 = f32[512,1536]{0,1:S(1)} fusion(bf16[512,1536]{1,0:T(8,128)(2,1)} %bitcast.102, bf16[1536,1536]{0,1:T(8,128)(2,1)} %bitcast.82), kind=kOutput, calls=%fused_computation.66 | convolution fusion | flops 2415919104 | bytes 9437184
  273.7 0.0 copy-start.4
  273.7 0.2 subtract_convert_fusion
  273.9 1.5 copy-done.4
  275.4 0.8 copy.56
  276.2 1.2 pad_bitcast_fusion.refs_5_
  277.4 2.9 convert_bitcast_fusion
  280.3 0.0 copy-start.2
  280.3 4.4 copy.67
  284.7 0.0 copy-done.2
  284.7 1.2 copy.69
  286.0 198.1 %layer_last.1 = bf16[4,128,7168]{2,1,0:T(8,128)(2,1)} custom-call(s32[512]{0:T(512)} %refs_0_.3, bf16[512,512]{1,0:T(8,128)(2,1)} %bitcast.92, bf16[512,128]{1,0:T(8,128)(2,1)} %bitcast.96, bf16[512,1024]{1,0:T(8,128)(2,1)} %bitcast.85, bf16[4096,512]{1,0:T(8,128)(2,1)} %bitcast.80, bf16[4096,128]{1,0:T(8,128)(2,1)} %pad_bitcast_fusion.refs_5_, ...), custom_call_target="tpu_custom_call" | custom-call | flops 35030827008 | bytes 198443008 | tf_op jit(solution)/shard_map/layer_last/pallas_call | solution.py:511
  484.1 0.9 slice_bitcast_fusion
  485.0 1.1 pad_maximum_fusion.3
  486.1 0.8 copy.48
  486.9 1.4 fusion.28
  488.3 2.1 pad_maximum_fusion
  490.4 6.6 %copy.72 = bf16[512,7168]{1,0:T(8,128)(2,1)} copy(bf16[512,7168]{1,0:T(8,128)(2,1)} %bitcast.78) | data formatting | bytes 14680064
  (24 shorter events, 0.2 us)
Async XLA Ops:
  26.2 6.7 %copy-start.12 = (bf16[2,1536]{1,0:T(2,128)(2,1)S(1)}, bf16[2,1536]{1,0:T(2,128)(2,1)}, u32[]{:S(2)}) copy-start(bf16[2,1536]{1,0:T(2,128)(2,1)} %param.23) | copy-start | bytes 18436
  26.2 13.3 %slice-start = ((s8[7340032]{0:T(1024)(128)(4,1)}), s8[3145728]{0:T(1024)(128)(4,1)S(1)}, s32[]{:S(2)}) async-start(s8[7340032]{0:T(1024)(128)(4,1)} %bitcast.76), calls=%async_computation | async-start | bytes 6291456
  32.9 6.6 %slice-start.1 = ((s8[7340032]{0:T(1024)(128)(4,1)}), s8[4194304]{0:T(1024)(128)(4,1)S(1)}, s32[]{:S(2)}) async-start(s8[7340032]{0:T(1024)(128)(4,1)} %bitcast.76), calls=%async_computation.1 | async-start | bytes 8388608
  39.5 9.4 %copy-start.13 = (s32[512]{0:T(512)S(1)}, s32[512]{0:T(512)}, u32[]{:S(2)}) copy-start(s32[512]{0:T(512)} %refs_0_.3) | copy-start | bytes 6148
  48.9 6.7 %copy-start = (f32[512,576]{1,0:T(8,128)}, f32[512,576]{1,0:T(8,128)S(1)}, u32[]{:S(2)}) copy-start(f32[512,576]{1,0:T(8,128)S(1)} %fusion.6) | copy-start | bytes 3538948
  49.0 6.1 %copy-start.16 = (bf16[2,512]{1,0:T(2,128)(2,1)S(1)}, bf16[2,512]{1,0:T(2,128)(2,1)}, u32[]{:S(2)}) copy-start(bf16[2,512]{1,0:T(2,128)(2,1)} %param.25) | copy-start | bytes 6148
  50.4 6.2 %copy-start.6 = (bf16[512,32]{1,0:T(8,128)(2,1)}, bf16[512,32]{1,0:T(8,128)(2,1)S(1)}, u32[]{:S(2)}) copy-start(bf16[512,32]{1,0:T(8,128)(2,1)S(1)} %get-tuple-element.27) | copy-start | bytes 98308
  50.4 6.2 %copy-start.7 = (bf16[512,32]{1,0:T(8,128)(2,1)}, bf16[512,32]{1,0:T(8,128)(2,1)S(1)}, u32[]{:S(2)}) copy-start(bf16[512,32]{1,0:T(8,128)(2,1)S(1)} %get-tuple-element.28) | copy-start | bytes 98308
  50.5 1.5 copy-start.8
  50.6 1.4 copy-start.10
  52.9 6.4 %copy-start.3 = (f32[512,1536]{0,1:S(1)}, f32[512,1536]{0,1}, u32[]{:S(2)}) copy-start(f32[512,1536]{0,1} %fusion.11) | copy-start | bytes 9437188
  55.1 5.5 %copy-start.14 = (f32[512]{0:T(512)}, f32[512]{0:T(512)S(1)}, u32[]{:S(2)}) copy-start(f32[512]{0:T(512)S(1)} %add_rsqrt_fusion.1) | copy-start | bytes 6148
  55.6 5.0 copy-start.15
  60.6 6.5 %copy-start.5 = (bf16[2,512,8,128]{3,2,1,0:T(8,128)(2,1)S(1)}, bf16[2,512,8,128]{3,2,1,0:T(8,128)(2,1)}, u32[]{:S(2)}) copy-start(bf16[2,512,8,128]{3,2,1,0:T(8,128)(2,1)} %param.28) | copy-start | bytes 6291460
  268.4 5.3 %copy-start.9 = (f32[512,32]{0,1:T(8,128)S(1)}, f32[512,32]{0,1:T(8,128)}, u32[]{:S(2)}) copy-start(f32[512,32]{0,1:T(8,128)} %copy-done.8) | copy-start | bytes 196612
  268.4 5.3 %copy-start.11 = (f32[512,32]{0,1:T(8,128)S(1)}, f32[512,32]{0,1:T(8,128)}, u32[]{:S(2)}) copy-start(f32[512,32]{0,1:T(8,128)} %copy-done.10) | copy-start | bytes 196612
  273.7 1.7 copy-start.4
  273.7 3.7 copy-start.1
  280.3 4.4 copy-start.2

commit v3 on v2

--- a/solution.py
+++ b/solution.py
@@ -15,28 +15,29 @@
 MESH = pl.DeviceIdType.MESH
 
 SUB = 8
-STEP = 32
+LANES = 128
+STEP = 16
 SUBS = 5
-SLOTS = 12
+SLOTS = 9
 CHUNKS = 4
 WIDE = 1024
 
 ORDER_LAST = (
-    'T', 'T', 'T', 'T', 'O00', 'T', 'A000', 'T', 'T', 'A100', 'T', 'O01', 'A200', 'T',
-    'A001', 'T', 'B000', 'T', 'A101', 'T', 'O02', 'B100', 'A201', 'T', 'B200', 'A002', 'T', 'B001',
-    'T', 'A102', 'T', 'O03', 'B101', 'A202', 'M', 'M', 'B201', 'A003', 'M', 'B002', 'M', 'M',
-    'M', 'A103', 'M', 'A010', 'M', 'M', 'B102', 'A203', 'M', 'B202', 'M', 'A110', 'A011', 'B003',
-    'M', 'M', 'M', 'A210', 'M', 'A111', 'A012', 'B010', 'B103', 'A211', 'B203', 'M', 'M', 'A112',
-    'M', 'B011', 'M', 'M', 'B110', 'A212', 'A013', 'B111', 'B210', 'B012', 'B211', 'A113', 'B112', 'A213',
-    'B212', 'B013', 'B113', 'B213',
+    'T', 'T', 'T', 'T', 'E00', 'T', 'T', 'O00', 'T', 'T', 'A000', 'E01', 'T', 'T',
+    'O01', 'T', 'A100', 'T', 'A001', 'E02', 'T', 'A200', 'O02', 'T', 'A101', 'T', 'B000', 'A002',
+    'T', 'E03', 'A201', 'O03', 'B100', 'B001', 'A003', 'B200', 'M', 'A102', 'M', 'M', 'B101', 'M',
+    'A202', 'M', 'B201', 'M', 'A103', 'M', 'B002', 'A010', 'M', 'M', 'A203', 'M', 'B102', 'A011',
+    'B003', 'B202', 'M', 'A110', 'M', 'M', 'M', 'A210', 'A111', 'M', 'B103', 'A012', 'B010', 'B203',
+    'M', 'A211', 'M', 'M', 'A112', 'M', 'B011', 'M', 'B110', 'A212', 'A013', 'B210', 'B111', 'B012',
+    'B211', 'A113', 'B112', 'A213', 'B212', 'B013', 'B113', 'B213',
 )
 ORDER_MID = (
-    'T', 'T', 'T', 'T', 'O00', 'T', 'A000', 'T', 'T', 'A100', 'T', 'O01', 'A200', 'T',
-    'A001', 'T', 'B000', 'T', 'A101', 'T', 'O02', 'B100', 'A201', 'T', 'B200', 'A002', 'T', 'B001',
-    'T', 'A102', 'T', 'O03', 'B101', 'A202', 'M', 'M', 'B201', 'A003', 'M', 'B002', 'M', 'M',
-    'M', 'A103', 'M', 'A010', 'M', 'M', 'B102', 'A203', 'M', 'B202', 'M', 'A110', 'A011', 'B003',
-    'M', 'M', 'M', 'A210', 'M', 'A111', 'A012', 'B103', 'A211', 'B203', 'M', 'M', 'A112', 'M',
-    'M', 'M', 'A212', 'A013', 'A113', 'A213',
+    'T', 'T', 'T', 'T', 'E00', 'T', 'O00', 'T', 'T', 'A000', 'T', 'E01', 'T', 'O01',
+    'T', 'A100', 'T', 'A001', 'T', 'E02', 'T', 'A200', 'O02', 'T', 'A101', 'T', 'B000', 'A002',
+    'T', 'E03', 'A201', 'O03', 'B100', 'A003', 'B001', 'B200', 'M', 'M', 'A102', 'M', 'M', 'M',
+    'A103', 'A202', 'A010', 'B101', 'A203', 'B201', 'M', 'M', 'B002', 'A110', 'M', 'M', 'B003', 'M',
+    'A210', 'B102', 'A011', 'B202', 'M', 'M', 'B103', 'M', 'M', 'B203', 'M', 'A111', 'M', 'M',
+    'A012', 'M', 'A211', 'M', 'M', 'A112', 'A013', 'A212', 'A113', 'A213',
 )
 
 
@@ -54,22 +55,30 @@
 
 
 def layer_body(layer, last, scale, *refs):
-    (pos_ref, cn_ref, kn_ref, uv_ref, q_hbm, qr_hbm, ckv_hbm, kpe_hbm, x_hbm, gain_ref, wo_hbm, wg_hbm, wu_hbm, wd_hbm), refs = refs[:14], refs[14:]
+    (pos_ref, cn_ref, kn_ref, uva_hbm, uvb_hbm, qa_hbm, qb_hbm, ra_hbm, rb_hbm, ckv_hbm, kpe_hbm, x_hbm, gain_ref, wo_hbm, wg_hbm, wu_hbm, wd_hbm), refs = refs[:17], refs[17:]
     if last:
         out_hbm, refs = refs[0], refs[1:]
     else:
         (next_gain_ref, q_gain_ref, kv_gain_ref, cos_hbm, sin_hbm, wdq_hbm, wdkv_hbm, own_out, cq_out, ckv_out, kpe_out), refs = refs[:11], refs[11:]
-    (wgu, wod, buf, r0, r1, r2, own, act, sc, ctx, posv, wsem, gsem, xsem, osem, ss, rs, ack, credit, csem, ksem, qsem, rsem), refs = refs[:23], refs[23:]
+    (wgu, wod, buf, r0, r1, r2, own, act, sc, ctx, posv, rope_t, fresh_v, wsem, gsem, xsem, osem, ss, rs, ack, credit, csem, ksem, qsem, uvsem, es, er), refs = refs[:27], refs[27:]
     if not last:
         cos_v, sin_v = refs
-    heads = 8
+    heads = 16
+    own_heads = 8
     keys = sc.shape[1]
-    n_lat = q_hbm.shape[1]
+    n_lat = qa_hbm.shape[2]
     n_rope = kpe_hbm.shape[1] // (ckv_hbm.shape[1] // keys)
-    steps = q_hbm.shape[0] // (STEP * heads)
+    steps = qa_hbm.shape[0]
+    per = steps // CHUNKS
     total = steps * (STEP // SUB)
+    blk = STEP * own_heads
     q_base = 3 * SUB * keys
     k_col = 4 * n_lat
+    v_col = 3 * n_lat
+    c_row = 4 * n_lat
+    c_rows = STEP * per
+    send_row = c_row + heads * c_rows
+    ho_row = send_row + 2 * CHUNKS * c_rows
     depth = wo_hbm.shape[1]
     cols = wd_hbm.shape[1]
     width = wd_hbm.shape[2]
@@ -101,9 +110,11 @@
     def cache_copies(t):
         slot = lax.rem(t, SLOTS)
         row, col = slot_at(slot)
-        return (pltpu.make_async_copy(ckv_hbm.at[layer, pl.ds(pl.multiple_of(t * (SUB * keys), SUB * keys), SUB * keys)],
+        sub = STEP // SUB
+        first = t // (per * sub) * rows + c * half + lax.rem(t, per * sub) * SUB
+        return (pltpu.make_async_copy(ckv_hbm.at[layer, pl.ds(pl.multiple_of(first * keys, SUB * keys), SUB * keys)],
                                       wgu.at[pl.ds(row, SUB * keys), pl.ds(col, n_lat)], csem.at[slot]),
-                pltpu.make_async_copy(kpe_hbm.at[layer, pl.ds(pl.multiple_of(t * (SUB * n_rope), SUB * n_rope), SUB * n_rope)],
+                pltpu.make_async_copy(kpe_hbm.at[layer, pl.ds(pl.multiple_of(first * n_rope, SUB * n_rope), SUB * n_rope)],
                                       wgu.at[pl.ds(pl.multiple_of(slot * (SUB * n_rope), SUB * n_rope), SUB * n_rope), pl.ds(k_col, keys)], ksem.at[slot]))
 
     def q_at(k):
@@ -111,12 +122,16 @@
 
     def q_copies(k):
         row, col = q_at(k)
-        n = STEP * heads
-        out = [pltpu.make_async_copy(q_hbm.at[pl.ds(pl.multiple_of(k * n, n), n)], wgu.at[pl.ds(row, n), pl.ds(col, n_lat)], qsem.at[k])]
-        for i in range(2):
-            out.append(pltpu.make_async_copy(qr_hbm.at[pl.ds(pl.multiple_of(k * n + i * 128, 128), 128)],
-                                             wod.at[pl.ds(depth, 128), pl.ds(pl.multiple_of((2 * k + i) * 128, 128), 128)], rsem.at[2 * k + i]))
+        out = []
+        for i, (lat_hbm, rope_hbm) in enumerate(((qa_hbm, ra_hbm), (qb_hbm, rb_hbm))):
+            out.append(pltpu.make_async_copy(lat_hbm.at[k], wgu.at[pl.ds(row + i * blk, blk), pl.ds(col, n_lat)], qsem.at[k, 2 * i]))
+            out.append(pltpu.make_async_copy(rope_hbm.at[k], wod.at[pl.ds(depth, LANES), pl.ds(pl.multiple_of((2 * k + i) * LANES, LANES), LANES)], qsem.at[k, 2 * i + 1]))
         return out
+
+    uv_cp = []
+    for i, uv_hbm in enumerate((uva_hbm, uvb_hbm)):
+        for b in range(2):
+            uv_cp.append(pltpu.make_async_copy(uv_hbm.at[layer, :, pl.ds(b * n_lat, n_lat)], wgu.at[pl.ds((2 * i + b) * n_lat, n_lat), pl.ds(v_col, n_lat)], uvsem.at[2 * i + b]))
 
     def start_all(cps):
         for cp in cps:
@@ -129,10 +144,15 @@
     start_all(q_copies(0))
     for t in range(STEP // SUB):
         start_all(cache_copies(t))
-    for k in range(1, steps):
-        start_all(q_copies(k))
+    start_all(q_copies(1))
     for t in range(STEP // SUB, SLOTS):
         start_all(cache_copies(t))
+
+    def more_q(k, _):
+        start_all(q_copies(k))
+        return 0
+    lax.fori_loop(2, steps, more_q, 0)
+    start_all(uv_cp)
 
     wo_cp = [pltpu.make_async_copy(wo_hbm.at[layer, :, pl.ds(j * WIDE, WIDE)], wod.at[pl.ds(0, depth), pl.ds(j * WIDE, WIDE)], wsem.at[j]) for j in range(tiles)]
     for cp in wo_cp:
@@ -146,9 +166,9 @@
     for cp in x_cp:
         cp.start()
     gu_cp = []
-    for j in range(cols // 128):
-        gu_cp.append(pltpu.make_async_copy(wg_hbm.at[layer, :, pl.ds(j * 128, 128)], wgu.at[:, pl.ds(2 * j * 128, 128)], gsem.at[2 * j]))
-        gu_cp.append(pltpu.make_async_copy(wu_hbm.at[layer, :, pl.ds(j * 128, 128)], wgu.at[:, pl.ds((2 * j + 1) * 128, 128)], gsem.at[2 * j + 1]))
+    for j in range(cols // LANES):
+        gu_cp.append(pltpu.make_async_copy(wg_hbm.at[layer, :, pl.ds(j * LANES, LANES)], wgu.at[:, pl.ds(2 * j * LANES, LANES)], gsem.at[2 * j]))
+        gu_cp.append(pltpu.make_async_copy(wu_hbm.at[layer, :, pl.ds(j * LANES, LANES)], wgu.at[:, pl.ds((2 * j + 1) * LANES, LANES)], gsem.at[2 * j + 1]))
     wd_cp = [pltpu.make_async_copy(wd_hbm.at[layer, :, pl.ds(j * WIDE, WIDE)], wod.at[:, pl.ds(j * WIDE, WIDE)], wsem.at[j]) for j in range(tiles)]
     if not last:
         dq = wdq_hbm.shape[2]
@@ -198,7 +218,32 @@
     def out_copy(r):
         return pltpu.make_async_copy(buf.at[r], out_hbm.at[r], osem.at[r])
 
+    def pair_copy(r, q):
+        src = wgu.at[pl.ds(send_row + (2 * r + q) * c_rows, c_rows), pl.ds(v_col, n_lat)]
+        dst = wgu.at[pl.ds(al(ho_row + (2 * r + q) * rows + c * c_rows), c_rows), pl.ds(v_col, n_lat)]
+        return pltpu.make_async_remote_copy(src_ref=src, dst_ref=dst, send_sem=es.at[q, r], recv_sem=er.at[q, r],
+                                            device_id={'tp': pair}, device_id_type=MESH)
+
+    def step_e(r):
+        if r == 0:
+            wait_all(uv_cp)
+        for own_side in (False, True):
+            for h in range(own_heads):
+                g = h if own_side else h + own_heads
+                val = jnp.dot(wgu[c_row + g * c_rows:c_row + (g + 1) * c_rows, v_col:v_col + n_lat],
+                              wgu[g // 4 * n_lat:(g // 4 + 1) * n_lat, v_col + g % 4 * LANES:v_col + (g % 4 + 1) * LANES], preferred_element_type=F32).astype(BF)
+                cs = slice(v_col + h % 4 * LANES, v_col + (h % 4 + 1) * LANES)
+                if own_side:
+                    wgu[pl.ds(al(ho_row + (2 * r + h // 4) * rows + c * c_rows), c_rows), cs] = val
+                else:
+                    wgu[send_row + (2 * r + h // 4) * c_rows:send_row + (2 * r + h // 4 + 1) * c_rows, cs] = val
+        for q in range(2):
+            pair_copy(r, q).start()
+
     def step_o(r):
+        for q in range(2):
+            pair_copy(r, q).wait_recv()
+            pair_copy(r, q).wait_send()
         if r == 0:
             for cp in x_cp:
                 cp.wait()
@@ -207,7 +252,8 @@
             if r == 0:
                 pltpu.make_async_copy(wo_hbm.at[layer, :, pl.ds(0, WIDE)], wod.at[pl.ds(0, depth), pl.ds(0, WIDE)], wsem.at[t]).wait()
             cs = pl.ds(pl.multiple_of(t * WIDE, WIDE), WIDE)
-            buf[r, :, cs] = jnp.dot(act[:, 0:depth], wod[0:depth, cs], preferred_element_type=F32).astype(BF)
+            acc = sum(jnp.dot(wgu[ho_row + (2 * r + q) * rows:ho_row + (2 * r + q + 1) * rows, v_col:v_col + n_lat], wod[q * n_lat:(q + 1) * n_lat, cs], preferred_element_type=F32) for q in range(2))
+            buf[r, :, cs] = acc.astype(BF)
             return 0
         lax.fori_loop(0, tiles, tile, 0)
         send('S0', 0, r)
@@ -215,16 +261,16 @@
     def step_m(m):
         r = m // SUBS
         part = lax.rem(m, SUBS)
-        n_gate = cols // 128 // 3
+        n_gate = cols // LANES // 3
 
         def gate(j, _):
             @pl.when(r == 0)
             def _():
                 for i in range(2):
-                    pltpu.make_async_copy(wg_hbm.at[layer, :, pl.ds(0, 128)], wgu.at[:, pl.ds(0, 128)], gsem.at[2 * j + i]).wait()
+                    pltpu.make_async_copy(wg_hbm.at[layer, :, pl.ds(0, LANES)], wgu.at[:, pl.ds(0, LANES)], gsem.at[2 * j + i]).wait()
             cs = pl.ds(pl.multiple_of(j * 256, 256), 256)
             pre = jnp.dot(buf[r], wgu[:, cs], preferred_element_type=F32)
-            act[:, pl.ds(pl.multiple_of(j * 128, 128), 128)] = (jax.nn.silu(pre[:, :128]) * pre[:, 128:]).astype(BF)
+            act[:, pl.ds(pl.multiple_of(j * LANES, LANES), LANES)] = (jax.nn.silu(pre[:, :LANES]) * pre[:, LANES:]).astype(BF)
             return 0
 
         def tile(t, _):
@@ -281,9 +327,13 @@
         nsub = STEP // SUB
         wait_all(q_copies(k))
         q_row, q_col = q_at(k)
-        qr_cols = [pl.ds(pl.multiple_of((2 * k + i) * 128, 128), 128) for i in range(2)]
-        for i in range(STEP):
-            posv[i * heads:(i + 1) * heads, :] = jnp.full((heads, 128), pos_ref[k * STEP + i], jnp.int32)
+        blocks = [(slice(b * LANES, (b + 1) * LANES), pl.ds(pl.multiple_of(q_col + b * LANES, LANES), LANES)) for b in range(n_lat // LANES)]
+        for b, (_, cs) in enumerate(blocks):
+            ctx[b] = wgu[pl.ds(q_row, rows_n), cs].astype(F32)
+        for i in range(2):
+            rope_t[i * blk:(i + 1) * blk, :] = wod[depth:depth + LANES, pl.ds(pl.multiple_of((2 * k + i) * LANES, LANES), LANES)].astype(F32)
+        cn = cn_ref[pl.ds(pl.multiple_of(k * STEP, STEP), STEP), :].astype(F32)
+        kn = kn_ref[pl.ds(pl.multiple_of(k * STEP, STEP), STEP), :].astype(F32)
         slots = []
         for j in range(nsub):
             t = k * nsub + j
@@ -294,49 +344,47 @@
             k_row = pl.multiple_of(slot * (SUB * n_rope), SUB * n_rope)
             for e in range(SUB):
                 i = j * SUB + e
-                lo = i // 2 * 16
-                up = i % 2 * heads
-                keys_i = wgu[pl.ds(row + e * keys, keys), pl.ds(col, n_lat)]
-                s_i = lax.dot_general(wgu[pl.ds(q_row + lo, 16), pl.ds(q_col, n_lat)], keys_i, NT, preferred_element_type=F32)
-                s_i = s_i + jnp.dot(wod[depth + lo % 128:depth + lo % 128 + 16, qr_cols[lo // 128]][:, :n_rope], wgu[pl.ds(k_row + e * n_rope, n_rope), pl.ds(k_col, keys)], preferred_element_type=F32)
-                sc[i * heads:(i + 1) * heads, :] = s_i[up:up + heads]
-        seqs = pl.ds(pl.multiple_of(k * STEP, STEP), STEP)
+                q = jnp.concatenate([ctx[b, pl.ds(i, heads, stride=STEP), :] for b in range(n_lat // LANES)], axis=1)
+                qr = rope_t[pl.ds(i, heads, stride=STEP), :]
+                s_i = lax.dot_general(q.astype(BF), wgu[pl.ds(row + e * keys, keys), pl.ds(col, n_lat)], NT, preferred_element_type=F32)
+                s_i = s_i + jnp.dot(qr[:, :n_rope].astype(BF), wgu[pl.ds(k_row + e * n_rope, n_rope), pl.ds(k_col, keys)], preferred_element_type=F32)
+                sc[i * heads:(i + 1) * heads, :] = s_i
+                part = qr * kn[i:i + 1]
+                for b, (lo, _) in enumerate(blocks):
+                    part = part + q[:, lo] * cn[i:i + 1, lo]
+                fresh_v[i * heads:(i + 1) * heads, :] = part
+                posv[i * heads:(i + 1) * heads, :] = jnp.full((heads, LANES), pos_ref[k * STEP + i], jnp.int32)
         col_id = lax.broadcasted_iota(jnp.int32, (rows_n, keys), 1)
         pv = posv[:, 0:1]
-        cn = cn_ref[seqs, :].astype(F32)
-        kn = kn_ref[seqs, :].astype(F32)
-        fresh = jnp.sum(wgu[pl.ds(q_row, rows_n), pl.ds(q_col, n_lat)].astype(F32) * jnp.broadcast_to(cn[:, None, :], (STEP, heads, n_lat)).reshape(rows_n, n_lat), axis=-1, keepdims=True)
-        kn8 = jnp.broadcast_to(kn[:, None, :], (STEP, heads, 128)).reshape(rows_n, 128)
-        fresh = fresh + jnp.sum(jnp.concatenate([wod[depth:depth + 128, cs].astype(F32) for cs in qr_cols], axis=0) * kn8, axis=-1, keepdims=True)
+        fresh = jnp.sum(fresh_v[...], axis=-1, keepdims=True)
         hit = col_id == pv
         sco = jnp.where(hit, fresh, sc[...]) * scale
         sco = jnp.where(col_id <= pv, sco, -jnp.inf)
         e_x = jnp.exp(sco - jnp.max(sco, axis=-1, keepdims=True))
         w = (e_x / jnp.sum(e_x, axis=-1, keepdims=True)).astype(BF).astype(F32)
-        new_prob = jnp.sum(jnp.where(hit, w, 0.0), axis=-1, keepdims=True)
-        new_part = (new_prob.reshape(STEP, heads, 1) * cn[:, None, :]).reshape(rows_n, n_lat)
-        for b in range(n_lat // 128):
-            ctx[b] = new_part[:, b * 128:(b + 1) * 128]
+        fresh_v[...] = jnp.broadcast_to(jnp.sum(jnp.where(hit, w, 0.0), axis=-1, keepdims=True), fresh_v.shape)
         sc[...] = jnp.where(hit, 0.0, w)
         for j in range(nsub):
             row, col = slots[j]
             for e in range(SUB):
-                rw = slice((j * SUB + e) * heads, (j * SUB + e + 1) * heads)
+                i = j * SUB + e
+                rw = slice(i * heads, (i + 1) * heads)
                 val = jnp.dot(sc[rw, :].astype(BF), wgu[pl.ds(row + e * keys, keys), pl.ds(col, n_lat)], preferred_element_type=F32)
-                for b in range(n_lat // 128):
-                    ctx[b, rw, :] = (ctx[b, rw, :] + val[:, b * 128:(b + 1) * 128]).astype(BF).astype(F32)
+                for b, (lo, _) in enumerate(blocks):
+                    ctx[b, rw, :] = val[:, lo] + fresh_v[rw, :] * cn[i:i + 1, lo]
             nxt = k * nsub + j + SLOTS
 
             @pl.when(nxt < total)
             def _():
                 start_all(cache_copies(nxt))
-        out_rows = pl.ds(pl.multiple_of(lax.rem(k, steps // CHUNKS) * STEP, STEP), STEP)
         for h in range(heads):
-            ctx_h = jnp.concatenate([ctx[b, pl.ds(h, STEP, stride=heads), :] for b in range(n_lat // 128)], axis=1).astype(BF)
-            act[out_rows, h * 128:(h + 1) * 128] = jnp.dot(ctx_h, uv_ref[:, h * 128:(h + 1) * 128], preferred_element_type=F32).astype(BF)
+            ctx_h = jnp.concatenate([ctx[b, pl.ds(h, STEP, stride=heads), :] for b in range(n_lat // LANES)], axis=1)
+            wgu[pl.ds(al(c_row + h * c_rows + lax.rem(k, per) * STEP), STEP), v_col:v_col + n_lat] = ctx_h.astype(BF)
 
     def event(op, ph, r):
-        if op == 'O':
+        if op == 'E':
+            step_e(r)
+        elif op == 'O':
             step_o(r)
         elif op == 'A0':
             landed('S0', ph, r, pair)
@@ -397,10 +445,10 @@
                         start_all(dq_cp)
                     for ev in evs:
                         if ev[0] == 'O' and ev[2] == CHUNKS - 1:
-                            start_all(gu_cp)
+                            start_all(gu_cp[:v_col // LANES] + gu_cp[k_col // LANES:])
                         event(*ev)
                         if ev[0] == 'O' and ev[2] == CHUNKS - 1:
-                            start_all(wd_cp)
+                            start_all(gu_cp[v_col // LANES:k_col // LANES] + wd_cp)
         return 0
     lax.fori_loop(0, steps, lambda k, _: run('T', step_t, k), 0)
     lax.fori_loop(0, SUBS * CHUNKS, lambda k, _: run('M', step_m, k), 0)
@@ -424,12 +472,12 @@
     kv = lax.dot_general(a(), wod[0:lat, :], NT, preferred_element_type=F32)
     inv = lax.rsqrt(jnp.mean(kv * kv, axis=-1, keepdims=True) + NORM_EPS)
     buf[:, mine, dq:dq + lat] = (kv * inv * kv_gain_ref[...].astype(F32)).astype(BF).reshape(CHUNKS, eighth, lat)
-    kp = lax.dot_general(a(), wod[lat:lat + 128, :], NT, preferred_element_type=F32)
+    kp = lax.dot_general(a(), wod[lat:lat + LANES, :], NT, preferred_element_type=F32)
     rope = dkv - lat
-    lane = lax.broadcasted_iota(jnp.int32, (n, 128), 1)
-    swap = jnp.where(lane < rope // 2, pltpu.roll(kp, 128 - rope // 2, 1), pltpu.roll(kp, rope // 2, 1))
-    kp = jnp.where(lane < rope, kp * cos_v[...].reshape(n, 128) + swap * sin_v[...].reshape(n, 128), 0.0)
-    buf[:, mine, dq + lat:dq + lat + 128] = kp.astype(BF).reshape(CHUNKS, eighth, 128)
+    lane = lax.broadcasted_iota(jnp.int32, (n, LANES), 1)
+    swap = jnp.where(lane < rope // 2, pltpu.roll(kp, LANES - rope // 2, 1), pltpu.roll(kp, rope // 2, 1))
+    kp = jnp.where(lane < rope, kp * cos_v[...].reshape(n, LANES) + swap * sin_v[...].reshape(n, LANES), 0.0)
+    buf[:, mine, dq + lat:dq + lat + LANES] = kp.astype(BF).reshape(CHUNKS, eighth, LANES)
     for cp in dq_cp:
         cp.wait()
     total_sq = jnp.zeros((n, 1), F32)
@@ -437,17 +485,18 @@
         v = jnp.dot(a(), wgu[:, j * 512:(j + 1) * 512], preferred_element_type=F32)
         total_sq = total_sq + jnp.sum(v * v, axis=-1, keepdims=True)
         for b in range(4):
-            ctx[b, j * n:(j + 1) * n, :] = v[:, b * 128:(b + 1) * 128]
+            ctx[b, j * n:(j + 1) * n, :] = v[:, b * LANES:(b + 1) * LANES]
     inv = lax.rsqrt(total_sq * (1.0 / dq) + NORM_EPS)
-    for j in range(dq // 128):
-        cs = slice(j * 128, (j + 1) * 128)
+    for j in range(dq // LANES):
+        cs = slice(j * LANES, (j + 1) * LANES)
         v = ctx[j % 4, j // 4 * n:(j // 4 + 1) * n, :]
-        buf[:, mine, cs] = (v * inv * q_gain_ref[:, cs].astype(F32)).astype(BF).reshape(CHUNKS, eighth, 128)
-
-    used = dq + lat + 128
-
-    def gather(k, off, rows_n, dev):
-        part = buf.at[:, pl.ds(al(off), rows_n), pl.ds(0, used)]
+        buf[:, mine, cs] = (v * inv * q_gain_ref[:, cs].astype(F32)).astype(BF).reshape(CHUNKS, eighth, LANES)
+
+    used = dq + lat + LANES
+    first = dq // LANES * LANES
+
+    def gather(k, off, rows_n, dev, lo=0):
+        part = buf.at[:, pl.ds(al(off), rows_n), pl.ds(lo, used - lo)]
         cp = pltpu.make_async_remote_copy(src_ref=part, dst_ref=part, send_sem=ss.at[k, 0], recv_sem=rs.at[k, 0],
                                           device_id={'tp': dev}, device_id_type=MESH)
         cp.start()
@@ -463,13 +512,13 @@
     g1.wait_recv()
     for r in range(CHUNKS):
         granted('S0', 1, r)
-    g2 = gather(11, half_own, half, pair)
+    g2 = gather(11, half_own, half, pair, first)
+    outs = [pltpu.make_async_copy(buf.at[:, pl.ds(al(half_own), half), pl.ds(0, dq)], cq_out, osem.at[1]),
+            pltpu.make_async_copy(buf.at[:, :, pl.ds(dq, lat)], ckv_out, osem.at[2]),
+            pltpu.make_async_copy(buf.at[:, :, pl.ds(dq + lat, LANES)], kpe_out, osem.at[3])]
+    outs[0].start()
     g2.wait_recv()
-    outs = [pltpu.make_async_copy(buf.at[:, :, pl.ds(0, dq)], cq_out, osem.at[1]),
-            pltpu.make_async_copy(buf.at[:, :, pl.ds(dq, lat)], ckv_out, osem.at[2]),
-            pltpu.make_async_copy(buf.at[:, :, pl.ds(dq + lat, 128)], kpe_out, osem.at[3])]
-    for cp in outs:
-        cp.start()
+    start_all(outs[1:])
     for cp in (g0, g1, g2):
         cp.wait_send()
     own_cp.wait()
@@ -477,20 +526,56 @@
         cp.wait()
 
 
-def fused_layer(layer, last, scale, pos, c_new, k_new, w_uv, q_lat, q_rope, ckv, kpe_t, resid, mlp_gain, w_o, w_gate, w_up, w_down, more):
-    n, width = c_new.shape[0], w_down.shape[2]
+def q_body(cq_ref, w_ref, uk_ref, cos_ref, sin_ref, lat_ref, rope_ref):
+    group, qk = w_ref.shape[0], w_ref.shape[1]
+    nope = uk_ref.shape[1] // group
+    steps = lat_ref.shape[0]
+    half = (qk - nope) // 2
+    for g in range(group):
+        w = jnp.concatenate([w_ref[g], w_ref[g, nope + half:, :], w_ref[g, nope:nope + half, :]], axis=0)
+        q = lax.dot_general(cq_ref[...], w, NT, preferred_element_type=F32)
+        rp, swap = q[:, nope:qk], q[:, qk:]
+        rope = (rp * cos_ref[:, :2 * half] + swap * sin_ref[:, :2 * half]).astype(BF)
+        lat = lax.dot_general(q[:, :nope].astype(BF), uk_ref[:, g * nope:(g + 1) * nope], NT, preferred_element_type=F32).astype(BF)
+        lat_ref[:, g] = lat.reshape(steps, STEP, lat.shape[1])
+        rope_ref[:, g, :, :2 * half] = rope.reshape(steps, STEP, 2 * half)
+        rope_ref[:, g, :, 2 * half:] = jnp.zeros((steps, STEP, rope_ref.shape[3] - 2 * half), BF)
+
+
+def q_heads(layer, c_q, w_uq_t, w_uk, cos_t, sin_t, group=2):
+    n, rank = c_q.shape
+    heads, qk = w_uq_t.shape[1], w_uq_t.shape[2]
+    lat = w_uk.shape[1]
+    nope = w_uk.shape[2] // heads
+    steps = n // STEP
+    q_lat, q_rope = pl.pallas_call(
+        q_body, grid=(heads // group,),
+        in_specs=[pl.BlockSpec((n, rank), lambda h: (0, 0)), pl.BlockSpec((None, group, qk, rank), lambda h: (layer, h, 0, 0)),
+                  pl.BlockSpec((None, lat, group * nope), lambda h: (layer, 0, h)),
+                  pl.BlockSpec((n, LANES), lambda h: (0, 0)), pl.BlockSpec((n, LANES), lambda h: (0, 0))],
+        out_specs=[pl.BlockSpec((steps, group, STEP, lat), lambda h: (0, h, 0, 0)), pl.BlockSpec((steps, group, STEP, LANES), lambda h: (0, h, 0, 0))],
+        out_shape=[jax.ShapeDtypeStruct((steps, heads, STEP, lat), BF), jax.ShapeDtypeStruct((steps, heads, STEP, LANES), BF)],
+        name='q_heads', compiler_params=pltpu.CompilerParams(dimension_semantics=('arbitrary',)),
+        cost_estimate=pl.CostEstimate(flops=2 * n * heads * (rank * qk + nope * lat), bytes_accessed=2 * rank * qk * heads, transcendentals=0),
+    )(c_q, w_uq_t, w_uk, cos_t, sin_t)
+    return q_lat.reshape(steps, heads * STEP, lat), q_rope.reshape(steps, heads * STEP, LANES)
+
+
+def fused_layer(layer, last, scale, pos, c_new, k_new, w_uv, q_parts, ckv, kpe_t, resid, mlp_gain, w_o, w_gate, w_up, w_down, more):
+    n, width = 2 * c_new.shape[0], w_down.shape[2]
     lat = c_new.shape[1]
     keys = kpe_t.shape[2]
     rows = n // CHUNKS
     depth, cols = w_o.shape[1], w_down.shape[1]
     vm = pl.BlockSpec(memory_space=pltpu.VMEM)
     hb = pl.BlockSpec(memory_space=pl.ANY)
-    args = [pos, c_new, k_new, w_uv, q_lat, q_rope, ckv, kpe_t, resid, mlp_gain, w_o, w_gate, w_up, w_down]
-    specs = [pl.BlockSpec(memory_space=pltpu.SMEM), vm, vm, vm, hb, hb, hb, hb, hb, vm, hb, hb, hb, hb]
+    args = [pos, c_new, k_new, *w_uv, *q_parts, ckv, kpe_t, resid, mlp_gain, w_o, w_gate, w_up, w_down]
+    specs = [pl.BlockSpec(memory_space=pltpu.SMEM), vm, vm] + [hb] * 9 + [vm, hb, hb, hb, hb]
     scratch = [pltpu.VMEM((width, 2 * cols), BF), pltpu.VMEM((cols, width), BF), pltpu.VMEM((CHUNKS, rows, width), BF),
                pltpu.VMEM((2, rows // 2, width), BF), pltpu.VMEM((CHUNKS, rows // 4, width), BF),
                pltpu.VMEM((CHUNKS, rows // 8, width), BF), pltpu.VMEM((CHUNKS, rows // 8, width), BF),
-               pltpu.VMEM((rows, cols), BF), pltpu.VMEM((STEP * 8, keys), F32), pltpu.VMEM((lat // 128, STEP * 8, 128), F32), pltpu.VMEM((STEP * 8, 128), jnp.int32)]
+               pltpu.VMEM((rows, cols), BF), pltpu.VMEM((STEP * 16, keys), F32), pltpu.VMEM((lat // LANES, STEP * 16, LANES), F32),
+               pltpu.VMEM((STEP * 16, LANES), jnp.int32), pltpu.VMEM((STEP * 16, LANES), F32), pltpu.VMEM((STEP * 16, LANES), F32)]
     if last:
         outs = jax.ShapeDtypeStruct((CHUNKS, rows, width), BF)
         out_specs = hb
@@ -498,16 +583,16 @@
         next_gain, q_gain, kv_gain, cos_t, sin_t, w_dq, w_dkv_t = more
         args += [next_gain, q_gain, kv_gain, cos_t, sin_t, w_dq, w_dkv_t]
         specs += [vm, vm, vm, hb, hb, hb, hb]
-        outs = (jax.ShapeDtypeStruct((CHUNKS, rows // 8, width), BF), jax.ShapeDtypeStruct((CHUNKS, rows, w_dq.shape[2]), BF),
-                jax.ShapeDtypeStruct((CHUNKS, rows, kv_gain.shape[1]), BF), jax.ShapeDtypeStruct((CHUNKS, rows, 128), BF))
+        outs = (jax.ShapeDtypeStruct((CHUNKS, rows // 8, width), BF), jax.ShapeDtypeStruct((CHUNKS, rows // 2, w_dq.shape[2]), BF),
+                jax.ShapeDtypeStruct((CHUNKS, rows, kv_gain.shape[1]), BF), jax.ShapeDtypeStruct((CHUNKS, rows, LANES), BF))
         out_specs = (hb,) * 4
-    scratch += [pltpu.SemaphoreType.DMA((width // WIDE,)), pltpu.SemaphoreType.DMA((2 * cols // 128,)),
+    scratch += [pltpu.SemaphoreType.DMA((width // WIDE,)), pltpu.SemaphoreType.DMA((2 * cols // LANES,)),
                 pltpu.SemaphoreType.DMA((3,)), pltpu.SemaphoreType.DMA((4,)),
                 pltpu.SemaphoreType.DMA((12, CHUNKS)), pltpu.SemaphoreType.DMA((12, CHUNKS)),
                 pltpu.SemaphoreType.REGULAR((6, CHUNKS)), pltpu.SemaphoreType.REGULAR, pltpu.SemaphoreType.DMA((SLOTS,)), pltpu.SemaphoreType.DMA((SLOTS,)),
-                pltpu.SemaphoreType.DMA((n // STEP,)), pltpu.SemaphoreType.DMA((2 * n // STEP,))]
+                pltpu.SemaphoreType.DMA((n // 2 // STEP, 4)), pltpu.SemaphoreType.DMA((4,)), pltpu.SemaphoreType.DMA((2, CHUNKS)), pltpu.SemaphoreType.DMA((2, CHUNKS))]
     if not last:
-        scratch += [pltpu.VMEM((CHUNKS, rows // 8, 128), F32)] * 2
+        scratch += [pltpu.VMEM((CHUNKS, rows // 8, LANES), F32)] * 2
     return pl.pallas_call(
         functools.partial(layer_body, layer, last, scale), in_specs=specs, out_specs=out_specs, out_shape=outs, scratch_shapes=scratch,
         name='layer_last' if last else 'layer_mid',
@@ -533,9 +618,9 @@
         inv_freq = jnp.exp(jnp.arange(half, dtype=F32) * (-2.0 * math.log(ROPE_BASE) / rope))
         angles = pos_ids.astype(F32)[:, None] * inv_freq
         cos_p, sin_p = jnp.cos(angles), jnp.sin(angles)
-        pad = jnp.zeros((n, 128 - rope), F32)
-        cos_t = jnp.concatenate([cos_p, cos_p, pad], axis=1).reshape(CHUNKS, rows, 128)
-        sin_t = jnp.concatenate([-sin_p, sin_p, pad], axis=1).reshape(CHUNKS, rows, 128)
+        pad = jnp.zeros((n, LANES - rope), F32)
+        cos_t = jnp.concatenate([cos_p, cos_p, pad], axis=1).reshape(CHUNKS, rows, LANES)
+        sin_t = jnp.concatenate([-sin_p, sin_p, pad], axis=1).reshape(CHUNKS, rows, LANES)
         kpe_t = jnp.swapaxes(kpe_cache, 2, 3)
         w_dkv_t = jnp.swapaxes(w_dkv, 1, 2)
         w_o2 = w_o.reshape(w_o.shape[0], -1, width)
@@ -543,28 +628,46 @@
 
         ckv_2d = ckv_cache.reshape(ckv_cache.shape[0], -1, lat)
         kpe_2d = kpe_t.reshape(kpe_t.shape[0], -1, kpe_t.shape[3])
-
-        def heads_of(layer, c_q):
-            q_full = jnp.einsum('bc,chd->bhd', c_q, w_uq[layer], preferred_element_type=F32)
-            q_nope = q_full[..., :nope].astype(BF)
-            q_rope = rotate(q_full[..., nope:], cos_p[:, None], sin_p[:, None]).astype(BF)
-            q_lat = jnp.einsum('bhn,chn->bhc', q_nope, w_uk[layer], preferred_element_type=F32).astype(BF)
-            q_rope = jnp.pad(q_rope, ((0, 0), (0, 0), (0, 128 - rope)))
-            return w_uv[layer].reshape(lat, -1), q_lat.reshape(-1, lat), q_rope.reshape(-1, 128), ckv_2d, kpe_2d
-
-        normed = rms_norm(x_in, attn_gain[0])
+        core = lax.rem(lax.axis_index('tp'), 2)
+        swap = [(i, i + 1 - 2 * (i % 2)) for i in range(mesh.shape['tp'])]
+
+        def mine(v):
+            v = v.reshape((CHUNKS, 2, rows // 2) + v.shape[1:])
+            v = lax.dynamic_index_in_dim(v, core, 1, keepdims=False)
+            return v.reshape((n // 2,) + v.shape[2:])
+
+        def whole(v):
+            other = lax.ppermute(v, 'tp', swap)
+            lo = jnp.where(core == 0, v, other).reshape((CHUNKS, 1, rows // 2) + v.shape[1:])
+            hi = jnp.where(core == 0, other, v).reshape((CHUNKS, 1, rows // 2) + v.shape[1:])
+            return jnp.concatenate([lo, hi], axis=1).reshape((n,) + v.shape[1:])
+
+        uq = [jnp.transpose(w_uq, (0, 2, 3, 1))]
+        uk = [w_uk.reshape(w_uk.shape[0], lat, -1)]
+        uv = [w_uv.reshape(w_uv.shape[0], lat, -1)]
+        for w in (uq, uk, uv):
+            w.append(lax.ppermute(w[0], 'tp', swap))
+        pos_own = mine(pos_ids)
+        cos_own, sin_own = mine(cos_t.reshape(n, LANES)), mine(sin_t.reshape(n, LANES))
+
+        def q_parts(layer, c_q):
+            (lat_a, rope_a), (lat_b, rope_b) = [q_heads(layer, c_q, uq[i], uk[i], cos_own, sin_own) for i in range(2)]
+            return lat_a, lat_b, rope_a, rope_b
+
+        normed = rms_norm(mine(x_in), attn_gain[0])
         c_q = rms_norm(jnp.dot(normed, w_dq[0], preferred_element_type=F32), q_gain[0])
         kv = jnp.dot(normed, w_dkv[0], preferred_element_type=F32)
         c_new0 = rms_norm(kv[:, :lat], kv_gain[0])
-        k_new0 = rotate(kv[:, lat:], cos_p, sin_p).astype(BF)
-        k_pad0 = jnp.pad(k_new0, ((0, 0), (0, 128 - rope)))
+        k_new0 = rotate(kv[:, lat:], cos_own[:, :half], sin_own[:, half:rope]).astype(BF)
+        k_pad0 = jnp.pad(k_new0, ((0, 0), (0, LANES - rope)))
         x_own, c_q, c_new1, k_pad1 = fused_layer(
-            0, False, scale, pos_ids, c_new0, k_pad0, *heads_of(0, c_q), x_in.reshape(CHUNKS, rows, width), mlp_gain[0:1], w_o2, w_gate, w_up, w_down,
+            0, False, scale, pos_own, c_new0, k_pad0, uv, q_parts(0, c_q), ckv_2d, kpe_2d, x_in.reshape(CHUNKS, rows, width), mlp_gain[0:1], w_o2, w_gate, w_up, w_down,
             (attn_gain[1:2], q_gain[1:2], kv_gain[1:2], cos_t, sin_t, w_dq, w_dkv_t))
         c_new1 = c_new1.reshape(n, lat)
-        k_pad1 = k_pad1.reshape(n, 128)
+        k_pad1 = k_pad1.reshape(n, LANES)
         k_new1 = k_pad1[:, :rope]
-        x_out = fused_layer(1, True, scale, pos_ids, c_new1, k_pad1, *heads_of(1, c_q.reshape(n, -1)), x_own, mlp_gain[1:2], w_o2, w_gate, w_up, w_down, None)
+        c_new0, k_new0 = whole(c_new0), whole(k_new0)
+        x_out = fused_layer(1, True, scale, pos_own, mine(c_new1), mine(k_pad1), uv, q_parts(1, c_q.reshape(n // 2, -1)), ckv_2d, kpe_2d, x_own, mlp_gain[1:2], w_o2, w_gate, w_up, w_down, None)
         return x_out.reshape(n, width), jnp.stack([c_new0, c_new1]), jnp.stack([k_new0, k_new1])
 
     return jax.shard_map(device_body, mesh=mesh, in_specs=in_specs, out_specs=out_specs, check_vma=False)

time: 507 us -> 429 us (0.85); the launches traced: 497 us -> 428 us
  matrix products: 44.8 us -> 15.8 us
  Pallas kernels: 396 us -> 372 us
  local copies, waits for them, and re-layouts: 36.5 us -> 20.8 us
    pallas_call x2, Pallas kernels: 396 us -> 339 us  [fused_layer(): pl.pallas_call(functools.partial(layer_body, layer, last, scale), in_spec...]
    pallas_call x0 -> x4, Pallas kernels: none -> 33.1 us  [q_heads(): pl.pallas_call(q_body, grid=(heads // group,), in_specs=[pl.BlockSpec((n,...]
    unnamed x2 -> x0, matrix products: 11.8 us -> none
    slice x3 -> x0, local copies, waits for them, and re-layouts: 10.5 us -> none  [the longest x1 6.72 us: heads_of(): w_uq[layer]]
    dot_general x1, matrix products: 19.4 us -> 10.4 us  [device_body(): jnp.dot(normed, w_dq[0], preferred_element_type=F32)]
    convert_element_type x2 -> x0, local copies, waits for them, and re-layouts: 8.74 us -> none  [heads_of(): jnp.einsum('bhn,chn->bhc', q_nope, w_uk[layer], preferred_element_type=F32)]
    reshape x2 -> x4, local copies, waits for them, and re-layouts: 2.43 us -> 8.85 us  [the longest x1 4.58 us: device_body(): uk = [w_uk.reshape(w_uk.shape[0], lat, -1)]]
    unnamed x44 -> x30, local copies, waits for them, and re-layouts: 13 us -> 7.39 us
  transfers between devices with their start and end apart: 0 -> 5, of which waited for: 0 -> 0; matrix products, arithmetic and copies ran while one was open for 0% -> 9% of each run, Pallas kernels for 0% -> 4%
where the time goes in v3:
time: 429 us; the launch traced here: 428 us
  Pallas kernels  372 us (87%)
  local copies, waits for them, and re-layouts  20.8 us (5%)
  other arithmetic  16.9 us (4%)
  matrix products  15.8 us (4%)
    pallas_call x2, Pallas kernels, fused_layer(): pl.pallas_call(functools.partial(layer_body, layer, last, scale), in_spec...  339 us
    pallas_call x4, Pallas kernels, q_heads(): pl.pallas_call(q_body, grid=(heads // group,), in_specs=[pl.BlockSpec((n,...  33.1 us
    dot_general x1, matrix products, device_body(): jnp.dot(normed, w_dq[0], preferred_element_type=F32)  10.4 us
  transfers between devices with their start and end apart: 5, of which 0 were waited for; matrix products, arithmetic and copies ran while one was open for 9% of the time, Pallas kernels for 4%

profile of v3, /device:TPU:1, one launch (start us, length us, event | category | flops | bytes accessed | tf_op | source)
XLA Modules:
  0.0 427.7 jit_solution(16092534564140968281)
XLA Ops:
  0.6 0.0 copy-start.10
  0.7 2.8 reshape.251.refs_3_
  3.5 0.0 copy-start
  3.5 0.0 collective-permute-start
  3.6 4.6 %reshape.252.uk_ref = bf16[2,512,1024]{2,1,0:T(8,128)(2,1)} reshape(bf16[2,512,8,128]{3,2,1,0:T(8,128)(2,1)} %param.27) | data formatting | bytes 4194304 | tf_op jit(solution)/shard_map/reshape | solution.py:646
  8.1 0.1 collective-permute-start.2
  8.2 0.4 collective-permute-start.1
  8.7 2.9 fusion.6
  11.5 0.7 fusion.15
  12.2 0.1 mul.145
  12.3 0.1 pad.26.clone
  12.4 1.0 multiply_cosine_fusion.1
  13.4 0.1 fusion.12
  13.6 0.0 copy-start.1
  13.6 3.2 fusion.8
  16.8 0.0 copy-done
  16.8 0.0 copy-done.12
  16.8 0.0 copy-start.11
  16.8 5.4 %fusion.3 = f32[256,576]{1,0:T(8,128)S(1)} fusion(bf16[256,7168]{1,0:T(8,128)(2,1)S(1)} %bitcast.81, bf16[2,7168,576]{1,2,0:T(8,128)(2,1)} %param.24), kind=kOutput, calls=%fused_computation.5 | convolution fusion | flops 2113929216 | bytes 12517376 | tf_op jit(solution)/shard_map/dot_general | solution.py:659
  22.3 0.0 copy-done.1
  22.3 0.0 copy-done.2
  22.3 0.1 subtract_convert_fusion
  22.4 0.1 pad_maximum_fusion.4
  22.5 0.1 collective-permute-start.4
  22.7 0.1 multiply_reduce_fusion.1
  22.8 0.0 copy-done.11
  22.8 0.0 copy-start.9
  22.8 0.6 fusion.17
  23.4 0.0 copy-done.9
  23.4 0.1 multiply_convert_fusion.1.refs_1_
  23.5 0.0 copy-start.8
  23.5 0.0 copy-start.13
  23.6 0.4 collective-permute-start.3
  24.0 10.4 %multiply_reduce_fusion = (f32[256]{0:T(256)S(1)}, f32[256,1536]{1,0:T(8,128)S(1)}) fusion(bf16[256,7168]{1,0:T(8,128)(2,1)S(1)} %bitcast.82, bf16[2,7168,1536]{2,1,0:T(8,128)(2,1)} %refs_22_.1), kind=kOutput, calls=%fused_computation.12 | convolution fusion | flops 5637931008 | bytes 27264000 | tf_op jit(solution)/shard_map/dot_general | solution.py:658
  34.5 1.0 fusion.13
  35.5 1.0 maximum_maximum_fusion.1
  36.5 1.1 multiply_convert_fusion.cq_ref
  37.5 8.2 %q_heads.4 = (bf16[16,8,16,512]{3,2,1,0:T(8,128)(2,1)}, bf16[16,8,16,128]{3,2,1,0:T(8,128)(2,1)}) custom-call(bf16[256,1536]{1,0:T(8,128)(2,1)} %multiply_convert_fusion.cq_ref, bf16[2,8,192,1536]{3,2,1,0:T(8,128)(2,1)} %bitcast.64, bf16[2,512,1024]{2,1,0:T(8,128)(2,1)} %reshape.252.uk_ref, f32[256,128]{1,0:T(8,128)} %bitcast.72, f32[256,128]{1,0:T(8,128)} %bitcast.77), custom_call_target="tpu_custom_call" | custom-call | flops 1476395008 | bytes 4718592 | tf_op jit(solution)/shard_map/q_heads/pallas_call | solution.py:551
  45.8 0.8 reshape.246
  46.6 0.6 slice.63.refs_18_
  47.2 0.7 reshape.247.refs_0_
  47.9 0.7 pad.4.refs_2_
  48.5 0.0 collective-permute-done.4
  48.5 0.1 broadcast_select_fusion.3
  48.7 0.1 copy.35
  48.8 0.8 stack_reshape.11
  49.6 0.0 collective-permute-done.3
  49.6 0.8 broadcast_select_fusion.1
  50.4 0.1 pad_maximum_fusion.1
  50.4 0.8 copy.34
  51.3 0.0 collective-permute-done.2.uk_ref
  51.3 0.0 collective-permute-done.1.w_ref
  51.3 8.2 %q_heads.5 = (bf16[16,8,16,512]{3,2,1,0:T(8,128)(2,1)}, bf16[16,8,16,128]{3,2,1,0:T(8,128)(2,1)}) custom-call(bf16[256,1536]{1,0:T(8,128)(2,1)} %multiply_convert_fusion.cq_ref, bf16[2,8,192,1536]{3,2,1,0:T(8,128)(2,1)} %collective-permute-done.1.w_ref, bf16[2,512,1024]{2,1,0:T(8,128)(2,1)} %collective-permute-done.2.uk_ref, f32[256,128]{1,0:T(8,128)} %bitcast.73, ...), custom_call_target="tpu_custom_call" | custom-call | flops 1476395008 | bytes 4718592 | tf_op jit(solution)/shard_map/q_heads/pallas_call | solution.py:551
  59.5 0.0 collective-permute-done.refs_4_
  59.5 168.4 %layer_mid.1 = (bf16[4,16,7168]{2,1,0:T(8,128)(2,1)}, bf16[4,64,1536]{2,1,0:T(8,128)(2,1)}, bf16[4,128,512]{2,1,0:T(8,128)(2,1)}, bf16[4,128,128]{2,1,0:T(8,128)(2,1)}) custom-call(s32[256]{0:T(256)} %reshape.247.refs_0_, bf16[256,512]{1,0:T(8,128)(2,1)} %copy-done.4, bf16[256,128]{1,0:T(8,128)(2,1)} %pad.4.refs_2_, bf16[2,512,1024]{2,1,0:T(8,128)(2,1)} %copy-done, ...), custom_call_target="tpu_custom_call" | custom-call | flops 35030827008 | bytes 198443008 | tf_op jit(solution)/shard_map/layer_mid/pallas_call | solution.py:596
  227.9 8.4 %q_heads.6 = (bf16[16,8,16,512]{3,2,1,0:T(8,128)(2,1)}, bf16[16,8,16,128]{3,2,1,0:T(8,128)(2,1)}) custom-call(bf16[256,1536]{1,0:T(8,128)(2,1)} %bitcast.83, bf16[2,8,192,1536]{3,2,1,0:T(8,128)(2,1)} %bitcast.65, bf16[2,512,1024]{2,1,0:T(8,128)(2,1)} %reshape.252.uk_ref, f32[256,128]{1,0:T(8,128)} %bitcast.74, f32[256,128]{1,0:T(8,128)} %bitcast.79), custom_call_target="tpu_custom_call" | custom-call | flops 1476395008 | bytes 4718592 | tf_op jit(solution)/shard_map/q_heads/pallas_call | solution.py:551
  236.3 0.7 constant_dynamic-slice_fusion
  237.0 0.7 copy.40
  237.7 0.7 constant_dynamic-slice_fusion.1
  238.4 8.2 %q_heads.7 = (bf16[16,8,16,512]{3,2,1,0:T(8,128)(2,1)}, bf16[16,8,16,128]{3,2,1,0:T(8,128)(2,1)}) custom-call(bf16[256,1536]{1,0:T(8,128)(2,1)} %bitcast.84, bf16[2,8,192,1536]{3,2,1,0:T(8,128)(2,1)} %collective-permute-done.1.w_ref, bf16[2,512,1024]{2,1,0:T(8,128)(2,1)} %collective-permute-done.2.uk_ref, f32[256,128]{1,0:T(8,128)} %bitcast.75, ...), custom_call_target="tpu_custom_call" | custom-call | flops 1476395008 | bytes 4718592 | tf_op jit(solution)/shard_map/q_heads/pallas_call | solution.py:551
  246.6 170.6 %layer_last.1 = bf16[4,128,7168]{2,1,0:T(8,128)(2,1)} custom-call(s32[256]{0:T(256)} %reshape.247.refs_0_, bf16[256,512]{1,0:T(8,128)(2,1)} %bitcast.92, bf16[256,128]{1,0:T(8,128)(2,1)} %bitcast.101, bf16[2,512,1024]{2,1,0:T(8,128)(2,1)} %copy-done, bf16[2,512,1024]{2,1,0:T(8,128)(2,1)} %collective-permute-done.refs_4_, bf16[16,128,512]{2,1,0:T(8,128)(2,1)} %bitcast.86, ...), custom_call_target="tpu_custom_call" | custom-call | flops 35030827008 | bytes 198443008 | tf_op jit(solution)/shard_map/layer_last/pallas_call | solution.py:596
  417.3 1.5 pad_maximum_fusion.3
  418.8 2.3 pad_maximum_fusion
  421.1 6.6 %copy.42 = bf16[512,7168]{1,0:T(8,128)(2,1)} copy(bf16[512,7168]{1,0:T(8,128)(2,1)} %bitcast.69) | data formatting | bytes 14680064
  (25 shorter events, 0.1 us)
Async XLA Ops:
  0.6 8.0 %copy-start.10 = (s32[512]{0:T(512)S(1)}, s32[512]{0:T(512)}, u32[]{:S(2)}) copy-start(s32[512]{0:T(512)} %param.18) | copy-start | bytes 6148
  0.6 10.9 %copy-start.6 = (bf16[2,7168]{1,0:T(2,128)(2,1)S(1)}, bf16[2,7168]{1,0:T(2,128)(2,1)}, u32[]{:S(2)}) copy-start(bf16[2,7168]{1,0:T(2,128)(2,1)} %param.30) | copy-start | bytes 86020
  0.7 10.9 %copy-start.7 = (bf16[2,7168]{1,0:T(2,128)(2,1)S(1)}, bf16[2,7168]{1,0:T(2,128)(2,1)}, u32[]{:S(2)}) copy-start(bf16[2,7168]{1,0:T(2,128)(2,1)} %param.21) | copy-start | bytes 86020
  3.5 13.3 %copy-start = (bf16[2,512,1024]{2,1,0:T(8,128)(2,1)}, bf16[2,512,1024]{2,1,0:T(8,128)(2,1)S(1)}, u32[]{:S(2)}) copy-start(bf16[2,512,1024]{2,1,0:T(8,128)(2,1)S(1)} %reshape.251.refs_3_) | copy-start | bytes 6291460
  3.5 56.0 %collective-permute-start = (bf16[2,512,1024]{2,1,0:T(8,128)(2,1)S(1)}, bf16[2,512,1024]{2,1,0:T(8,128)(2,1)}, u32[]{:S(2)}, u32[]{:S(2)}) collective-permute-start(bf16[2,512,1024]{2,1,0:T(8,128)(2,1)S(1)} %reshape.251.refs_3_), channel_id=1, source_target_pairs={{0,1},{1,0},{2,3},{3,2},{4,5},{5,4},{6,7},{7,6}} | collective-permute-start | bytes 6291464 | tf_op jit(solution)/shard_map/ppermute | solution.py:649
  8.1 43.1 %collective-permute-start.2 = (bf16[2,512,1024]{2,1,0:T(8,128)(2,1)}, bf16[2,512,1024]{2,1,0:T(8,128)(2,1)}, u32[]{:S(2)}, u32[]{:S(2)}) collective-permute-start(bf16[2,512,1024]{2,1,0:T(8,128)(2,1)} %reshape.252.uk_ref), channel_id=1, source_target_pairs={{0,1},{1,0},{2,3},{3,2},{4,5},{5,4},{6,7},{7,6}} | collective-permute-start | bytes 6291464 | tf_op jit(solution)/shard_map/ppermute | solution.py:649
  8.2 43.0 %collective-permute-start.1 = (bf16[2,8,192,1536]{3,2,1,0:T(8,128)(2,1)}, bf16[2,8,192,1536]{3,2,1,0:T(8,128)(2,1)}, u32[]{:S(2)}, u32[]{:S(2)}) collective-permute-start(bf16[2,8,192,1536]{3,2,1,0:T(8,128)(2,1)} %bitcast.63), channel_id=1, source_target_pairs={{0,1},{1,0},{2,3},{3,2},{4,5},{5,4},{6,7},{7,6}} | collective-permute-start | bytes 28311560 | tf_op jit(solution)/shard_map/ppermute | solution.py:649
  12.2 4.6 %copy-start.12 = (f32[32]{0:T(128)}, f32[32]{0:T(128)S(1)}, u32[]{:S(2)}) copy-start(f32[32]{0:T(128)S(1)} %multiply_exponential_fusion) | copy-start | bytes 388
  13.6 8.7 %copy-start.1 = (f32[4,1,64,128]{3,2,0,1:T(8,128)}, f32[4,1,64,128]{3,2,0,1:T(8,128)S(1)}, u32[]{:S(2)}) copy-start(f32[4,1,64,128]{3,2,0,1:T(8,128)S(1)} %get-tuple-element.49) | copy-start | bytes 393220
  13.6 8.7 %copy-start.2 = (f32[4,1,64,128]{3,2,0,1:T(8,128)}, f32[4,1,64,128]{3,2,0,1:T(8,128)S(1)}, u32[]{:S(2)}) copy-start(f32[4,1,64,128]{3,2,0,1:T(8,128)S(1)} %get-tuple-element.50) | copy-start | bytes 393220
  16.8 6.0 %copy-start.11 = (bf16[2,512]{1,0:T(2,128)(2,1)S(1)}, bf16[2,512]{1,0:T(2,128)(2,1)}, u32[]{:S(2)}) copy-start(bf16[2,512]{1,0:T(2,128)(2,1)} %param.25) | copy-start | bytes 6148
  22.5 26.0 %collective-permute-start.4 = (bf16[256,64]{1,0:T(8,128)(2,1)S(1)}, bf16[256,64]{1,0:T(8,128)(2,1)S(1)}, u32[]{:S(2)}, u32[]{:S(2)}) collective-permute-start(bf16[256,64]{1,0:T(8,128)(2,1)S(1)} %pad_maximum_fusion.4), channel_id=1, source_target_pairs={{0,1},{1,0},{2,3},{3,2},{4,5},{5,4},{6,7},{7,6}} | collective-permute-start | bytes 98312 | tf_op jit(solution)/shard_map/ppermute | solution.py:640
  22.8 0.6 copy-start.9
  23.5 10.9 %copy-start.4 = (bf16[256,512]{1,0:T(8,128)(2,1)}, bf16[256,512]{1,0:T(8,128)(2,1)S(1)}, u32[]{:S(2)}) copy-start(bf16[256,512]{1,0:T(8,128)(2,1)S(1)} %multiply_convert_fusion.1.refs_1_) | copy-start | bytes 786436
  23.5 10.9 %copy-start.8 = (bf16[2,1536]{1,0:T(2,128)(2,1)S(1)}, bf16[2,1536]{1,0:T(2,128)(2,1)}, u32[]{:S(2)}) copy-start(bf16[2,1536]{1,0:T(2,128)(2,1)} %param.23) | copy-start | bytes 18436
  23.5 10.9 %copy-start.13 = (f32[32]{0:T(128)S(1)}, f32[32]{0:T(128)}, u32[]{:S(2)}) copy-start(f32[32]{0:T(128)} %copy-done.12) | copy-start | bytes 388
  23.6 26.0 %collective-permute-start.3 = (bf16[256,512]{1,0:T(8,128)(2,1)S(1)}, bf16[256,512]{1,0:T(8,128)(2,1)S(1)}, u32[]{:S(2)}, u32[]{:S(2)}) collective-permute-start(bf16[256,512]{1,0:T(8,128)(2,1)S(1)} %multiply_convert_fusion.1.refs_1_), channel_id=1, source_target_pairs={{0,1},{1,0},{2,3},{3,2},{4,5},{5,4},{6,7},{7,6}} | collective-permute-start | bytes 786440 | tf_op jit(solution)/shard_map/ppermute | solution.py:640
  227.9 8.4 %copy-start.5 = (bf16[4,128,128]{2,1,0:T(8,128)(2,1)S(1)}, bf16[4,128,128]{2,1,0:T(8,128)(2,1)}, u32[]{:S(2)}) copy-start(bf16[4,128,128]{2,1,0:T(8,128)(2,1)} %get-tuple-element.20) | copy-start | bytes 393220
  227.9 9.8 %copy-start.3 = (bf16[4,128,512]{2,1,0:T(8,128)(2,1)S(1)}, bf16[4,128,512]{2,1,0:T(8,128)(2,1)}, u32[]{:S(2)}) copy-start(bf16[4,128,512]{2,1,0:T(8,128)(2,1)} %get-tuple-element.19) | copy-start | bytes 1572868

commit v4 on v3

--- a/solution.py
+++ b/solution.py
@@ -526,36 +526,57 @@
         cp.wait()
 
 
-def q_body(cq_ref, w_ref, uk_ref, cos_ref, sin_ref, lat_ref, rope_ref):
-    group, qk = w_ref.shape[0], w_ref.shape[1]
-    nope = uk_ref.shape[1] // group
-    steps = lat_ref.shape[0]
+def q_body(layer, cq_ref, w_hbm, uk_ref, cos_ref, sin_ref, lat_hbm, rope_hbm, wv, latv, ropev, wsem, lsem, rsem):
+    heads, qk = wv.shape[:2]
+    nope = uk_ref.shape[1] // heads
+    steps = latv.shape[1]
     half = (qk - nope) // 2
-    for g in range(group):
-        w = jnp.concatenate([w_ref[g], w_ref[g, nope + half:, :], w_ref[g, nope:nope + half, :]], axis=0)
+
+    def load(h):
+        return pltpu.make_async_copy(w_hbm.at[layer, h], wv.at[h], wsem.at[h])
+
+    def stores(h):
+        return (pltpu.make_async_copy(latv.at[h], lat_hbm.at[:, h], lsem.at[h]), pltpu.make_async_copy(ropev.at[h], rope_hbm.at[:, h], rsem.at[h]))
+
+    for h in range(heads):
+        load(h).start()
+    ropev[...] = jnp.zeros_like(ropev)
+
+    def head(h, _):
+        load(h).wait()
+        w = jnp.concatenate([wv[h], wv[h, nope + half:, :], wv[h, nope:nope + half, :]], axis=0)
         q = lax.dot_general(cq_ref[...], w, NT, preferred_element_type=F32)
         rp, swap = q[:, nope:qk], q[:, qk:]
         rope = (rp * cos_ref[:, :2 * half] + swap * sin_ref[:, :2 * half]).astype(BF)
-        lat = lax.dot_general(q[:, :nope].astype(BF), uk_ref[:, g * nope:(g + 1) * nope], NT, preferred_element_type=F32).astype(BF)
-        lat_ref[:, g] = lat.reshape(steps, STEP, lat.shape[1])
-        rope_ref[:, g, :, :2 * half] = rope.reshape(steps, STEP, 2 * half)
-        rope_ref[:, g, :, 2 * half:] = jnp.zeros((steps, STEP, rope_ref.shape[3] - 2 * half), BF)
-
-
-def q_heads(layer, c_q, w_uq_t, w_uk, cos_t, sin_t, group=2):
+        uk = uk_ref[:, pl.ds(pl.multiple_of(h * nope, nope), nope)]
+        lat = lax.dot_general(q[:, :nope].astype(BF), uk, NT, preferred_element_type=F32).astype(BF)
+        latv[h] = lat.reshape(steps, STEP, lat.shape[1])
+        ropev[h, :, :, :2 * half] = rope.reshape(steps, STEP, 2 * half)
+        for cp in stores(h):
+            cp.start()
+        return 0
+    lax.fori_loop(0, heads, head, 0)
+    for h in range(heads):
+        for cp in stores(h):
+            cp.wait()
+
+
+def q_heads(layer, c_q, w_uq_t, w_uk, cos_t, sin_t):
     n, rank = c_q.shape
     heads, qk = w_uq_t.shape[1], w_uq_t.shape[2]
     lat = w_uk.shape[1]
     nope = w_uk.shape[2] // heads
     steps = n // STEP
+    hb = pl.BlockSpec(memory_space=pl.ANY)
     q_lat, q_rope = pl.pallas_call(
-        q_body, grid=(heads // group,),
-        in_specs=[pl.BlockSpec((n, rank), lambda h: (0, 0)), pl.BlockSpec((None, group, qk, rank), lambda h: (layer, h, 0, 0)),
-                  pl.BlockSpec((None, lat, group * nope), lambda h: (layer, 0, h)),
-                  pl.BlockSpec((n, LANES), lambda h: (0, 0)), pl.BlockSpec((n, LANES), lambda h: (0, 0))],
-        out_specs=[pl.BlockSpec((steps, group, STEP, lat), lambda h: (0, h, 0, 0)), pl.BlockSpec((steps, group, STEP, LANES), lambda h: (0, h, 0, 0))],
+        functools.partial(q_body, layer), grid=(1,),
+        in_specs=[pl.BlockSpec((n, rank), lambda i: (0, 0)), hb, pl.BlockSpec((None, lat, heads * nope), lambda i: (layer, 0, 0)),
+                  pl.BlockSpec((n, LANES), lambda i: (0, 0)), pl.BlockSpec((n, LANES), lambda i: (0, 0))],
+        out_specs=[hb, hb],
         out_shape=[jax.ShapeDtypeStruct((steps, heads, STEP, lat), BF), jax.ShapeDtypeStruct((steps, heads, STEP, LANES), BF)],
-        name='q_heads', compiler_params=pltpu.CompilerParams(dimension_semantics=('arbitrary',)),
+        scratch_shapes=[pltpu.VMEM((heads, qk, rank), BF), pltpu.VMEM((heads, steps, STEP, lat), BF), pltpu.VMEM((heads, steps, STEP, LANES), BF)]
+        + [pltpu.SemaphoreType.DMA((heads,))] * 3,
+        name='q_heads',
         cost_estimate=pl.CostEstimate(flops=2 * n * heads * (rank * qk + nope * lat), bytes_accessed=2 * rank * qk * heads, transcendentals=0),
     )(c_q, w_uq_t, w_uk, cos_t, sin_t)
     return q_lat.reshape(steps, heads * STEP, lat), q_rope.reshape(steps, heads * STEP, LANES)

time: 429 us -> 431 us (level)
  no operation moved by 1% of the time
where the time goes in v4:
time: 431 us; the launch traced here: 430 us
  Pallas kernels  375 us (87%)
  local copies, waits for them, and re-layouts  20.8 us (5%)
  other arithmetic  16.9 us (4%)
  matrix products  15.8 us (4%)
    pallas_call x2, Pallas kernels, fused_layer(): pl.pallas_call(functools.partial(layer_body, layer, last, scale), in_spec...  339 us
    pallas_call x4, Pallas kernels, q_heads(): pl.pallas_call(functools.partial(q_body, layer), grid=(1,), in_specs=[pl....  35.3 us
    dot_general x1, matrix products, device_body(): jnp.dot(normed, w_dq[0], preferred_element_type=F32)  10.4 us
  transfers between devices with their start and end apart: 5, of which 0 were waited for; matrix products, arithmetic and copies ran while one was open for 9% of the time, Pallas kernels for 4%

profile of v4, /device:TPU:1, one launch (start us, length us, event | category | flops | bytes accessed | tf_op | source)
XLA Modules:
  0.0 430.2 jit_solution(12605945485448442505)
XLA Ops:
  0.6 0.0 copy-start.10
  0.6 0.0 copy-start.6
  0.7 2.8 reshape.251.refs_3_
  3.5 0.0 copy-start
  3.5 0.0 collective-permute-start
  3.6 4.6 %reshape.252.uk_ref = bf16[2,512,1024]{2,1,0:T(8,128)(2,1)} reshape(bf16[2,512,8,128]{3,2,1,0:T(8,128)(2,1)} %param.27) | data formatting | bytes 4194304 | tf_op jit(solution)/shard_map/reshape | solution.py:667
  8.1 0.1 collective-permute-start.2
  8.2 0.4 collective-permute-start.1
  8.7 2.9 fusion.6
  11.5 0.7 fusion.15
  12.2 0.1 mul.145
  12.3 0.1 pad.26.clone
  12.4 1.0 multiply_cosine_fusion.1
  13.4 0.1 fusion.12
  13.6 0.0 copy-start.1
  13.6 3.2 fusion.8
  16.8 0.0 copy-done
  16.8 0.0 copy-done.12
  16.8 0.0 copy-start.11
  16.8 5.4 %fusion.3 = f32[256,576]{1,0:T(8,128)S(1)} fusion(bf16[256,7168]{1,0:T(8,128)(2,1)S(1)} %bitcast.81, bf16[2,7168,576]{1,2,0:T(8,128)(2,1)} %param.24), kind=kOutput, calls=%fused_computation.5 | convolution fusion | flops 2113929216 | bytes 12517376 | tf_op jit(solution)/shard_map/dot_general | solution.py:680
  22.3 0.0 copy-done.1
  22.3 0.0 copy-done.2
  22.3 0.1 subtract_convert_fusion
  22.4 0.1 pad_maximum_fusion.4
  22.5 0.1 collective-permute-start.4
  22.7 0.1 multiply_reduce_fusion.1
  22.8 0.0 copy-done.11
  22.8 0.0 copy-start.9
  22.8 0.6 fusion.17
  23.4 0.1 multiply_convert_fusion.1.refs_1_
  23.5 0.0 copy-start.8
  23.5 0.0 copy-start.13
  23.6 0.4 collective-permute-start.3
  24.0 10.4 %multiply_reduce_fusion = (f32[256]{0:T(256)S(1)}, f32[256,1536]{1,0:T(8,128)S(1)}) fusion(bf16[256,7168]{1,0:T(8,128)(2,1)S(1)} %bitcast.82, bf16[2,7168,1536]{2,1,0:T(8,128)(2,1)} %refs_22_.1), kind=kOutput, calls=%fused_computation.12 | convolution fusion | flops 5637931008 | bytes 27264000 | tf_op jit(solution)/shard_map/dot_general | solution.py:679
  34.5 1.0 fusion.13
  35.5 1.0 maximum_maximum_fusion.1
  36.5 1.1 multiply_convert_fusion.cq_ref
  37.5 8.8 %q_heads.4 = (bf16[16,8,16,512]{3,2,1,0:T(8,128)(2,1)}, bf16[16,8,16,128]{3,2,1,0:T(8,128)(2,1)}) custom-call(bf16[256,1536]{1,0:T(8,128)(2,1)} %multiply_convert_fusion.cq_ref, bf16[2,8,192,1536]{3,2,1,0:T(8,128)(2,1)} %bitcast.64, bf16[2,512,1024]{2,1,0:T(8,128)(2,1)} %reshape.252.uk_ref, f32[256,128]{1,0:T(8,128)} %bitcast.72, f32[256,128]{1,0:T(8,128)} %bitcast.77), custom_call_target="tpu_custom_call" | custom-call | flops 1476395008 | bytes 4718592 | tf_op jit(solution)/shard_map/q_heads/pallas_call | solution.py:571
  46.4 0.8 reshape.246
  47.1 0.6 slice.63.refs_18_
  47.8 0.7 reshape.247.refs_0_
  48.4 0.7 pad.4.refs_2_
  49.1 0.0 collective-permute-done.4
  49.1 0.1 broadcast_select_fusion.3
  49.2 0.1 copy.35
  49.4 0.8 stack_reshape.11
  50.2 0.0 collective-permute-done.3
  50.2 0.8 broadcast_select_fusion.1
  51.0 0.1 pad_maximum_fusion.1
  51.0 0.8 copy.34
  51.9 0.0 collective-permute-done.2.uk_ref
  51.9 0.0 collective-permute-done.1.w_hbm
  51.9 8.8 %q_heads.5 = (bf16[16,8,16,512]{3,2,1,0:T(8,128)(2,1)}, bf16[16,8,16,128]{3,2,1,0:T(8,128)(2,1)}) custom-call(bf16[256,1536]{1,0:T(8,128)(2,1)} %multiply_convert_fusion.cq_ref, bf16[2,8,192,1536]{3,2,1,0:T(8,128)(2,1)} %collective-permute-done.1.w_hbm, bf16[2,512,1024]{2,1,0:T(8,128)(2,1)} %collective-permute-done.2.uk_ref, f32[256,128]{1,0:T(8,128)} %bitcast.73, ...), custom_call_target="tpu_custom_call" | custom-call | flops 1476395008 | bytes 4718592 | tf_op jit(solution)/shard_map/q_heads/pallas_call | solution.py:571
  60.7 0.0 collective-permute-done.refs_4_
  60.7 168.6 %layer_mid.1 = (bf16[4,16,7168]{2,1,0:T(8,128)(2,1)}, bf16[4,64,1536]{2,1,0:T(8,128)(2,1)}, bf16[4,128,512]{2,1,0:T(8,128)(2,1)}, bf16[4,128,128]{2,1,0:T(8,128)(2,1)}) custom-call(s32[256]{0:T(256)} %reshape.247.refs_0_, bf16[256,512]{1,0:T(8,128)(2,1)} %copy-done.4, bf16[256,128]{1,0:T(8,128)(2,1)} %pad.4.refs_2_, bf16[2,512,1024]{2,1,0:T(8,128)(2,1)} %copy-done, ...), custom_call_target="tpu_custom_call" | custom-call | flops 35030827008 | bytes 198443008 | tf_op jit(solution)/shard_map/layer_mid/pallas_call | solution.py:617
  229.3 8.9 %q_heads.6 = (bf16[16,8,16,512]{3,2,1,0:T(8,128)(2,1)}, bf16[16,8,16,128]{3,2,1,0:T(8,128)(2,1)}) custom-call(bf16[256,1536]{1,0:T(8,128)(2,1)} %bitcast.83, bf16[2,8,192,1536]{3,2,1,0:T(8,128)(2,1)} %bitcast.65, bf16[2,512,1024]{2,1,0:T(8,128)(2,1)} %reshape.252.uk_ref, f32[256,128]{1,0:T(8,128)} %bitcast.74, f32[256,128]{1,0:T(8,128)} %bitcast.79), custom_call_target="tpu_custom_call" | custom-call | flops 1476395008 | bytes 4718592 | tf_op jit(solution)/shard_map/q_heads/pallas_call | solution.py:571
  238.2 0.7 constant_dynamic-slice_fusion
  238.8 0.7 copy.40
  239.5 0.7 constant_dynamic-slice_fusion.1
  240.3 8.8 %q_heads.7 = (bf16[16,8,16,512]{3,2,1,0:T(8,128)(2,1)}, bf16[16,8,16,128]{3,2,1,0:T(8,128)(2,1)}) custom-call(bf16[256,1536]{1,0:T(8,128)(2,1)} %bitcast.84, bf16[2,8,192,1536]{3,2,1,0:T(8,128)(2,1)} %collective-permute-done.1.w_hbm, bf16[2,512,1024]{2,1,0:T(8,128)(2,1)} %collective-permute-done.2.uk_ref, f32[256,128]{1,0:T(8,128)} %bitcast.75, ...), custom_call_target="tpu_custom_call" | custom-call | flops 1476395008 | bytes 4718592 | tf_op jit(solution)/shard_map/q_heads/pallas_call | solution.py:571
  249.1 170.7 %layer_last.1 = bf16[4,128,7168]{2,1,0:T(8,128)(2,1)} custom-call(s32[256]{0:T(256)} %reshape.247.refs_0_, bf16[256,512]{1,0:T(8,128)(2,1)} %bitcast.92, bf16[256,128]{1,0:T(8,128)(2,1)} %bitcast.101, bf16[2,512,1024]{2,1,0:T(8,128)(2,1)} %copy-done, bf16[2,512,1024]{2,1,0:T(8,128)(2,1)} %collective-permute-done.refs_4_, bf16[16,128,512]{2,1,0:T(8,128)(2,1)} %bitcast.86, ...), custom_call_target="tpu_custom_call" | custom-call | flops 35030827008 | bytes 198443008 | tf_op jit(solution)/shard_map/layer_last/pallas_call | solution.py:617
  419.8 1.5 pad_maximum_fusion.3
  421.3 2.3 pad_maximum_fusion
  423.6 6.6 %copy.42 = bf16[512,7168]{1,0:T(8,128)(2,1)} copy(bf16[512,7168]{1,0:T(8,128)(2,1)} %bitcast.69) | data formatting | bytes 14680064
  (25 shorter events, 0.1 us)
Async XLA Ops:
  0.6 8.0 %copy-start.10 = (s32[512]{0:T(512)S(1)}, s32[512]{0:T(512)}, u32[]{:S(2)}) copy-start(s32[512]{0:T(512)} %param.18) | copy-start | bytes 6148
  0.6 10.9 %copy-start.6 = (bf16[2,7168]{1,0:T(2,128)(2,1)S(1)}, bf16[2,7168]{1,0:T(2,128)(2,1)}, u32[]{:S(2)}) copy-start(bf16[2,7168]{1,0:T(2,128)(2,1)} %param.30) | copy-start | bytes 86020
  0.7 10.9 %copy-start.7 = (bf16[2,7168]{1,0:T(2,128)(2,1)S(1)}, bf16[2,7168]{1,0:T(2,128)(2,1)}, u32[]{:S(2)}) copy-start(bf16[2,7168]{1,0:T(2,128)(2,1)} %param.21) | copy-start | bytes 86020
  3.5 13.3 %copy-start = (bf16[2,512,1024]{2,1,0:T(8,128)(2,1)}, bf16[2,512,1024]{2,1,0:T(8,128)(2,1)S(1)}, u32[]{:S(2)}) copy-start(bf16[2,512,1024]{2,1,0:T(8,128)(2,1)S(1)} %reshape.251.refs_3_) | copy-start | bytes 6291460
  3.5 57.1 %collective-permute-start = (bf16[2,512,1024]{2,1,0:T(8,128)(2,1)S(1)}, bf16[2,512,1024]{2,1,0:T(8,128)(2,1)}, u32[]{:S(2)}, u32[]{:S(2)}) collective-permute-start(bf16[2,512,1024]{2,1,0:T(8,128)(2,1)S(1)} %reshape.251.refs_3_), channel_id=1, source_target_pairs={{0,1},{1,0},{2,3},{3,2},{4,5},{5,4},{6,7},{7,6}} | collective-permute-start | bytes 6291464 | tf_op jit(solution)/shard_map/ppermute | solution.py:670
  8.1 43.7 %collective-permute-start.2 = (bf16[2,512,1024]{2,1,0:T(8,128)(2,1)}, bf16[2,512,1024]{2,1,0:T(8,128)(2,1)}, u32[]{:S(2)}, u32[]{:S(2)}) collective-permute-start(bf16[2,512,1024]{2,1,0:T(8,128)(2,1)} %reshape.252.uk_ref), channel_id=1, source_target_pairs={{0,1},{1,0},{2,3},{3,2},{4,5},{5,4},{6,7},{7,6}} | collective-permute-start | bytes 6291464 | tf_op jit(solution)/shard_map/ppermute | solution.py:670
  8.2 43.6 %collective-permute-start.1 = (bf16[2,8,192,1536]{3,2,1,0:T(8,128)(2,1)}, bf16[2,8,192,1536]{3,2,1,0:T(8,128)(2,1)}, u32[]{:S(2)}, u32[]{:S(2)}) collective-permute-start(bf16[2,8,192,1536]{3,2,1,0:T(8,128)(2,1)} %bitcast.63), channel_id=1, source_target_pairs={{0,1},{1,0},{2,3},{3,2},{4,5},{5,4},{6,7},{7,6}} | collective-permute-start | bytes 28311560 | tf_op jit(solution)/shard_map/ppermute | solution.py:670
  12.2 4.6 %copy-start.12 = (f32[32]{0:T(128)}, f32[32]{0:T(128)S(1)}, u32[]{:S(2)}) copy-start(f32[32]{0:T(128)S(1)} %multiply_exponential_fusion) | copy-start | bytes 388
  13.6 8.7 %copy-start.1 = (f32[4,1,64,128]{3,2,0,1:T(8,128)}, f32[4,1,64,128]{3,2,0,1:T(8,128)S(1)}, u32[]{:S(2)}) copy-start(f32[4,1,64,128]{3,2,0,1:T(8,128)S(1)} %get-tuple-element.49) | copy-start | bytes 393220
  13.6 8.7 %copy-start.2 = (f32[4,1,64,128]{3,2,0,1:T(8,128)}, f32[4,1,64,128]{3,2,0,1:T(8,128)S(1)}, u32[]{:S(2)}) copy-start(f32[4,1,64,128]{3,2,0,1:T(8,128)S(1)} %get-tuple-element.50) | copy-start | bytes 393220
  16.8 6.0 %copy-start.11 = (bf16[2,512]{1,0:T(2,128)(2,1)S(1)}, bf16[2,512]{1,0:T(2,128)(2,1)}, u32[]{:S(2)}) copy-start(bf16[2,512]{1,0:T(2,128)(2,1)} %param.25) | copy-start | bytes 6148
  22.5 26.5 %collective-permute-start.4 = (bf16[256,64]{1,0:T(8,128)(2,1)S(1)}, bf16[256,64]{1,0:T(8,128)(2,1)S(1)}, u32[]{:S(2)}, u32[]{:S(2)}) collective-permute-start(bf16[256,64]{1,0:T(8,128)(2,1)S(1)} %pad_maximum_fusion.4), channel_id=1, source_target_pairs={{0,1},{1,0},{2,3},{3,2},{4,5},{5,4},{6,7},{7,6}} | collective-permute-start | bytes 98312 | tf_op jit(solution)/shard_map/ppermute | solution.py:661
  22.8 0.6 copy-start.9
  23.5 10.9 %copy-start.4 = (bf16[256,512]{1,0:T(8,128)(2,1)}, bf16[256,512]{1,0:T(8,128)(2,1)S(1)}, u32[]{:S(2)}) copy-start(bf16[256,512]{1,0:T(8,128)(2,1)S(1)} %multiply_convert_fusion.1.refs_1_) | copy-start | bytes 786436
  23.5 10.9 %copy-start.8 = (bf16[2,1536]{1,0:T(2,128)(2,1)S(1)}, bf16[2,1536]{1,0:T(2,128)(2,1)}, u32[]{:S(2)}) copy-start(bf16[2,1536]{1,0:T(2,128)(2,1)} %param.23) | copy-start | bytes 18436
  23.5 10.9 %copy-start.13 = (f32[32]{0:T(128)S(1)}, f32[32]{0:T(128)}, u32[]{:S(2)}) copy-start(f32[32]{0:T(128)} %copy-done.12) | copy-start | bytes 388
  23.6 26.6 %collective-permute-start.3 = (bf16[256,512]{1,0:T(8,128)(2,1)S(1)}, bf16[256,512]{1,0:T(8,128)(2,1)S(1)}, u32[]{:S(2)}, u32[]{:S(2)}) collective-permute-start(bf16[256,512]{1,0:T(8,128)(2,1)S(1)} %multiply_convert_fusion.1.refs_1_), channel_id=1, source_target_pairs={{0,1},{1,0},{2,3},{3,2},{4,5},{5,4},{6,7},{7,6}} | collective-permute-start | bytes 786440 | tf_op jit(solution)/shard_map/ppermute | solution.py:661
  229.2 8.9 %copy-start.5 = (bf16[4,128,128]{2,1,0:T(8,128)(2,1)S(1)}, bf16[4,128,128]{2,1,0:T(8,128)(2,1)}, u32[]{:S(2)}) copy-start(bf16[4,128,128]{2,1,0:T(8,128)(2,1)} %get-tuple-element.20) | copy-start | bytes 393220
  229.3 10.3 %copy-start.3 = (bf16[4,128,512]{2,1,0:T(8,128)(2,1)S(1)}, bf16[4,128,512]{2,1,0:T(8,128)(2,1)}, u32[]{:S(2)}) copy-start(bf16[4,128,512]{2,1,0:T(8,128)(2,1)} %get-tuple-element.19) | copy-start | bytes 1572868
